TPU v7x, 32 devices: a whole 2x2x4 slice. The times are simulated.
32 devices in a mesh: grp: 4 (over x, core), sub: 8 (over z, y).
Axes of the slice: x: 2, y: 2, z: 4, core: 2. Of those that a mesh axis runs over, the one named last changes fastest.
Arguments:
- fine_res: float32 [3, 131072], P(None, ('grp', 'sub'))
- node_map: int32 [2, 131072], P(None, ('grp', 'sub')), may hold values from 0 to 16383, as said below
- connect: int32 [4, 32768], P(None, 'sub'), may hold values from 0 to 16383, as said below
- grads: float32 [3, 3, 32768], P(None, None, 'sub'), may hold values from -6 to 6
- moduli: float32 [2, 32768], P(None, 'sub'), may hold values from 0.2 to 2
- mass: float32 [16384], P('sub'), may hold values from 0.5 to 4
Outputs:
- correction: float32 [3, 131072], P(None, ('grp', 'sub'))
Inputs may be any that keep to these rules, and one draw needn't show every extreme that they name: `node_map`: fine nodes 4096 * b to 4096 * (b + 1) - 1 lie in column c = b % 8; both their entries are coarse nodes c * 2048 to (c + 1) * 2048 - 1 or the first 1024 nodes of column c + 1; the two entries are equal at vertices. `connect`: tetrahedra c * 4096 to (c + 1) * 4096 - 1 lie in column c; their nodes are coarse nodes of column c or the first 1024 nodes of column c + 1.
All inputs are finite; a program needn't handle non-finite values.
Results may differ from a plain program's by a relative error of at most 0.0001.
Values sent between devices are 32-bit elements; how exact they have to be, the bound alone decides.
No kernel may reach another device: no remote copies, remote signals or barrier semaphores. Data moves between devices by JAX's collectives and lax.ppermute only.
A program may use at most 64 MiB of HBM per device.

v0:
```python
import jax
import jax.numpy as jnp
from jax import lax
from jax.sharding import PartitionSpec as P

CN = 2048
CI = 1024
CE = 4096
ITERS = 3


def shifted(shard, axis, by):
    size = lax.axis_size(axis)
    pairs = [(i, i + by) for i in range(size) if 0 <= i + by < size]
    return lax.ppermute(shard, axis, pairs)


def element_forces(field, connect, grads, moduli, count):
    last = -(grads[:, 0] + grads[:, 1] + grads[:, 2])
    shape_grads = (grads[:, 0], grads[:, 1], grads[:, 2], last)
    displ_grad = jnp.zeros((3, 3, connect.shape[1]), jnp.float32)
    for corner in range(4):
        moved = jnp.take(field, connect[corner], axis=1)
        displ_grad = displ_grad + moved[:, None, :] * shape_grads[corner][None, :, :]
    strain = 0.5 * (displ_grad + jnp.transpose(displ_grad, (1, 0, 2)))
    trace = strain[0, 0] + strain[1, 1] + strain[2, 2]
    identity = jnp.eye(3, dtype=jnp.float32)[:, :, None]
    stress = 2.0 * moduli[1] * strain + moduli[0] * trace * identity
    forces = jnp.zeros((3, count), jnp.float32)
    for corner in range(4):
        nodal = jnp.sum(stress * shape_grads[corner][None, :, :], axis=1)
        forces = forces.at[:, connect[corner]].add(nodal)
    return forces


def squares(residual):
    return lax.psum(jnp.sum(residual * residual), "sub")


def body(fine_res, node_map, connect, grads, moduli, mass):
    column = lax.axis_index("sub")
    offset = column * CN
    local_map = node_map - offset
    local_conn = connect - offset
    span = CN + CI
    share = CE // lax.axis_size("grp")
    start = lax.axis_index("grp") * share
    local_conn = lax.dynamic_slice_in_dim(local_conn, start, share, 1)
    grads = lax.dynamic_slice_in_dim(grads, start, share, 2)
    moduli = lax.dynamic_slice_in_dim(moduli, start, share, 1)
    half = 0.5 * fine_res
    partial_rhs = (
        jnp.zeros((3, span), jnp.float32)
        .at[:, local_map[0]]
        .add(half)
        .at[:, local_map[1]]
        .add(half)
    )
    column_rhs = lax.psum(partial_rhs, "grp")
    carried = shifted(column_rhs[:, CN:], "sub", 1)
    rhs = column_rhs[:, :CN].at[:, :CI].add(carried)
    solution = jnp.zeros(rhs.shape, jnp.float32)
    residual = rhs
    direction = rhs
    norm_now = squares(residual)
    for step in range(ITERS):
        operate_upper = shifted(direction[:, :CI], "sub", -1)
        operate_extended = jnp.concatenate([direction, operate_upper], axis=1)
        forces = element_forces(operate_extended, local_conn, grads, moduli, span)
        forces = lax.psum(forces, "grp")
        returned = shifted(forces[:, CN:], "sub", 1)
        own = forces[:, :CN] + mass[None, :] * direction
        image = own.at[:, :CI].add(returned)
        curv = jnp.sum(direction * image)
        alpha = norm_now / lax.psum(curv, "sub")
        solution = solution + alpha * direction
        residual = residual - alpha * image
        if step + 1 < ITERS:
            norm_next = squares(residual)
            direction = residual + norm_next / norm_now * direction
            norm_now = norm_next
    upper = shifted(solution[:, :CI], "sub", -1)
    extended = jnp.concatenate([solution, upper], axis=1)
    return 0.5 * (
        jnp.take(extended, local_map[0], axis=1) + jnp.take(extended, local_map[1], axis=1)
    )


def solution(mesh):
    in_specs = (
        P(None, ("grp", "sub")),
        P(None, ("grp", "sub")),
        P(None, "sub"),
        P(None, None, "sub"),
        P(None, "sub"),
        P("sub"),
    )
    out_specs = P(None, ("grp", "sub"))
    return jax.shard_map(body, mesh=mesh, in_specs=in_specs, out_specs=out_specs, check_vma=False)
```

profile of v0, /device:TPU:0, one launch (start us, length us, event | category | flops | bytes accessed | tf_op | source)
XLA Modules:
  0.0 632.4 jit_solution(18020449593061128261)
XLA Ops:
  2.3 23.6 %scatter_custom_fusion = f32[3,3072]{0,1:T(8,128)} fusion(s32[4096]{0:T(1024)S(1)} %bitcast.139, f32[4096,3]{1,0:T(8,128)S(1)} %copy.154, f32[]{:T(128)} %constant.127.clone.1), kind=kCustom, calls=%fused_computation.56 | custom fusion | flops 12288 | bytes 36868 | tf_op jit(solution)/shard_map/scatter-add | solution.py:55
  25.9 22.7 %scatter_fusion = f32[3,3072]{0,1:T(8,128)} fusion(f32[3,3072]{0,1:T(8,128)} %scatter_custom_fusion, s32[4096]{0:T(1024)S(1)} %bitcast.112, f32[4096,3]{1,0:T(8,128)S(1)} %copy.154), kind=kCustom, calls=%fused_computation.15 | custom fusion | flops 12288 | bytes 163840 | tf_op jit(solution)/shard_map/scatter-add | solution.py:57
  48.5 34.5 %psum.70 = f32[3,3072]{0,1:T(8,128)S(1)} all-reduce(f32[3,3072]{0,1:T(8,128)} %scatter_fusion), channel_id=1, replica_groups=mesh['grp'=4,'sub'=8] {'grp'}, use_global_device_ids=true, to_apply=%region_2.0 | all-reduce | flops 9216 | bytes 73728 | tf_op jit(solution)/shard_map/psum | solution.py:59
  90.0 9.4 %collective-permute-done = f32[3,1024]{0,1:T(8,128)S(1)} collective-permute-done((f32[3,1024]{0,1:T(8,128)}, f32[3,1024]{0,1:T(8,128)S(1)}, u32[]{:S(2)}, u32[]{:S(2)}) %collective-permute-start) | collective-permute-done | bytes 12320 | tf_op jit(solution)/shard_map/ppermute | solution.py:15
  101.5 14.5 %collective-permute-done.1 = f32[3,1024]{0,1:T(8,128)S(1)} collective-permute-done((f32[3,1024]{0,1:T(8,128)S(1)}, f32[3,1024]{0,1:T(8,128)S(1)}, u32[]{:S(2)}, u32[]{:S(2)}) %collective-permute-start.1) | collective-permute-done | bytes 12320 | tf_op jit(solution)/shard_map/ppermute | solution.py:15
  139.3 6.8 %scatter_custom_fusion.2 = f32[3,3072]{0,1:T(8,128)S(1)} fusion(s32[1024]{0:T(1024)S(1)} %bitcast.140, f32[1024,3]{1,0:T(8,128)} %copy.165, f32[]{:T(128)} %constant.127.clone.1), kind=kCustom, calls=%fused_computation.54 | custom fusion | flops 3072 | bytes 37376 | tf_op jit(solution)/shard_map/scatter-add | solution.py:32
  146.1 7.0 %scatter_fusion.1 = f32[3,3072]{0,1:T(8,128)S(1)} fusion(f32[3,3072]{0,1:T(8,128)S(1)} %scatter_custom_fusion.2, s32[1024]{0:T(1024)S(1)} %bitcast.109, f32[1024,3]{1,0:T(8,128)} %copy.166), kind=kCustom, calls=%fused_computation.17 | custom fusion | flops 3072 | bytes 40960 | tf_op jit(solution)/shard_map/scatter-add | solution.py:32
  153.1 7.2 %scatter_fusion.2 = f32[3,3072]{0,1:T(8,128)S(1)} fusion(f32[3,3072]{0,1:T(8,128)S(1)} %scatter_fusion.1, s32[1024]{0:T(1024)S(1)} %bitcast.106, f32[1024,3]{1,0:T(8,128)} %copy.167), kind=kCustom, calls=%fused_computation.18 | custom fusion | flops 3072 | bytes 40960 | tf_op jit(solution)/shard_map/scatter-add | solution.py:32
  166.9 32.0 %psum.72 = f32[3,3072]{0,1:T(8,128)} all-reduce(f32[3,3072]{0,1:T(8,128)S(1)} %scatter_fusion.3), channel_id=1, replica_groups=mesh['grp'=4,'sub'=8] {'grp'}, use_global_device_ids=true, to_apply=%region_14.16 | all-reduce | flops 9216 | bytes 73728 | tf_op jit(solution)/shard_map/psum | solution.py:70
  205.9 10.0 %collective-permute-done.2 = f32[3,1024]{0,1:T(8,128)S(1)} collective-permute-done((f32[3,1024]{0,1:T(8,128)S(1)}, f32[3,1024]{0,1:T(8,128)S(1)}, u32[]{:S(2)}, u32[]{:S(2)}) %collective-permute-start.2) | collective-permute-done | bytes 12320 | tf_op jit(solution)/shard_map/ppermute | solution.py:15
  217.6 22.1 %all-reduce = (f32[]{:T(128)}, f32[]{:T(128)}) all-reduce(f32[]{:T(128)} %get-tuple-element.56, f32[]{:T(128)} %get-tuple-element.55), channel_id=1, replica_groups=mesh['grp'=4,'sub'=8] {'sub'}, use_global_device_ids=true, to_apply=%region_5.0 | all-reduce | flops 2 | bytes 16 | tf_op jit(solution)/shard_map/psum | solution.py:37
  242.0 17.9 %psum.74 = f32[]{:T(128)} all-reduce(f32[]{:T(128)} %get-tuple-element.75), channel_id=1, replica_groups=mesh['grp'=4,'sub'=8] {'sub'}, use_global_device_ids=true, to_apply=%region_18.20 | all-reduce | flops 1 | bytes 8 | tf_op jit(solution)/shard_map/psum | solution.py:37
  262.7 10.1 %collective-permute-done.3 = f32[3,1024]{0,1:T(8,128)S(1)} collective-permute-done((f32[3,1024]{0,1:T(8,128)S(1)}, f32[3,1024]{0,1:T(8,128)S(1)}, u32[]{:S(2)}, u32[]{:S(2)}) %collective-permute-start.3) | collective-permute-done | bytes 12320 | tf_op jit(solution)/shard_map/ppermute | solution.py:15
  299.7 7.4 %scatter_custom_fusion.6 = f32[3,3072]{0,1:T(8,128)} fusion(s32[1024]{0:T(1024)S(1)} %bitcast.141, f32[1024,3]{1,0:T(8,128)S(1)} %copy.177, f32[]{:T(128)} %constant.127.clone.1), kind=kCustom, calls=%fused_computation.52 | custom fusion | flops 3072 | bytes 36868 | tf_op jit(solution)/shard_map/scatter-add | solution.py:32
  308.6 8.0 %scatter_fusion.4 = f32[3,3072]{0,1:T(8,128)} fusion(f32[3,3072]{0,1:T(8,128)} %scatter_custom_fusion.6, s32[1024]{0:T(1024)S(1)} %bitcast.110, f32[1024,3]{1,0:T(8,128)S(1)} %copy.178), kind=kCustom, calls=%fused_computation.21 | custom fusion | flops 3072 | bytes 40960 | tf_op jit(solution)/shard_map/scatter-add | solution.py:32
  316.6 8.0 %scatter_fusion.5 = f32[3,3072]{0,1:T(8,128)} fusion(f32[3,3072]{0,1:T(8,128)} %scatter_fusion.4, s32[1024]{0:T(1024)S(1)} %bitcast.107, f32[1024,3]{1,0:T(8,128)S(1)} %copy.179), kind=kCustom, calls=%fused_computation.22 | custom fusion | flops 3072 | bytes 40960 | tf_op jit(solution)/shard_map/scatter-add | solution.py:32
  324.6 8.4 %scatter_fusion.6 = f32[3,3072]{0,1:T(8,128)} fusion(f32[3,3072]{0,1:T(8,128)} %scatter_fusion.5, s32[1024]{0:T(1024)S(1)} %bitcast.104, f32[1024,3]{1,0:T(8,128)} %copy.180), kind=kCustom, calls=%fused_computation.23 | custom fusion | flops 3072 | bytes 40960 | tf_op jit(solution)/shard_map/scatter-add | solution.py:32
  333.0 32.7 %psum.75 = f32[3,3072]{0,1:T(8,128)} all-reduce(f32[3,3072]{0,1:T(8,128)} %scatter_fusion.6), channel_id=1, replica_groups=mesh['grp'=4,'sub'=8] {'grp'}, use_global_device_ids=true, to_apply=%region_27.29 | all-reduce | flops 9216 | bytes 73728 | tf_op jit(solution)/shard_map/psum | solution.py:70
  373.2 10.0 %collective-permute-done.4 = f32[3,1024]{0,1:T(8,128)S(1)} collective-permute-done((f32[3,1024]{0,1:T(8,128)S(1)}, f32[3,1024]{0,1:T(8,128)S(1)}, u32[]{:S(2)}, u32[]{:S(2)}) %collective-permute-start.4) | collective-permute-done | bytes 12320 | tf_op jit(solution)/shard_map/ppermute | solution.py:15
  384.9 20.3 %psum.76 = f32[]{:T(128)} all-reduce(f32[]{:T(128)} %multiply_reduce_fusion.2), channel_id=1, replica_groups=mesh['grp'=4,'sub'=8] {'sub'}, use_global_device_ids=true, to_apply=%region_29.31 | all-reduce | flops 1 | bytes 8 | tf_op jit(solution)/shard_map/psum | solution.py:75
  408.8 17.7 %psum.77 = f32[]{:T(128)} all-reduce(f32[]{:T(128)} %multiply_reduce_fusion.1), channel_id=1, replica_groups=mesh['grp'=4,'sub'=8] {'sub'}, use_global_device_ids=true, to_apply=%region_31.33 | all-reduce | flops 1 | bytes 8 | tf_op jit(solution)/shard_map/psum | solution.py:37
  431.0 9.5 %collective-permute-done.5 = f32[3,1024]{0,1:T(8,128)S(1)} collective-permute-done((f32[3,1024]{0,1:T(8,128)S(1)}, f32[3,1024]{0,1:T(8,128)S(1)}, u32[]{:S(2)}, u32[]{:S(2)}) %collective-permute-start.5) | collective-permute-done | bytes 12320 | tf_op jit(solution)/shard_map/ppermute | solution.py:15
  477.8 7.6 %scatter_custom_fusion.10 = f32[3,3072]{0,1:T(8,128)} fusion(s32[1024]{0:T(1024)S(1)} %bitcast.142, f32[1024,3]{1,0:T(8,128)} %copy.189, f32[]{:T(128)} %constant.127.clone.1), kind=kCustom, calls=%fused_computation.50 | custom fusion | flops 3072 | bytes 37376 | tf_op jit(solution)/shard_map/scatter-add | solution.py:32
  488.6 8.4 %scatter_fusion.7 = f32[3,3072]{0,1:T(8,128)} fusion(f32[3,3072]{0,1:T(8,128)} %scatter_custom_fusion.10, s32[1024]{0:T(1024)S(1)} %bitcast.111, f32[1024,3]{1,0:T(8,128)} %copy.190), kind=kCustom, calls=%fused_computation.25 | custom fusion | flops 3072 | bytes 40960 | tf_op jit(solution)/shard_map/scatter-add | solution.py:32
  496.9 8.4 %scatter_fusion.8 = f32[3,3072]{0,1:T(8,128)} fusion(f32[3,3072]{0,1:T(8,128)} %scatter_fusion.7, s32[1024]{0:T(1024)S(1)} %bitcast.108, f32[1024,3]{1,0:T(8,128)} %copy.191), kind=kCustom, calls=%fused_computation.26 | custom fusion | flops 3072 | bytes 40960 | tf_op jit(solution)/shard_map/scatter-add | solution.py:32
  505.3 8.4 %scatter_fusion.9 = f32[3,3072]{0,1:T(8,128)} fusion(f32[3,3072]{0,1:T(8,128)} %scatter_fusion.8, s32[1024]{0:T(1024)S(1)} %bitcast.105, f32[1024,3]{1,0:T(8,128)} %copy.192), kind=kCustom, calls=%fused_computation.27 | custom fusion | flops 3072 | bytes 40960 | tf_op jit(solution)/shard_map/scatter-add | solution.py:32
  513.7 32.9 %psum.78 = f32[3,3072]{0,1:T(8,128)} all-reduce(f32[3,3072]{0,1:T(8,128)} %scatter_fusion.9), channel_id=1, replica_groups=mesh['grp'=4,'sub'=8] {'grp'}, use_global_device_ids=true, to_apply=%region_40.42 | all-reduce | flops 9216 | bytes 73728 | tf_op jit(solution)/shard_map/psum | solution.py:70
  554.0 9.9 %collective-permute-done.6 = f32[3,1024]{0,1:T(8,128)S(1)} collective-permute-done((f32[3,1024]{0,1:T(8,128)S(1)}, f32[3,1024]{0,1:T(8,128)S(1)}, u32[]{:S(2)}, u32[]{:S(2)}) %collective-permute-start.6) | collective-permute-done | bytes 12320 | tf_op jit(solution)/shard_map/ppermute | solution.py:15
  565.6 20.2 %psum.79 = f32[]{:T(128)} all-reduce(f32[]{:T(128)} %multiply_reduce_fusion), channel_id=1, replica_groups=mesh['grp'=4,'sub'=8] {'sub'}, use_global_device_ids=true, to_apply=%region_42.44 | all-reduce | flops 1 | bytes 8 | tf_op jit(solution)/shard_map/psum | solution.py:75
  588.7 9.9 %collective-permute-done.7 = f32[3,1024]{0,1:T(8,128)S(1)} collective-permute-done((f32[3,1024]{0,1:T(8,128)S(1)}, f32[3,1024]{0,1:T(8,128)S(1)}, u32[]{:S(2)}, u32[]{:S(2)}) %collective-permute-start.7) | collective-permute-done | bytes 12320 | tf_op jit(solution)/shard_map/ppermute | solution.py:15
  598.7 14.1 %gather_fusion.12 = f32[4096,3]{1,0:T(8,128)} fusion(f32[3,3072]{0,1:T(8,128)S(1)} %pad_maximum_fusion.3, s32[4096]{0:T(1024)S(1)} %fusion.12), kind=kCustom, calls=%fused_computation.1.clone | custom fusion | bytes 114688 | tf_op jit(solution)/shard_map/jit(_take)/gather | solution.py:85
  615.0 14.1 %gather_fusion.13 = f32[4096,3]{1,0:T(8,128)} fusion(f32[3,3072]{0,1:T(8,128)S(1)} %pad_maximum_fusion.3, s32[4096]{0:T(1024)S(1)} %fusion.13), kind=kCustom, calls=%fused_computation.13.clone | custom fusion | bytes 114688 | tf_op jit(solution)/shard_map/jit(_take)/gather | solution.py:85
  (126 shorter events, 151.5 us)
Async XLA Ops:
  83.9 15.5 %collective-permute-start = (f32[3,1024]{0,1:T(8,128)}, f32[3,1024]{0,1:T(8,128)S(1)}, u32[]{:S(2)}, u32[]{:S(2)}) collective-permute-start(f32[3,1024]{0,1:T(8,128)} %slice.282), channel_id=1, source_target_pairs={{0,1},{1,2},{2,3},{3,4},{4,5},{5,6},{6,7},{8,9},{9,10},{10,11},{11... | collective-permute-start | bytes 36872 | tf_op jit(solution)/shard_map/ppermute | solution.py:15
  89.3 12.1 %copy-start.3 = (f32[2,4096]{1,0:T(2,128)S(1)}, f32[2,4096]{1,0:T(2,128)}, u32[]{:S(2)}) copy-start(f32[2,4096]{1,0:T(2,128)} %param.22) | copy-start | bytes 98308
  100.1 15.9 %collective-permute-start.1 = (f32[3,1024]{0,1:T(8,128)S(1)}, f32[3,1024]{0,1:T(8,128)S(1)}, u32[]{:S(2)}, u32[]{:S(2)}) collective-permute-start(f32[3,1024]{0,1:T(8,128)S(1)} %get-tuple-element.80), channel_id=1, source_target_pairs={{1,0},{2,1},{3,2},{4,3},{5,4},{6,5},{7,6},{9,8},{10,9},{11,10},{12... | collective-permute-start | bytes 36872 | tf_op jit(solution)/shard_map/ppermute | solution.py:15
  166.9 37.4 %copy-start.2 = (f32[2048]{0:T(1024)S(1)}, f32[2048]{0:T(1024)}, u32[]{:S(2)}) copy-start(f32[2048]{0:T(1024)} %param.23) | copy-start | bytes 24580
  200.0 15.9 %collective-permute-start.2 = (f32[3,1024]{0,1:T(8,128)S(1)}, f32[3,1024]{0,1:T(8,128)S(1)}, u32[]{:S(2)}, u32[]{:S(2)}) collective-permute-start(f32[3,1024]{0,1:T(8,128)S(1)} %slice.292), channel_id=1, source_target_pairs={{0,1},{1,2},{2,3},{3,4},{4,5},{5,6},{6,7},{8,9},{9,10},{10,11},{11... | collective-permute-start | bytes 36872 | tf_op jit(solution)/shard_map/ppermute | solution.py:15
  242.0 19.3 %copy-start.1 = (f32[3,2048]{0,1:T(8,128)}, f32[3,2048]{0,1:T(8,128)S(1)}, u32[]{:S(2)}) copy-start(f32[3,2048]{0,1:T(8,128)S(1)} %get-tuple-element.76) | copy-start | bytes 73732
  261.4 11.4 %collective-permute-start.3 = (f32[3,1024]{0,1:T(8,128)S(1)}, f32[3,1024]{0,1:T(8,128)S(1)}, u32[]{:S(2)}, u32[]{:S(2)}) collective-permute-start(f32[3,1024]{0,1:T(8,128)S(1)} %slice.293), channel_id=1, source_target_pairs={{1,0},{2,1},{3,2},{4,3},{5,4},{6,5},{7,6},{9,8},{10,9},{11,10},{12... | collective-permute-start | bytes 36872 | tf_op jit(solution)/shard_map/ppermute | solution.py:15
  366.8 16.4 %collective-permute-start.4 = (f32[3,1024]{0,1:T(8,128)S(1)}, f32[3,1024]{0,1:T(8,128)S(1)}, u32[]{:S(2)}, u32[]{:S(2)}) collective-permute-start(f32[3,1024]{0,1:T(8,128)S(1)} %slice.299), channel_id=1, source_target_pairs={{0,1},{1,2},{2,3},{3,4},{4,5},{5,6},{6,7},{8,9},{9,10},{10,11},{11... | collective-permute-start | bytes 36872 | tf_op jit(solution)/shard_map/ppermute | solution.py:15
  384.0 24.7 %copy-start = (f32[3,2048]{0,1:T(8,128)}, f32[3,2048]{0,1:T(8,128)S(1)}, u32[]{:S(2)}) copy-start(f32[3,2048]{0,1:T(8,128)S(1)} %fusion.9) | copy-start | bytes 73732
  429.4 11.1 %collective-permute-start.5 = (f32[3,1024]{0,1:T(8,128)S(1)}, f32[3,1024]{0,1:T(8,128)S(1)}, u32[]{:S(2)}, u32[]{:S(2)}) collective-permute-start(f32[3,1024]{0,1:T(8,128)S(1)} %slice.300), channel_id=1, source_target_pairs={{1,0},{2,1},{3,2},{4,3},{5,4},{6,5},{7,6},{9,8},{10,9},{11,10},{12... | collective-permute-start | bytes 36872 | tf_op jit(solution)/shard_map/ppermute | solution.py:15
  547.6 16.3 %collective-permute-start.6 = (f32[3,1024]{0,1:T(8,128)S(1)}, f32[3,1024]{0,1:T(8,128)S(1)}, u32[]{:S(2)}, u32[]{:S(2)}) collective-permute-start(f32[3,1024]{0,1:T(8,128)S(1)} %slice.306), channel_id=1, source_target_pairs={{0,1},{1,2},{2,3},{3,4},{4,5},{5,6},{6,7},{8,9},{9,10},{10,11},{11... | collective-permute-start | bytes 36872 | tf_op jit(solution)/shard_map/ppermute | solution.py:15
  587.4 11.3 %collective-permute-start.7 = (f32[3,1024]{0,1:T(8,128)S(1)}, f32[3,1024]{0,1:T(8,128)S(1)}, u32[]{:S(2)}, u32[]{:S(2)}) collective-permute-start(f32[3,1024]{0,1:T(8,128)S(1)} %slice.307), channel_id=1, source_target_pairs={{1,0},{2,1},{3,2},{4,3},{5,4},{6,5},{7,6},{9,8},{10,9},{11,10},{12... | collective-permute-start | bytes 36872 | tf_op jit(solution)/shard_map/ppermute | solution.py:15
where the time goes:
time: 643 us; the launch traced here: 632 us
  blocking collectives  230 us (36%)
  other arithmetic  177 us (28%)
  local copies, waits for them, and re-layouts  111 us (17%)
  waiting for transfers between devices  83.2 us (13%)
  starting transfers between devices  22.8 us (4%)
  between operations  7.65 us (1%)
    psum x3, blocking collectives, body(): forces = lax.psum(forces, 'grp')  97.6 us
    scatter-add x12, other arithmetic, element_forces(): forces = forces.at[:, connect[corner]].add(nodal)  92.1 us
    ppermute x8, waiting for transfers between devices, shifted(): return lax.ppermute(shard, axis, pairs)  83.2 us
    psum x3, blocking collectives, squares(): return lax.psum(jnp.sum(residual * residual), 'sub')  57.7 us
    gather x12, local copies, waits for them, and re-layouts, element_forces(): moved = jnp.take(field, connect[corner], axis=1)  56.8 us
    scatter-add x2, other arithmetic, body(): partial_rhs = jnp.zeros((3, span), jnp.float32).at[:, local_map[0]].add(h...  46.2 us
    psum x2, blocking collectives, body(): alpha = norm_now / lax.psum(curv, 'sub')  40.5 us
    psum x1, blocking collectives, body(): column_rhs = lax.psum(partial_rhs, 'grp')  34.5 us
  transfers between devices with their start and end apart: 8, of which 8 were waited for; matrix products, arithmetic and copies ran while one was open for 1% of the time, Pallas kernels for 0%

commit v1 on v0

v1 whole, which is shorter than its diff:
```python
import functools

import jax
import jax.numpy as jnp
from jax import lax
from jax.experimental import pallas as pl
from jax.experimental.pallas import tpu as pltpu
from jax.sharding import PartitionSpec as P

CI = 1024
LANE = 128
LO = 256
HP = 16
RC = 8


def split3(x):
    a = x.astype(jnp.bfloat16).astype(jnp.float32)
    r = x - a
    b = r.astype(jnp.bfloat16).astype(jnp.float32)
    return a, b, r - b


def gather(table, idxs, rows):
    lo = [i & (LANE - 1) for i in idxs]
    hi = [i >> 7 for i in idxs]
    out = [[jnp.zeros((8, LANE), jnp.float32)] * 3 for _ in idxs]
    for h in range(rows * LO // LANE):
        r, half = divmod(h, LO // LANE)
        cols = slice(half * LANE, (half + 1) * LANE)
        masks = [i == h for i in hi]
        for c in range(3):
            row = jnp.broadcast_to(table[c * HP + r : c * HP + r + 1, cols], (8, LANE))
            for k in range(len(idxs)):
                got = jnp.take_along_axis(row, lo[k], axis=1, mode="promise_in_bounds")
                out[k][c] = jnp.where(masks[k], got, out[k][c])
    return out


def scatter(idx_ref, parts_ref, acc_ref, count):
    acc_ref[...] = jnp.zeros(acc_ref.shape, jnp.float32)
    lo_iota = lax.broadcasted_iota(jnp.int32, (LO, LANE), 0)
    hi_iota = lax.broadcasted_iota(jnp.int32, (HP, LANE), 0)

    def step(i, carry):
        hot, moved = [], []
        for t in range(RC):
            row = i * RC + t
            ix = idx_ref[pl.ds(row, 1), :]
            hot.append(jnp.where(lo_iota == (ix & (LO - 1)), 1.0, 0.0).astype(jnp.bfloat16))
            mask = hi_iota == (ix >> 8)
            moved.append(
                jnp.concatenate(
                    [
                        jnp.where(mask, parts_ref[pl.ds(p * count + row, 1), :], 0.0).astype(jnp.bfloat16)
                        for p in range(9)
                    ],
                    axis=0,
                )
            )
        acc_ref[...] += lax.dot_general(
            jnp.concatenate(hot, axis=1),
            jnp.concatenate(moved, axis=1),
            (((1,), (1,)), ((), ())),
            preferred_element_type=jnp.float32,
        )
        return carry

    lax.fori_loop(0, count // RC, step, 0)
    total = jnp.transpose(acc_ref[...])
    n = 3 * HP
    return total[:n] + total[n : 2 * n] + total[2 * n :]


def rhs_kernel(col_ref, map_ref, fine_ref, out_ref, idx_ref, parts_ref, acc_ref, *, own):
    count = map_ref.shape[0]
    idx_ref[...] = map_ref[...] - col_ref[0] * own
    for c in range(3):
        pieces = split3(0.5 * fine_ref[c * count // 2 : (c + 1) * count // 2, :])
        for s in range(3):
            for k in range(2):
                at = (s * 3 + c) * count + k * count // 2
                parts_ref[at : at + count // 2, :] = pieces[s]
    out_ref[...] = scatter(idx_ref, parts_ref, acc_ref, count)


def apply_elements(col_ref, table, conn_ref, grads_ref, moduli_ref, idx_ref, parts_ref, energy_ref, rows, own):
    per = moduli_ref.shape[0] // 2
    idx_ref[...] = conn_ref[...] - col_ref[0] * own
    energy_ref[...] = jnp.zeros((8, LANE), jnp.float32)

    def step(j, carry):
        at = j * 8
        idxs = [idx_ref[pl.ds(k * per + at, 8), :] for k in range(4)]
        v = gather(table, idxs, rows)
        g = [[grads_ref[pl.ds((d * 3 + a) * per + at, 8), :] for d in range(3)] for a in range(3)]
        lam = moduli_ref[pl.ds(at, 8), :]
        mu = moduli_ref[pl.ds(per + at, 8), :]
        w = [[v[a][i] - v[3][i] for i in range(3)] for a in range(3)]
        grad = [[w[0][i] * g[0][j] + w[1][i] * g[1][j] + w[2][i] * g[2][j] for j in range(3)] for i in range(3)]
        strain = [[0.5 * (grad[i][j] + grad[j][i]) for j in range(3)] for i in range(3)]
        bulk = lam * (strain[0][0] + strain[1][1] + strain[2][2])
        stress = [[2.0 * mu * strain[i][j] + (bulk if i == j else 0.0) for j in range(3)] for i in range(3)]
        work = sum(stress[i][i] * strain[i][i] for i in range(3))
        work = work + 2.0 * (
            stress[0][1] * strain[0][1] + stress[0][2] * strain[0][2] + stress[1][2] * strain[1][2]
        )
        energy_ref[...] += work
        if parts_ref is not None:
            count = 4 * per
            for i in range(3):
                f = [sum(stress[i][j] * g[a][j] for j in range(3)) for a in range(3)]
                f.append(-(f[0] + f[1] + f[2]))
                for a in range(4):
                    pieces = split3(f[a])
                    for s in range(3):
                        parts_ref[pl.ds((s * 3 + i) * count + a * per + at, 8), :] = pieces[s]
        return carry

    lax.fori_loop(0, per // 8, step, 0)
    return jnp.sum(energy_ref[...])


def own_rows(own):
    r = lax.broadcasted_iota(jnp.int32, (3 * HP, LO), 0) & (HP - 1)
    return r < own // LO


def per_component(x):
    return jnp.concatenate([x, x, x], axis=0)


def add_halo(own_part, col, recv_ref, own, rows):
    size = recv_ref.shape[0]
    k = CI // LO
    before = jnp.maximum(col - 1, 0)
    after = jnp.minimum(col + 1, size - 1)
    down = recv_ref[pl.ds(before, 1)][0]
    up = recv_ref[pl.ds(after, 1)][0]
    down = jnp.where(col > 0, down, 0.0)
    up = jnp.where(col < size - 1, up, 0.0)
    blank = [jnp.zeros((HP - k, LO), jnp.float32), jnp.zeros((own // LO, LO), jnp.float32)]
    pieces = []
    for c in range(3):
        pieces.append(down[c * k : (c + 1) * k])
        pieces.append(jnp.zeros((own // LO - k, LO), jnp.float32))
        pieces.append(up[c * k : (c + 1) * k])
        pieces.append(jnp.zeros((HP - own // LO - k, LO), jnp.float32))
    del blank
    return own_part + jnp.concatenate(pieces, axis=0)


def pack(msg_ref, table, col, scalars, own):
    size = msg_ref.shape[0]
    k = CI // LO
    base = own // LO
    lower = [table[c * HP : c * HP + k] for c in range(3)]
    upper = [table[c * HP + base : c * HP + base + k] for c in range(3)]
    rid = lax.broadcasted_iota(jnp.int32, (HP - 3 * k, LO), 0)
    tail = jnp.zeros((HP - 3 * k, LO), jnp.float32)
    for i, s in enumerate(scalars):
        tail = jnp.where(rid == i, s, tail)
    msg_ref[...] = jnp.broadcast_to(
        jnp.concatenate([jnp.zeros((3 * k, LO), jnp.float32), tail], axis=0)[None], msg_ref.shape
    )

    @pl.when(col > 0)
    def _():
        msg_ref[pl.ds(col - 1, 1)] = jnp.concatenate(lower + [tail], axis=0)[None]

    @pl.when(col < size - 1)
    def _():
        msg_ref[pl.ds(col + 1, 1)] = jnp.concatenate(upper + [tail], axis=0)[None]


def reduced(recv_ref, i, width):
    k = 3 * CI // LO if width == HP else 0
    return jnp.sum(recv_ref[:, k + i : k + i + 1, 0:1])


def first_kernel(col_ref, sum_ref, halo_ref, mass_ref, conn_ref, grads_ref, moduli_ref,
                 msg_ref, r_ref, f_ref, idx_ref, parts_ref, acc_ref, energy_ref, *, own, rows):
    col = col_ref[0]
    r_ref[...] = add_halo(sum_ref[...], col, halo_ref, own, rows)
    mine = own_rows(own)
    r = jnp.where(mine, r_ref[...], 0.0)
    mass = per_component(mass_ref[...])
    rr = jnp.sum(r * r)
    energy = apply_elements(col_ref, r_ref, conn_ref, grads_ref, moduli_ref, idx_ref, parts_ref, energy_ref, rows, own)
    curv = energy + jnp.sum(mass * r * r)
    f = scatter(idx_ref, parts_ref, acc_ref, idx_ref.shape[0])
    f_ref[...] = f
    pack(msg_ref, f, col, [rr, curv], own)


def second_kernel(col_ref, recv_ref, r0_ref, f0_ref, mass_ref, conn_ref, grads_ref, moduli_ref,
                  msg_ref, r_ref, f_ref, image_ref, sc_ref, idx_ref, parts_ref, acc_ref, energy_ref, *, own, rows):
    col = col_ref[0]
    mass = per_component(mass_ref[...])
    rr0 = reduced(recv_ref, 0, HP)
    curv0 = reduced(recv_ref, 1, HP)
    alpha0 = rr0 / curv0
    image = add_halo(f0_ref[...] + mass * r0_ref[...], col, recv_ref, own, rows)
    image_ref[...] = image
    r_ref[...] = r0_ref[...] - alpha0 * image
    r = jnp.where(own_rows(own), r_ref[...], 0.0)
    rr = jnp.sum(r * r)
    cross = jnp.sum(r * image)
    energy = apply_elements(col_ref, r_ref, conn_ref, grads_ref, moduli_ref, idx_ref, parts_ref, energy_ref, rows, own)
    own_curv = energy + jnp.sum(mass * r * r)
    f = scatter(idx_ref, parts_ref, acc_ref, idx_ref.shape[0])
    f_ref[...] = f
    pack(msg_ref, f, col, [rr, own_curv, cross], own)
    sc_ref[0] = rr0
    sc_ref[1] = curv0
    sc_ref[2] = alpha0


def third_kernel(col_ref, sc_ref, recv_ref, r0_ref, r1_ref, f1_ref, image_ref, mass_ref, conn_ref, grads_ref,
                 moduli_ref, msg_ref, r_ref, d_ref, x_ref, out_sc_ref, idx_ref, energy_ref, *, own, rows):
    col = col_ref[0]
    mass = per_component(mass_ref[...])
    rr0, curv0, alpha0 = sc_ref[0], sc_ref[1], sc_ref[2]
    rr1 = reduced(recv_ref, 0, HP)
    own_curv = reduced(recv_ref, 1, HP)
    cross = reduced(recv_ref, 2, HP)
    beta = rr1 / rr0
    curv1 = own_curv + 2.0 * beta * cross + beta * beta * curv0
    alpha1 = rr1 / curv1
    r1 = r1_ref[...]
    image = add_halo(f1_ref[...] + mass * r1, col, recv_ref, own, rows) + beta * image_ref[...]
    d = r1 + beta * r0_ref[...]
    d_ref[...] = d
    x_ref[...] = alpha0 * r0_ref[...] + alpha1 * d
    r_ref[...] = r1 - alpha1 * image
    r = jnp.where(own_rows(own), r_ref[...], 0.0)
    rr = jnp.sum(r * r)
    cross = jnp.sum(r * image)
    energy = apply_elements(col_ref, r_ref, conn_ref, grads_ref, moduli_ref, idx_ref, None, energy_ref, rows, own)
    own_curv = energy + jnp.sum(mass * r * r)
    rid = lax.broadcasted_iota(jnp.int32, msg_ref.shape, 1)
    msg_ref[...] = jnp.where(rid == 0, rr, jnp.where(rid == 1, own_curv, cross))
    out_sc_ref[0] = rr1
    out_sc_ref[1] = curv1


def last_kernel(col_ref, sc_ref, recv_ref, r_ref, d_ref, x_ref, map_ref, out_ref, table_ref, *, own, rows):
    col = col_ref[0]
    rr1, curv1 = sc_ref[0], sc_ref[1]
    rr2 = reduced(recv_ref, 0, 8)
    own_curv = reduced(recv_ref, 1, 8)
    cross = reduced(recv_ref, 2, 8)
    beta = rr2 / rr1
    curv2 = own_curv + 2.0 * beta * cross + beta * beta * curv1
    alpha2 = rr2 / curv2
    table_ref[...] = 0.5 * (x_ref[...] + alpha2 * (r_ref[...] + beta * d_ref[...]))
    per = map_ref.shape[0] // 2

    def step(j, carry):
        at = j * 8
        idxs = [map_ref[pl.ds(k * per + at, 8), :] - col * own for k in range(2)]
        v = gather(table_ref, idxs, rows)
        for c in range(3):
            out_ref[pl.ds(c * per + at, 8), :] = v[0][c] + v[1][c]
        return carry

    lax.fori_loop(0, per // 8, step, 0)


def call(kernel, outs, scratch, smem_in, n_in):
    vm = pl.BlockSpec(memory_space=pltpu.VMEM)
    sm = pl.BlockSpec(memory_space=pltpu.SMEM)
    out_specs = [sm if len(o.shape) == 1 else vm for o in outs]
    return pl.pallas_call(
        kernel,
        out_shape=outs,
        in_specs=[sm] * smem_in + [vm] * n_in,
        out_specs=out_specs,
        scratch_shapes=scratch,
    )


def body(fine_res, node_map, connect, grads, moduli, mass):
    size = lax.axis_size("sub")
    groups = lax.axis_size("grp")
    own = mass.shape[0]
    fine = node_map.shape[1]
    elems = connect.shape[1]
    rows = (own + CI) // LO
    col = lax.axis_index("sub").astype(jnp.int32).reshape(1)
    f32 = functools.partial(jax.ShapeDtypeStruct, dtype=jnp.float32)
    table = f32((3 * HP, LO))
    msg = f32((size, HP, LO))
    map2 = node_map.reshape(2 * fine // LANE, LANE)
    fine2 = fine_res.reshape(3 * fine // LANE, LANE)
    conn2 = connect.reshape(4 * elems // LANE, LANE)
    grads2 = grads.reshape(9 * elems // LANE, LANE)
    moduli2 = moduli.reshape(2 * elems // LANE, LANE)
    acc = pltpu.VMEM((LO, 9 * HP), jnp.float32)
    fcount = 2 * fine // LANE
    ecount = 4 * elems // LANE

    (partial,) = call(
        functools.partial(rhs_kernel, own=own),
        [table],
        [pltpu.VMEM((fcount, LANE), jnp.int32), pltpu.VMEM((9 * fcount, LANE), jnp.float32), acc],
        1,
        2,
    )(col, map2, fine2)
    summed = partial
    for k in range(1, groups):
        summed = summed + lax.ppermute(partial, "grp", [(i, (i + k) % groups) for i in range(groups)])
    k = CI // LO
    s3 = summed.reshape(3, HP, LO)
    lower = s3[:, :k].reshape(3 * k, LO)
    upper = s3[:, own // LO : own // LO + k].reshape(3 * k, LO)
    mass2 = mass.reshape(own // LO, LO)
    down = jnp.concatenate([lower, mass2[:k]], axis=0)
    up = jnp.concatenate([upper, jnp.zeros((k, LO), jnp.float32)], axis=0)
    c0 = col[0]
    halo = jnp.zeros((size, HP, LO), jnp.float32)
    halo = jnp.where((jnp.arange(size) == c0 - 1)[:, None, None], down[None], halo)
    halo = jnp.where((jnp.arange(size) == c0 + 1)[:, None, None], up[None], halo)
    halo = lax.all_to_all(halo, "sub", 0, 0)
    mass_next = lax.dynamic_slice_in_dim(halo, jnp.minimum(c0 + 1, size - 1), 1, 0)[0, 3 * k :]
    mass_ext = jnp.concatenate([mass2, mass_next, jnp.zeros((HP - own // LO - k, LO), jnp.float32)], axis=0)

    idx = pltpu.VMEM((ecount, LANE), jnp.int32)
    parts = pltpu.VMEM((9 * ecount, LANE), jnp.float32)
    energy = pltpu.VMEM((8, LANE), jnp.float32)
    kw = dict(own=own, rows=rows)
    m0, r0, f0 = call(functools.partial(first_kernel, **kw), [msg, table, table], [idx, parts, acc, energy], 1, 6)(
        col, summed, halo, mass_ext, conn2, grads2, moduli2
    )
    m0 = lax.all_to_all(m0, "sub", 0, 0)
    m1, r1, f1, image, sc = call(
        functools.partial(second_kernel, **kw), [msg, table, table, table, f32((3,))], [idx, parts, acc, energy], 1, 7
    )(col, m0, r0, f0, mass_ext, conn2, grads2, moduli2)
    m1 = lax.all_to_all(m1, "sub", 0, 0)
    m2, r2, d1, x2, sc = call(
        functools.partial(third_kernel, **kw), [f32((size, 8, LANE)), table, table, table, f32((2,))], [idx, energy], 2, 9
    )(col, sc, m1, r0, r1, f1, image, mass_ext, conn2, grads2, moduli2)
    m2 = lax.all_to_all(m2, "sub", 0, 0)
    (out,) = call(
        functools.partial(last_kernel, **kw), [f32((3 * fine // LANE, LANE))], [pltpu.VMEM((3 * HP, LO), jnp.float32)], 2, 5
    )(col, sc, m2, r2, d1, x2, map2)
    return out.reshape(3, fine)


def solution(mesh):
    in_specs = (
        P(None, ("grp", "sub")),
        P(None, ("grp", "sub")),
        P(None, "sub"),
        P(None, None, "sub"),
        P(None, "sub"),
        P("sub"),
    )
    out_specs = P(None, ("grp", "sub"))
    return jax.shard_map(body, mesh=mesh, in_specs=in_specs, out_specs=out_specs, check_vma=False)
```

time: 643 us -> 95.1 us (0.15); the launches traced: 632 us -> 94.3 us
  blocking collectives: 230 us -> 33.3 us
  other arithmetic: 177 us -> 2.23 us
  local copies, waits for them, and re-layouts: 111 us -> 7.19 us
  waiting for transfers between devices: 83.2 us -> 8.28 us
  Pallas kernels: 0 us -> 34 us
  starting transfers between devices: 22.8 us -> 9.17 us
  between operations: 7.65 us -> 0.1 us
    psum x9 -> x0, blocking collectives: 230 us -> none  [the longest x3 97.6 us: body(): forces = lax.psum(forces, 'grp')]
    scatter-add x18 -> x0, other arithmetic: 141 us -> none  [the longest x12 92.1 us: element_forces(): forces = forces.at[:, connect[corner]].add(nodal)]
    gather x16 -> x0, local copies, waits for them, and re-layouts: 89.4 us -> none  [the longest x12 56.8 us: element_forces(): moved = jnp.take(field, connect[corner], axis=1)]
    ppermute x8 -> x3, waiting for transfers between devices: 83.2 us -> 3.33 us  [body(): lax.ppermute(partial, 'grp', [(i, (i + k) % groups) for i in range(groups)])]
    pallas_call x0 -> x5, Pallas kernels: none -> 34 us  [the longest x1 10.9 us: body(): call(functools.partial(second_kernel, **kw), [msg, table, table, table, f...]
    all_to_all x0 -> x3, blocking collectives: none -> 33.3 us  [the longest x1 11.3 us: body(): m1 = lax.all_to_all(m1, 'sub', 0, 0)]
    ppermute x8 -> x3, starting transfers between devices: 22.8 us -> 3.2 us  [body(): lax.ppermute(partial, 'grp', [(i, (i + k) % groups) for i in range(groups)])]
    select_n x14 -> x1, other arithmetic: 16.2 us -> 0.74 us  [body(): jnp.where((jnp.arange(size) == c0 + 1)[:, None, None], up[None], halo)]
  transfers between devices with their start and end apart: 8 -> 4, of which waited for: 8 -> 3; matrix products, arithmetic and copies ran while one was open for 1% -> 2% of each run, Pallas kernels for 0% -> 0%
where the time goes in v1:
time: 95.1 us; the launch traced here: 94.3 us
  Pallas kernels  34 us (36%)
  blocking collectives  33.3 us (35%)
  starting transfers between devices  9.17 us (10%)
  waiting for transfers between devices  8.28 us (9%)
  local copies, waits for them, and re-layouts  7.19 us (8%)
  other arithmetic  2.23 us (2%)
    all_to_all x1, blocking collectives, body(): m1 = lax.all_to_all(m1, 'sub', 0, 0)  11.3 us
    all_to_all x1, blocking collectives, body(): m0 = lax.all_to_all(m0, 'sub', 0, 0)  11.3 us
    pallas_call x1, Pallas kernels, body(): call(functools.partial(second_kernel, **kw), [msg, table, table, table, f...  10.9 us
    pallas_call x1, Pallas kernels, body(): call(functools.partial(first_kernel, **kw), [msg, table, table], [idx, pa...  10.7 us
    all_to_all x1, blocking collectives, body(): m2 = lax.all_to_all(m2, 'sub', 0, 0)  10.6 us
    all_to_all x1, starting transfers between devices, body(): halo = lax.all_to_all(halo, 'sub', 0, 0)  5.97 us
    pallas_call x1, Pallas kernels, body(): call(functools.partial(third_kernel, **kw), [f32((size, 8, LANE)), table,...  5.7 us
    all_to_all x1, waiting for transfers between devices, body(): halo = lax.all_to_all(halo, 'sub', 0, 0)  4.96 us
  transfers between devices with their start and end apart: 4, of which 3 were waited for; matrix products, arithmetic and copies ran while one was open for 2% of the time, Pallas kernels for 0%

profile of v1, /device:TPU:0, one launch (start us, length us, event | category | flops | bytes accessed | tf_op | source)
XLA Modules:
  0.0 94.3 jit_solution(15780535402430464364)
XLA Ops:
  0.0 1.4 %reshape.53.map_ref = s32[64,128]{1,0:T(8,128)} reshape(s32[2,4096]{1,0:T(2,128)} %param.7) | data formatting | bytes 65536 | tf_op jit(solution)/shard_map/reshape | solution.py:294
  1.4 0.0 copy-done.3
  1.4 0.7 reshape.54.fine_ref
  2.1 4.1 %shard_map.64 = f32[48,256]{1,0:T(8,128)} custom-call(s32[1]{0:T(128)} %bitcast.col_ref, s32[64,128]{1,0:T(8,128)} %reshape.53.map_ref, f32[96,128]{1,0:T(8,128)} %reshape.54.fine_ref), custom_call_target="tpu_custom_call" | custom-call | tf_op jit(solution)/shard_map/pallas_call | solution.py:303
  6.2 2.4 %collective-permute-start.2 = (f32[48,256]{1,0:T(8,128)}, f32[48,256]{1,0:T(8,128)S(1)}, u32[]{:S(2)}, u32[]{:S(2)}) collective-permute-start(f32[48,256]{1,0:T(8,128)} %shard_map.64), channel_id=1, source_target_pairs={{0,24},{8,0},{16,8},{24,16},{1,25},{9,1},{17,9},{25,17},{2,26},{10... | collective-permute-start | bytes 147464 | tf_op jit(solution)/shard_map/ppermute | solution.py:312
  8.6 0.6 collective-permute-start.1
  9.2 0.2 collective-permute-start
  9.4 0.7 slice-done
  10.1 0.8 collective-permute-done.2
  10.9 2.5 %collective-permute-done.1 = f32[48,256]{1,0:T(8,128)S(1)} collective-permute-done((f32[48,256]{1,0:T(8,128)}, f32[48,256]{1,0:T(8,128)S(1)}, u32[]{:S(2)}, u32[]{:S(2)}) %collective-permute-start.1) | collective-permute-done | bytes 49184 | tf_op jit(solution)/shard_map/ppermute | solution.py:312
  13.4 0.0 collective-permute-done
  13.4 0.8 add_add_fusion.sum_ref
  14.3 0.6 copy-done.1
  14.9 0.7 select_select_fusion
  15.6 6.0 %all-to-all-start = ((f32[8,16,256]{2,1,0:T(8,128)}), f32[8,16,256]{2,1,0:T(8,128)S(1)}, u32[]{:S(2)}, u32[]{:S(2)}) async-start(f32[8,16,256]{2,1,0:T(8,128)} %select_select_fusion), calls=%async_computation | async-start | bytes 262144 | tf_op jit(solution)/shard_map/all_to_all | solution.py:324
  21.6 0.0 copy-done.6
  21.6 0.0 copy-start.4
  21.6 0.6 reshape.61.moduli_ref
  22.3 0.2 copy-done.4
  22.4 0.7 reshape.59.conn_ref
  23.1 0.8 reshape.60.grads_ref
  23.9 0.1 pad.3.clone
  24.0 5.0 %all-to-all-done.halo_ref = f32[8,16,256]{2,1,0:T(8,128)S(1)} async-done(((f32[8,16,256]{2,1,0:T(8,128)}), f32[8,16,256]{2,1,0:T(8,128)S(1)}, u32[]{:S(2)}, u32[]{:S(2)}) %all-to-all-start) | async-done | bytes 131104 | tf_op jit(solution)/shard_map/all_to_all | solution.py:324
  28.9 0.7 maximum_maximum_fusion.mass_ref
  29.6 10.7 %shard_map.65 = (f32[8,16,256]{2,1,0:T(8,128)}, f32[48,256]{1,0:T(8,128)}, f32[48,256]{1,0:T(8,128)}) custom-call(s32[1]{0:T(128)} %bitcast.col_ref, f32[48,256]{1,0:T(8,128)} %copy-done.1, f32[8,16,256]{2,1,0:T(8,128)} %copy-done, f32[16,256]{1,0:T(8,128)} %maximum_maximum_fusion.mass_ref, s32[128,128]{1,0:T(8,128)} %reshape.59.conn_ref, ...), custom_call_target="tpu_custom_call" | custom-call | tf_op jit(solution)/shard_map/pallas_call | solution.py:332
  40.3 11.3 %all_to_all.20.recv_ref = f32[8,16,256]{2,1,0:T(8,128)} all-to-all(f32[8,16,256]{2,1,0:T(8,128)} %get-tuple-element.18), channel_id=1, replica_groups=mesh['grp'=4,'sub'=8] {'sub'}, dimensions={0} | all-to-all | bytes 262144 | tf_op jit(solution)/shard_map/all_to_all | solution.py:335
  51.6 10.9 %shard_map.66 = (f32[8,16,256]{2,1,0:T(8,128)}, f32[48,256]{1,0:T(8,128)}, f32[48,256]{1,0:T(8,128)}, f32[48,256]{1,0:T(8,128)}, f32[3]{0:T(128)}) custom-call(s32[1]{0:T(128)} %bitcast.col_ref, f32[8,16,256]{2,1,0:T(8,128)} %all_to_all.20.recv_ref, f32[48,256]{1,0:T(8,128)} %get-tuple-element.19.r0_ref, f32[48,256]{1,0:T(8,128)} %get-tuple-element.20.f0_ref, ...), custom_call_target="tpu_custom_call" | custom-call | tf_op jit(solution)/shard_map/pallas_call | solution.py:336
  62.5 11.3 %all_to_all.21.recv_ref = f32[8,16,256]{2,1,0:T(8,128)} all-to-all(f32[8,16,256]{2,1,0:T(8,128)} %get-tuple-element.22), channel_id=1, replica_groups=mesh['grp'=4,'sub'=8] {'sub'}, dimensions={0} | all-to-all | bytes 262144 | tf_op jit(solution)/shard_map/all_to_all | solution.py:339
  73.9 5.7 %shard_map.67 = (f32[8,8,128]{2,1,0:T(8,128)}, f32[48,256]{1,0:T(8,128)}, f32[48,256]{1,0:T(8,128)}, f32[48,256]{1,0:T(8,128)}, f32[2]{0:T(128)}) custom-call(s32[1]{0:T(128)} %bitcast.col_ref, f32[3]{0:T(128)} %get-tuple-element.21.sc_ref, f32[8,16,256]{2,1,0:T(8,128)} %all_to_all.21.recv_ref, f32[48,256]{1,0:T(8,128)} %get-tuple-element.19.r0_ref, ...), custom_call_target="tpu_custom_call" | custom-call | tf_op jit(solution)/shard_map/pallas_call | solution.py:340
  79.6 10.6 %all_to_all.22.recv_ref = f32[8,8,128]{2,1,0:T(8,128)} all-to-all(f32[8,8,128]{2,1,0:T(8,128)} %get-tuple-element.27), channel_id=1, replica_groups=mesh['grp'=4,'sub'=8] {'sub'}, dimensions={0} | all-to-all | bytes 65536 | tf_op jit(solution)/shard_map/all_to_all | solution.py:343
  90.2 2.6 %shard_map.68 = f32[96,128]{1,0:T(8,128)} custom-call(s32[1]{0:T(128)} %bitcast.col_ref, f32[2]{0:T(128)} %get-tuple-element.26.sc_ref, f32[8,8,128]{2,1,0:T(8,128)} %all_to_all.22.recv_ref, f32[48,256]{1,0:T(8,128)} %get-tuple-element.28.r_ref, f32[48,256]{1,0:T(8,128)} %get-tuple-element.29.d_ref, f32[48,256]{1,0:T(8,128)} %get-tuple-element.30.x_ref, ...), custom_call_target="tpu_custom_call" | custom-call | tf_op jit(solution)/shard_map/pallas_call | solution.py:344
  92.8 1.4 %reshape.62 = f32[3,4096]{1,0:T(4,128)} reshape(f32[96,128]{1,0:T(8,128)} %shard_map.68) | data formatting | bytes 98304 | tf_op jit(solution)/shard_map/reshape | solution.py:347
  (20 shorter events, 0.1 us)
Async XLA Ops:
  0.0 1.4 %copy-start.3 = (f32[3,4096]{1,0:T(4,128)S(1)}, f32[3,4096]{1,0:T(4,128)}, u32[]{:S(2)}) copy-start(f32[3,4096]{1,0:T(4,128)} %param.6) | copy-start | bytes 147460
  6.2 4.7 %collective-permute-start.2 = (f32[48,256]{1,0:T(8,128)}, f32[48,256]{1,0:T(8,128)S(1)}, u32[]{:S(2)}, u32[]{:S(2)}) collective-permute-start(f32[48,256]{1,0:T(8,128)} %shard_map.64), channel_id=1, source_target_pairs={{0,24},{8,0},{16,8},{24,16},{1,25},{9,1},{17,9},{25,17},{2,26},{10... | collective-permute-start | bytes 147464 | tf_op jit(solution)/shard_map/ppermute | solution.py:312
  8.6 4.8 %collective-permute-start.1 = (f32[48,256]{1,0:T(8,128)}, f32[48,256]{1,0:T(8,128)S(1)}, u32[]{:S(2)}, u32[]{:S(2)}) collective-permute-start(f32[48,256]{1,0:T(8,128)} %shard_map.64), channel_id=1, source_target_pairs={{0,16},{8,24},{16,0},{24,8},{1,17},{9,25},{17,1},{25,9},{2,18},{10... | collective-permute-start | bytes 147464 | tf_op jit(solution)/shard_map/ppermute | solution.py:312
  9.2 4.3 %collective-permute-start = (f32[48,256]{1,0:T(8,128)}, f32[48,256]{1,0:T(8,128)S(1)}, u32[]{:S(2)}, u32[]{:S(2)}) collective-permute-start(f32[48,256]{1,0:T(8,128)} %shard_map.64), channel_id=1, source_target_pairs={{0,8},{8,16},{16,24},{24,0},{1,9},{9,17},{17,25},{25,1},{2,10},{10... | collective-permute-start | bytes 147464 | tf_op jit(solution)/shard_map/ppermute | solution.py:312
  9.4 0.7 slice-start
  14.2 0.6 copy-start.1
  15.6 6.0 %copy-start.6 = (f32[2048]{0:T(1024)S(1)}, f32[2048]{0:T(1024)}, u32[]{:S(2)}) copy-start(f32[2048]{0:T(1024)} %param.11) | copy-start | bytes 24580
  15.6 6.0 %copy-start.5 = (f32[2,4096]{1,0:T(2,128)S(1)}, f32[2,4096]{1,0:T(2,128)}, u32[]{:S(2)}) copy-start(f32[2,4096]{1,0:T(2,128)} %param.10) | copy-start | bytes 98308
  15.6 7.5 %copy-start.2 = (f32[3,3,4096]{2,1,0:T(4,128)S(1)}, f32[3,3,4096]{2,1,0:T(4,128)}, u32[]{:S(2)}) copy-start(f32[3,3,4096]{2,1,0:T(4,128)} %param.9) | copy-start | bytes 442372
  15.6 13.3 %all-to-all-start = ((f32[8,16,256]{2,1,0:T(8,128)}), f32[8,16,256]{2,1,0:T(8,128)S(1)}, u32[]{:S(2)}, u32[]{:S(2)}) async-start(f32[8,16,256]{2,1,0:T(8,128)} %select_select_fusion), calls=%async_computation | async-start | bytes 262144 | tf_op jit(solution)/shard_map/all_to_all | solution.py:324
  21.6 0.8 copy-start.4
  28.9 0.7 copy-start

commit v2 on v1

v2 whole, which is shorter than its diff:
```python
import functools

import jax
import jax.numpy as jnp
from jax import lax
from jax.experimental import pallas as pl
from jax.experimental.pallas import tpu as pltpu
from jax.sharding import PartitionSpec as P

CI = 1024
LANE = 128
LO = 256
HP = 16
RC = 32


def split3(x):
    a = x.astype(jnp.bfloat16).astype(jnp.float32)
    r = x - a
    b = r.astype(jnp.bfloat16).astype(jnp.float32)
    return a, b, r - b


def gather(table, idxs, rows):
    out = []
    for ix in idxs:
        lo = ix & (LANE - 1)
        hi = ix >> 7
        got = [jnp.zeros((8, LANE), jnp.float32)] * 3
        for h in range(rows * LO // LANE):
            r, half = divmod(h, LO // LANE)
            mask = hi == h
            for c in range(3):
                row = table[c * HP + r : c * HP + r + 1, half * LANE : (half + 1) * LANE]
                row = jnp.broadcast_to(row, (8, LANE))
                moved = jnp.take_along_axis(row, lo, axis=1, mode="promise_in_bounds")
                got[c] = jnp.where(mask, moved, got[c])
        out.append(got)
    return out


def scatter(idx_ref, parts_ref, acc_ref, count):
    acc_ref[...] = jnp.zeros(acc_ref.shape, jnp.float32)
    lo_iota = lax.broadcasted_iota(jnp.int32, (LO, LANE), 0)
    hi_iota = lax.broadcasted_iota(jnp.int32, (HP, LANE), 0)

    def step(i, carry):
        hot, moved = [], []
        for t in range(RC):
            row = i * RC + t
            ix = idx_ref[pl.ds(row, 1), :]
            hot.append(jnp.where(lo_iota == (ix & (LO - 1)), 1.0, 0.0).astype(jnp.bfloat16))
            mask = hi_iota == (ix >> 8)
            moved.append(
                jnp.concatenate(
                    [
                        jnp.where(mask, parts_ref[pl.ds(p * count + row, 1), :], 0.0).astype(jnp.bfloat16)
                        for p in range(9)
                    ],
                    axis=0,
                )
            )
        acc_ref[...] += lax.dot_general(
            jnp.concatenate(hot, axis=1),
            jnp.concatenate(moved, axis=1),
            (((1,), (1,)), ((), ())),
            preferred_element_type=jnp.float32,
        )
        return carry

    lax.fori_loop(0, count // RC, step, 0)
    total = jnp.transpose(acc_ref[...])
    n = 3 * HP
    return total[:n] + total[n : 2 * n] + total[2 * n :]


def lines(ref, lead, dst, base, f=lambda x: x):
    n = ref.shape[-1] // LANE
    for q in range(n):
        dst[base + q : base + q + 1, :] = f(ref[lead + (slice(q * LANE, (q + 1) * LANE),)])


def rhs_kernel(col_ref, map_ref, fine_ref, mass_ref, out_ref, lower_ref, upper_ref, idx_ref,
               half_ref, parts_ref, acc_ref, *, own):
    half = map_ref.shape[1] // LANE
    count = 2 * half
    shift = col_ref[0] * own
    for k in range(2):
        lines(map_ref, (slice(k, k + 1),), idx_ref, k * half, lambda x: x - shift)
    for c in range(3):
        lines(fine_ref, (slice(c, c + 1),), half_ref, c * half)
    for c in range(3):
        pieces = split3(0.5 * half_ref[c * half : (c + 1) * half, :])
        for s in range(3):
            for k in range(2):
                at = (s * 3 + c) * count + k * half
                parts_ref[at : at + half, :] = pieces[s]
    table = scatter(idx_ref, parts_ref, acc_ref, count)
    out_ref[...] = table
    k = CI // LO
    lower, upper = shared(table, own)
    mass = jnp.concatenate([mass_ref[pl.ds(0, k, stride=2), :], mass_ref[pl.ds(1, k, stride=2), :]], axis=1)
    lower_ref[...] = jnp.concatenate([lower, mass], axis=0)
    upper_ref[...] = upper


def prep_kernel(col_ref, conn_ref, grads_ref, moduli_ref, idx_ref, g_ref, m_ref, *, own):
    per = moduli_ref.shape[1] // LANE
    shift = col_ref[0] * own
    for a in range(4):
        lines(conn_ref, (slice(a, a + 1),), idx_ref, a * per, lambda x: x - shift)
    for d in range(3):
        for a in range(3):
            lines(grads_ref, (d, slice(a, a + 1)), g_ref, (d * 3 + a) * per)
    for i in range(2):
        lines(moduli_ref, (slice(i, i + 1),), m_ref, i * per)


def shared(table, own):
    k = CI // LO
    base = own // LO
    lower = jnp.concatenate([table[c * HP : c * HP + k] for c in range(3)], axis=0)
    upper = jnp.concatenate([table[c * HP + base : c * HP + base + k] for c in range(3)], axis=0)
    return lower, upper


def halo_kernel(col_ref, table_ref, before_ref, after_ref, mass_ref, out_ref, mass_out_ref, *, own, size):
    col = col_ref[0]
    k = CI // LO
    after = after_ref[...]
    out_ref[...] = add_halo(table_ref[...], col, before_ref[...], after[: 3 * k], own, size)
    mine = jnp.concatenate(
        [mass_ref[pl.ds(0, own // LO, stride=2), :], mass_ref[pl.ds(1, own // LO, stride=2), :]], axis=1
    )
    pad = jnp.zeros((HP - own // LO - k, LO), jnp.float32)
    mass_out_ref[...] = jnp.concatenate([mine, after[3 * k :], pad], axis=0)


def apply_elements(table, idx_ref, grads_ref, moduli_ref, parts_ref, energy_ref, rows):
    per = moduli_ref.shape[0] // 2
    energy_ref[...] = jnp.zeros((8, LANE), jnp.float32)

    def step(j, carry):
        at = j * 8
        idxs = [idx_ref[pl.ds(k * per + at, 8), :] for k in range(4)]
        v = gather(table, idxs, rows)
        g = [[grads_ref[pl.ds((d * 3 + a) * per + at, 8), :] for d in range(3)] for a in range(3)]
        lam = moduli_ref[pl.ds(at, 8), :]
        mu = moduli_ref[pl.ds(per + at, 8), :]
        w = [[v[a][i] - v[3][i] for i in range(3)] for a in range(3)]
        grad = [[w[0][i] * g[0][j] + w[1][i] * g[1][j] + w[2][i] * g[2][j] for j in range(3)] for i in range(3)]
        strain = [[0.5 * (grad[i][j] + grad[j][i]) for j in range(3)] for i in range(3)]
        bulk = lam * (strain[0][0] + strain[1][1] + strain[2][2])
        stress = [[2.0 * mu * strain[i][j] + (bulk if i == j else 0.0) for j in range(3)] for i in range(3)]
        work = sum(stress[i][i] * strain[i][i] for i in range(3))
        work = work + 2.0 * (
            stress[0][1] * strain[0][1] + stress[0][2] * strain[0][2] + stress[1][2] * strain[1][2]
        )
        energy_ref[...] += work
        if parts_ref is not None:
            count = 4 * per
            for i in range(3):
                f = [sum(stress[i][j] * g[a][j] for j in range(3)) for a in range(3)]
                f.append(-(f[0] + f[1] + f[2]))
                for a in range(4):
                    pieces = split3(f[a])
                    for s in range(3):
                        parts_ref[pl.ds((s * 3 + i) * count + a * per + at, 8), :] = pieces[s]
        return carry

    lax.fori_loop(0, per // 8, step, 0)
    return jnp.sum(energy_ref[...])


def own_rows(own):
    r = lax.broadcasted_iota(jnp.int32, (3 * HP, LO), 0) & (HP - 1)
    return r < own // LO


def per_component(x):
    return jnp.concatenate([x, x, x], axis=0)


def add_halo(own_part, col, down, up, own, size):
    k = CI // LO
    down = jnp.where(col > 0, down, 0.0)
    up = jnp.where(col < size - 1, up, 0.0)
    pieces = []
    for c in range(3):
        pieces.append(down[c * k : (c + 1) * k])
        pieces.append(jnp.zeros((own // LO - k, LO), jnp.float32))
        pieces.append(up[c * k : (c + 1) * k])
        pieces.append(jnp.zeros((HP - own // LO - k, LO), jnp.float32))
    return own_part + jnp.concatenate(pieces, axis=0)


def add_received(own_part, col, recv_ref, own):
    size = recv_ref.shape[0]
    k = 3 * CI // LO
    down = recv_ref[pl.ds(jnp.maximum(col - 1, 0), 1)][0]
    up = recv_ref[pl.ds(jnp.minimum(col + 1, size - 1), 1)][0]
    return add_halo(own_part, col, down[:k], up[:k], own, size)


def pack(msg_ref, table, col, scalars, own):
    size = msg_ref.shape[0]
    k = CI // LO
    lower, upper = shared(table, own)
    rid = lax.broadcasted_iota(jnp.int32, (HP - 3 * k, LO), 0)
    tail = jnp.zeros((HP - 3 * k, LO), jnp.float32)
    for i, s in enumerate(scalars):
        tail = jnp.where(rid == i, s, tail)
    msg_ref[...] = jnp.broadcast_to(
        jnp.concatenate([jnp.zeros((3 * k, LO), jnp.float32), tail], axis=0)[None], msg_ref.shape
    )

    @pl.when(col > 0)
    def _():
        msg_ref[pl.ds(col - 1, 1)] = jnp.concatenate([lower, tail], axis=0)[None]

    @pl.when(col < size - 1)
    def _():
        msg_ref[pl.ds(col + 1, 1)] = jnp.concatenate([upper, tail], axis=0)[None]


def reduced(recv_ref, i, width):
    k = 3 * CI // LO if width == HP else 0
    return jnp.sum(recv_ref[:, k + i : k + i + 1, 0:1])


def first_kernel(col_ref, *refs, own, rows, groups):
    sum_refs = refs[:groups]
    mass_ref, idx_ref, grads_ref, moduli_ref, msg_ref, r_ref, f_ref, parts_ref, acc_ref, energy_ref = refs[groups:]
    total = sum_refs[0][...]
    for ref in sum_refs[1:]:
        total = total + ref[...]
    r_ref[...] = total
    r = jnp.where(own_rows(own), total, 0.0)
    mass = per_component(mass_ref[...])
    rr = jnp.sum(r * r)
    energy = apply_elements(r_ref, idx_ref, grads_ref, moduli_ref, parts_ref, energy_ref, rows)
    curv = energy + jnp.sum(mass * r * r)
    f = scatter(idx_ref, parts_ref, acc_ref, idx_ref.shape[0])
    f_ref[...] = f
    pack(msg_ref, f, col_ref[0], [rr, curv], own)


def second_kernel(col_ref, recv_ref, r0_ref, f0_ref, mass_ref, idx_ref, grads_ref, moduli_ref,
                  msg_ref, r_ref, f_ref, image_ref, sc_ref, parts_ref, acc_ref, energy_ref, *, own, rows):
    col = col_ref[0]
    mass = per_component(mass_ref[...])
    rr0 = reduced(recv_ref, 0, HP)
    curv0 = reduced(recv_ref, 1, HP)
    alpha0 = rr0 / curv0
    image = add_received(f0_ref[...] + mass * r0_ref[...], col, recv_ref, own)
    image_ref[...] = image
    r_ref[...] = r0_ref[...] - alpha0 * image
    r = jnp.where(own_rows(own), r_ref[...], 0.0)
    rr = jnp.sum(r * r)
    cross = jnp.sum(r * image)
    energy = apply_elements(r_ref, idx_ref, grads_ref, moduli_ref, parts_ref, energy_ref, rows)
    own_curv = energy + jnp.sum(mass * r * r)
    f = scatter(idx_ref, parts_ref, acc_ref, idx_ref.shape[0])
    f_ref[...] = f
    pack(msg_ref, f, col, [rr, own_curv, cross], own)
    sc_ref[0] = rr0
    sc_ref[1] = curv0
    sc_ref[2] = alpha0


def third_kernel(col_ref, sc_ref, recv_ref, r0_ref, r1_ref, f1_ref, image_ref, mass_ref, idx_ref, grads_ref,
                 moduli_ref, msg_ref, r_ref, d_ref, x_ref, out_sc_ref, energy_ref, *, own, rows):
    col = col_ref[0]
    mass = per_component(mass_ref[...])
    rr0, curv0, alpha0 = sc_ref[0], sc_ref[1], sc_ref[2]
    rr1 = reduced(recv_ref, 0, HP)
    own_curv = reduced(recv_ref, 1, HP)
    cross = reduced(recv_ref, 2, HP)
    beta = rr1 / rr0
    curv1 = own_curv + 2.0 * beta * cross + beta * beta * curv0
    alpha1 = rr1 / curv1
    r1 = r1_ref[...]
    image = add_received(f1_ref[...] + mass * r1, col, recv_ref, own) + beta * image_ref[...]
    d = r1 + beta * r0_ref[...]
    d_ref[...] = d
    x_ref[...] = alpha0 * r0_ref[...] + alpha1 * d
    r_ref[...] = r1 - alpha1 * image
    r = jnp.where(own_rows(own), r_ref[...], 0.0)
    rr = jnp.sum(r * r)
    cross = jnp.sum(r * image)
    energy = apply_elements(r_ref, idx_ref, grads_ref, moduli_ref, None, energy_ref, rows)
    own_curv = energy + jnp.sum(mass * r * r)
    rid = lax.broadcasted_iota(jnp.int32, msg_ref.shape, 1)
    msg_ref[...] = jnp.where(rid == 0, rr, jnp.where(rid == 1, own_curv, cross))
    out_sc_ref[0] = rr1
    out_sc_ref[1] = curv1


def last_kernel(sc_ref, recv_ref, r_ref, d_ref, x_ref, idx_ref, out_ref, table_ref, *, rows):
    rr1, curv1 = sc_ref[0], sc_ref[1]
    rr2 = reduced(recv_ref, 0, 8)
    own_curv = reduced(recv_ref, 1, 8)
    cross = reduced(recv_ref, 2, 8)
    beta = rr2 / rr1
    curv2 = own_curv + 2.0 * beta * cross + beta * beta * curv1
    alpha2 = rr2 / curv2
    table_ref[...] = 0.5 * (x_ref[...] + alpha2 * (r_ref[...] + beta * d_ref[...]))
    per = idx_ref.shape[0] // 2
    for j in range(per // 8):
        v = gather(table_ref, [idx_ref[k * per + j * 8 : k * per + j * 8 + 8, :] for k in range(2)], rows)
        for c in range(3):
            got = v[0][c] + v[1][c]
            for q in range(8):
                at = (j * 8 + q) * LANE
                out_ref[c : c + 1, at : at + LANE] = got[q : q + 1, :]


def call(kernel, args, outs, scratch=()):
    spaces = {"s": pltpu.SMEM, "v": pltpu.VMEM, "h": pltpu.VMEM}
    arrays = [pltpu.with_memory_space_constraint(x, pltpu.VMEM) if m == "v" else x for x, m in args]
    return pl.pallas_call(
        kernel,
        out_shape=[o for o, _ in outs],
        in_specs=[pl.BlockSpec(memory_space=spaces[m]) for _, m in args],
        out_specs=[pl.BlockSpec(memory_space=spaces[m]) for _, m in outs],
        scratch_shapes=list(scratch),
    )(*arrays)


def rotated(x, axis, by):
    n = lax.axis_size(axis)
    return lax.ppermute(x, axis, [(i, (i + by) % n) for i in range(n)])


def body(fine_res, node_map, connect, grads, moduli, mass):
    size = lax.axis_size("sub")
    groups = lax.axis_size("grp")
    own = mass.shape[0]
    fine = node_map.shape[1]
    elems = connect.shape[1]
    rows = (own + CI) // LO
    k = CI // LO
    col = lax.axis_index("sub").astype(jnp.int32).reshape(1)
    fcount = 2 * fine // LANE
    ecount = 4 * elems // LANE

    def kept(*shape, dtype=jnp.float32):
        return pltpu.VMEM(shape, dtype), "v"

    table = kept(3 * HP, LO)
    msg = kept(size, HP, LO)
    scalars = lambda n: (jax.ShapeDtypeStruct((n,), jnp.float32), "s")
    acc = pltpu.VMEM((LO, 9 * HP), jnp.float32)
    parts = pltpu.VMEM((9 * ecount, LANE), jnp.float32)
    energy = pltpu.VMEM((8, LANE), jnp.float32)
    mass2 = mass.reshape(own // LANE, LANE)

    partial, lower, upper, map_idx = call(
        functools.partial(rhs_kernel, own=own),
        [(col, "s"), (node_map, "h"), (fine_res, "h"), (mass2, "h")],
        [table, kept(4 * k, LO), kept(3 * k, LO), kept(fcount, LANE, dtype=jnp.int32)],
        [pltpu.VMEM((3 * fcount // 2, LANE), jnp.float32), pltpu.VMEM((9 * fcount, LANE), jnp.float32), acc],
    )
    before = rotated(upper, "sub", 1)
    after = rotated(lower, "sub", -1)
    idx, g, mod = call(
        functools.partial(prep_kernel, own=own),
        [(col, "s"), (connect, "h"), (grads, "h"), (moduli, "h")],
        [kept(ecount, LANE, dtype=jnp.int32), kept(9 * elems // LANE, LANE), kept(2 * elems // LANE, LANE)],
    )
    part, mass_ext = call(
        functools.partial(halo_kernel, own=own, size=size),
        [(col, "s"), (partial, "v"), (before, "v"), (after, "v"), (mass2, "h")],
        [table, kept(HP, LO)],
    )
    sums = [part] + [rotated(part, "grp", i) for i in range(1, groups)]
    elements = [(mass_ext, "v"), (idx, "v"), (g, "v"), (mod, "v")]
    kw = dict(own=own, rows=rows)
    m0, r0, f0 = call(
        functools.partial(first_kernel, groups=groups, **kw),
        [(col, "s")] + [(x, "v") for x in sums] + elements,
        [msg, table, table],
        [parts, acc, energy],
    )
    m0 = lax.all_to_all(m0, "sub", 0, 0)
    m1, r1, f1, image, sc = call(
        functools.partial(second_kernel, **kw),
        [(col, "s"), (m0, "v"), (r0, "v"), (f0, "v")] + elements,
        [msg, table, table, table, scalars(3)],
        [parts, acc, energy],
    )
    m1 = lax.all_to_all(m1, "sub", 0, 0)
    m2, r2, d1, x2, sc = call(
        functools.partial(third_kernel, **kw),
        [(col, "s"), (sc, "s"), (m1, "v"), (r0, "v"), (r1, "v"), (f1, "v"), (image, "v")] + elements,
        [kept(size, 8, LANE), table, table, table, scalars(2)],
        [energy],
    )
    m2 = lax.all_to_all(m2, "sub", 0, 0)
    (out,) = call(
        functools.partial(last_kernel, rows=rows),
        [(sc, "s"), (m2, "v"), (r2, "v"), (d1, "v"), (x2, "v"), (map_idx, "v")],
        [(jax.ShapeDtypeStruct((3, fine), jnp.float32), "h")],
        [pltpu.VMEM((3 * HP, LO), jnp.float32)],
    )
    return out


def solution(mesh):
    in_specs = (
        P(None, ("grp", "sub")),
        P(None, ("grp", "sub")),
        P(None, "sub"),
        P(None, None, "sub"),
        P(None, "sub"),
        P("sub"),
    )
    out_specs = P(None, ("grp", "sub"))
    return jax.shard_map(body, mesh=mesh, in_specs=in_specs, out_specs=out_specs, check_vma=False)
```

time: 95.1 us -> 65.4 us (0.69)
  Pallas kernels: 34 us -> 19.9 us
  local copies, waits for them, and re-layouts: 7.19 us -> 0 us
  blocking collectives: 33.3 us -> 28.5 us
  other arithmetic: 2.23 us -> 0 us
  starting transfers between devices: 9.17 us -> 7.85 us
    pallas_call x5 -> x7, Pallas kernels: 34 us -> 19.9 us  [call(): pl.pallas_call(kernel, out_shape=[o for o, _ in outs], in_specs=[pl.Block...]
    all_to_all x1 -> x0, starting transfers between devices: 5.97 us -> none  [body(): halo = lax.all_to_all(halo, 'sub', 0, 0)]
    reshape x9 -> x0, local copies, waits for them, and re-layouts: 5.66 us -> none  [the longest x1 1.45 us: body(): return out.reshape(3, fine)]
    ppermute x3 -> x5, waiting for transfers between devices: 3.33 us -> 8.74 us  [rotated(): return lax.ppermute(x, axis, [(i, (i + by) % n) for i in range(n)])]
    all_to_all x1 -> x0, waiting for transfers between devices: 4.96 us -> none  [body(): halo = lax.all_to_all(halo, 'sub', 0, 0)]
    ppermute x3 -> x5, starting transfers between devices: 3.2 us -> 7.85 us  [rotated(): return lax.ppermute(x, axis, [(i, (i + by) % n) for i in range(n)])]
    all_to_all x1, blocking collectives: 11.3 us -> 9.74 us  [body(): m1 = lax.all_to_all(m1, 'sub', 0, 0)]
    all_to_all x1, blocking collectives: 11.3 us -> 9.74 us  [body(): m0 = lax.all_to_all(m0, 'sub', 0, 0)]
  transfers between devices with their start and end apart: 4 -> 5, of which waited for: 3 -> 3; matrix products, arithmetic and copies ran while one was open for 2% -> 0% of each run, Pallas kernels for 0% -> 2%
where the time goes in v2:
time: 65.4 us; the launch traced here: 65 us
  blocking collectives  28.5 us (44%)
  Pallas kernels  19.9 us (30%)
  waiting for transfers between devices  8.74 us (13%)
  starting transfers between devices  7.85 us (12%)
    pallas_call x7, Pallas kernels, call(): pl.pallas_call(kernel, out_shape=[o for o, _ in outs], in_specs=[pl.Block...  19.9 us
    all_to_all x1, blocking collectives, body(): m0 = lax.all_to_all(m0, 'sub', 0, 0)  9.74 us
    all_to_all x1, blocking collectives, body(): m1 = lax.all_to_all(m1, 'sub', 0, 0)  9.74 us
    all_to_all x1, blocking collectives, body(): m2 = lax.all_to_all(m2, 'sub', 0, 0)  9.06 us
    ppermute x5, waiting for transfers between devices, rotated(): return lax.ppermute(x, axis, [(i, (i + by) % n) for i in range(n)])  8.74 us
    ppermute x5, starting transfers between devices, rotated(): return lax.ppermute(x, axis, [(i, (i + by) % n) for i in range(n)])  7.85 us
  transfers between devices with their start and end apart: 5, of which 3 were waited for; matrix products, arithmetic and copies ran while one was open for 0% of the time, Pallas kernels for 2%

profile of v2, /device:TPU:0, one launch (start us, length us, event | category | flops | bytes accessed | tf_op | source)
XLA Modules:
  0.0 65.0 jit_solution(6070559586012898261)
XLA Ops:
  0.0 2.5 %shard_map.64 = (f32[48,256]{1,0:T(8,128)S(1)}, f32[16,256]{1,0:T(8,128)S(1)}, f32[12,256]{1,0:T(8,128)S(1)}, s32[64,128]{1,0:T(8,128)S(1)}) custom-call(s32[1]{0:T(128)} %bitcast.col_ref, s32[2,4096]{1,0:T(2,128)} %map_ref.1, f32[3,4096]{1,0:T(4,128)} %fine_ref.1, f32[16,128]{1,0:T(8,128)} %bitcast.2), custom_call_target="tpu_custom_call" | custom-call | tf_op jit(solution)/shard_map/pallas_call | solution.py:321
  2.5 6.1 %collective-permute-start.1 = (f32[16,256]{1,0:T(8,128)S(1)}, f32[16,256]{1,0:T(8,128)S(1)}, u32[]{:S(2)}, u32[]{:S(2)}) collective-permute-start(f32[16,256]{1,0:T(8,128)S(1)} %get-tuple-element.29), channel_id=1, source_target_pairs={{0,7},{1,0},{2,1},{3,2},{4,3},{5,4},{6,5},{7,6},{8,15},{9,8},{10,9... | collective-permute-start | bytes 49160 | tf_op jit(solution)/shard_map/ppermute | solution.py:332
  8.6 0.0 collective-permute-start
  8.6 6.4 %collective-permute-done.before_ref = f32[12,256]{1,0:T(8,128)S(1)} collective-permute-done((f32[12,256]{1,0:T(8,128)S(1)}, f32[12,256]{1,0:T(8,128)S(1)}, u32[]{:S(2)}, u32[]{:S(2)}) %collective-permute-start) | collective-permute-done | bytes 12320 | tf_op jit(solution)/shard_map/ppermute | solution.py:332
  15.0 0.0 collective-permute-done.1.after_ref
  15.0 0.7 %shard_map.65 = (f32[48,256]{1,0:T(8,128)S(1)}, f32[16,256]{1,0:T(8,128)S(1)}) custom-call(s32[1]{0:T(128)} %bitcast.col_ref, f32[48,256]{1,0:T(8,128)S(1)} %get-tuple-element.27.table_ref, f32[12,256]{1,0:T(8,128)S(1)} %collective-permute-done.before_ref, f32[16,256]{1,0:T(8,128)S(1)} %collective-permute-done.1.after_ref, f32[16,128]{1,0:T(8,128)} %bitcast.3), custom_call_target="tpu_custom_call" | custom-call | tf_op jit(solution)/shard_map/pallas_call | solution.py:321
  15.8 0.1 collective-permute-start.4
  15.8 1.6 %collective-permute-start.3 = (f32[48,256]{1,0:T(8,128)S(1)}, f32[48,256]{1,0:T(8,128)S(1)}, u32[]{:S(2)}, u32[]{:S(2)}) collective-permute-start(f32[48,256]{1,0:T(8,128)S(1)} %get-tuple-element.30.refs_0_), channel_id=1, source_target_pairs={{0,16},{8,24},{16,0},{24,8},{1,17},{9,25},{17,1},{25,9},{2,18},{10... | collective-permute-start | bytes 147464 | tf_op jit(solution)/shard_map/ppermute | solution.py:332
  17.4 0.2 collective-permute-start.2
  17.5 1.1 %shard_map.66 = (s32[128,128]{1,0:T(8,128)S(1)}, f32[288,128]{1,0:T(8,128)S(1)}, f32[64,128]{1,0:T(8,128)S(1)}) custom-call(s32[1]{0:T(128)} %bitcast.col_ref, s32[4,4096]{1,0:T(4,128)} %conn_ref.1, f32[3,3,4096]{2,1,0:T(4,128)} %grads_ref.1, f32[2,4096]{1,0:T(2,128)} %moduli_ref.1), custom_call_target="tpu_custom_call" | custom-call | tf_op jit(solution)/shard_map/pallas_call | solution.py:321
  18.6 0.0 collective-permute-done.4.refs_3_
  18.6 1.8 %collective-permute-done.3.refs_2_ = f32[48,256]{1,0:T(8,128)S(1)} collective-permute-done((f32[48,256]{1,0:T(8,128)S(1)}, f32[48,256]{1,0:T(8,128)S(1)}, u32[]{:S(2)}, u32[]{:S(2)}) %collective-permute-start.3) | collective-permute-done | bytes 49184 | tf_op jit(solution)/shard_map/ppermute | solution.py:332
  20.5 0.5 collective-permute-done.2.refs_1_
  20.9 5.0 %shard_map.67 = (f32[8,16,256]{2,1,0:T(8,128)S(1)}, f32[48,256]{1,0:T(8,128)S(1)}, f32[48,256]{1,0:T(8,128)S(1)}) custom-call(s32[1]{0:T(128)} %bitcast.col_ref, f32[48,256]{1,0:T(8,128)S(1)} %get-tuple-element.30.refs_0_, f32[48,256]{1,0:T(8,128)S(1)} %collective-permute-done.2.refs_1_, f32[48,256]{1,0:T(8,128)S(1)} %collective-permute-done.3.refs_2_, ...), custom_call_target="tpu_custom_call" | custom-call | tf_op jit(solution)/shard_map/pallas_call | solution.py:321
  25.9 9.7 %all_to_all.15.recv_ref = f32[8,16,256]{2,1,0:T(8,128)S(1)} all-to-all(f32[8,16,256]{2,1,0:T(8,128)S(1)} %get-tuple-element.35), channel_id=1, replica_groups=mesh['grp'=4,'sub'=8] {'sub'}, dimensions={0} | all-to-all | bytes 262144 | tf_op jit(solution)/shard_map/all_to_all | solution.py:385
  35.7 5.6 %shard_map.68 = (f32[8,16,256]{2,1,0:T(8,128)S(1)}, f32[48,256]{1,0:T(8,128)S(1)}, f32[48,256]{1,0:T(8,128)S(1)}, f32[48,256]{1,0:T(8,128)S(1)}, f32[3]{0:T(128)}) custom-call(s32[1]{0:T(128)} %bitcast.col_ref, f32[8,16,256]{2,1,0:T(8,128)S(1)} %all_to_all.15.recv_ref, f32[48,256]{1,0:T(8,128)S(1)} %get-tuple-element.36.r0_ref, ...), custom_call_target="tpu_custom_call" | custom-call | tf_op jit(solution)/shard_map/pallas_call | solution.py:321
  41.3 9.7 %all_to_all.16.recv_ref = f32[8,16,256]{2,1,0:T(8,128)S(1)} all-to-all(f32[8,16,256]{2,1,0:T(8,128)S(1)} %get-tuple-element.39), channel_id=1, replica_groups=mesh['grp'=4,'sub'=8] {'sub'}, dimensions={0} | all-to-all | bytes 262144 | tf_op jit(solution)/shard_map/all_to_all | solution.py:392
  51.0 2.7 %shard_map.69 = (f32[8,8,128]{2,1,0:T(8,128)S(1)}, f32[48,256]{1,0:T(8,128)S(1)}, f32[48,256]{1,0:T(8,128)S(1)}, f32[48,256]{1,0:T(8,128)S(1)}, f32[2]{0:T(128)}) custom-call(s32[1]{0:T(128)} %bitcast.col_ref, f32[3]{0:T(128)} %get-tuple-element.38.sc_ref, f32[8,16,256]{2,1,0:T(8,128)S(1)} %all_to_all.16.recv_ref, f32[48,256]{1,0:T(8,128)S(1)} %get-tuple-element.36.r0_ref, ...), custom_call_target="tpu_custom_call" | custom-call | tf_op jit(solution)/shard_map/pallas_call | solution.py:321
  53.8 9.1 %all_to_all.17.recv_ref = f32[8,8,128]{2,1,0:T(8,128)S(1)} all-to-all(f32[8,8,128]{2,1,0:T(8,128)S(1)} %get-tuple-element.44), channel_id=1, replica_groups=mesh['grp'=4,'sub'=8] {'sub'}, dimensions={0} | all-to-all | bytes 65536 | tf_op jit(solution)/shard_map/all_to_all | solution.py:399
  62.8 2.2 %shard_map.70 = f32[3,4096]{1,0:T(4,128)} custom-call(f32[2]{0:T(128)} %get-tuple-element.43.sc_ref, f32[8,8,128]{2,1,0:T(8,128)S(1)} %all_to_all.17.recv_ref, f32[48,256]{1,0:T(8,128)S(1)} %get-tuple-element.45.r_ref, f32[48,256]{1,0:T(8,128)S(1)} %get-tuple-element.46.d_ref, f32[48,256]{1,0:T(8,128)S(1)} %get-tuple-element.47.x_ref, ...), custom_call_target="tpu_custom_call" | custom-call | tf_op jit(solution)/shard_map/pallas_call | solution.py:321
Async XLA Ops:
  2.5 12.5 %collective-permute-start.1 = (f32[16,256]{1,0:T(8,128)S(1)}, f32[16,256]{1,0:T(8,128)S(1)}, u32[]{:S(2)}, u32[]{:S(2)}) collective-permute-start(f32[16,256]{1,0:T(8,128)S(1)} %get-tuple-element.29), channel_id=1, source_target_pairs={{0,7},{1,0},{2,1},{3,2},{4,3},{5,4},{6,5},{7,6},{8,15},{9,8},{10,9... | collective-permute-start | bytes 49160 | tf_op jit(solution)/shard_map/ppermute | solution.py:332
  8.6 6.4 %collective-permute-start = (f32[12,256]{1,0:T(8,128)S(1)}, f32[12,256]{1,0:T(8,128)S(1)}, u32[]{:S(2)}, u32[]{:S(2)}) collective-permute-start(f32[12,256]{1,0:T(8,128)S(1)} %get-tuple-element.28), channel_id=1, source_target_pairs={{0,1},{1,2},{2,3},{3,4},{4,5},{5,6},{6,7},{7,0},{8,9},{9,10},{10,1... | collective-permute-start | bytes 36872 | tf_op jit(solution)/shard_map/ppermute | solution.py:332
  15.8 2.9 %collective-permute-start.4 = (f32[48,256]{1,0:T(8,128)S(1)}, f32[48,256]{1,0:T(8,128)S(1)}, u32[]{:S(2)}, u32[]{:S(2)}) collective-permute-start(f32[48,256]{1,0:T(8,128)S(1)} %get-tuple-element.30.refs_0_), channel_id=1, source_target_pairs={{0,24},{8,0},{16,8},{24,16},{1,25},{9,1},{17,9},{25,17},{2,26},{10... | collective-permute-start | bytes 147464 | tf_op jit(solution)/shard_map/ppermute | solution.py:332
  15.8 4.7 %collective-permute-start.3 = (f32[48,256]{1,0:T(8,128)S(1)}, f32[48,256]{1,0:T(8,128)S(1)}, u32[]{:S(2)}, u32[]{:S(2)}) collective-permute-start(f32[48,256]{1,0:T(8,128)S(1)} %get-tuple-element.30.refs_0_), channel_id=1, source_target_pairs={{0,16},{8,24},{16,0},{24,8},{1,17},{9,25},{17,1},{25,9},{2,18},{10... | collective-permute-start | bytes 147464 | tf_op jit(solution)/shard_map/ppermute | solution.py:332
  17.4 3.6 %collective-permute-start.2 = (f32[48,256]{1,0:T(8,128)S(1)}, f32[48,256]{1,0:T(8,128)S(1)}, u32[]{:S(2)}, u32[]{:S(2)}) collective-permute-start(f32[48,256]{1,0:T(8,128)S(1)} %get-tuple-element.30.refs_0_), channel_id=1, source_target_pairs={{0,8},{8,16},{16,24},{24,0},{1,9},{9,17},{17,25},{25,1},{2,10},{10... | collective-permute-start | bytes 147464 | tf_op jit(solution)/shard_map/ppermute | solution.py:332

commit v3 on v2

--- a/solution.py
+++ b/solution.py
@@ -12,6 +12,9 @@
 LO = 256
 HP = 16
 RC = 32
+
+PAIRS = ((0, 0), (1, 1), (2, 2), (0, 1), (0, 2), (1, 2))
+SYM = ((0, 3, 4), (3, 1, 5), (4, 5, 2))
 
 
 def split3(x):
@@ -124,7 +127,7 @@
     return lower, upper
 
 
-def halo_kernel(col_ref, table_ref, before_ref, after_ref, mass_ref, out_ref, mass_out_ref, *, own, size):
+def halo_kernel(col_ref, table_ref, before_ref, after_ref, mass_ref, moduli_ref, out_ref, mass_out_ref, *, own, size):
     col = col_ref[0]
     k = CI // LO
     after = after_ref[...]
@@ -136,31 +139,25 @@
     mass_out_ref[...] = jnp.concatenate([mine, after[3 * k :], pad], axis=0)
 
 
-def apply_elements(table, idx_ref, grads_ref, moduli_ref, parts_ref, energy_ref, rows):
+def apply_elements(table, idx_ref, grads_ref, moduli_ref, strain_ref, parts_ref, rows):
     per = moduli_ref.shape[0] // 2
-    energy_ref[...] = jnp.zeros((8, LANE), jnp.float32)
+    count = 4 * per
 
     def step(j, carry):
         at = j * 8
-        idxs = [idx_ref[pl.ds(k * per + at, 8), :] for k in range(4)]
-        v = gather(table, idxs, rows)
+        v = gather(table, [idx_ref[pl.ds(k * per + at, 8), :] for k in range(4)], rows)
         g = [[grads_ref[pl.ds((d * 3 + a) * per + at, 8), :] for d in range(3)] for a in range(3)]
-        lam = moduli_ref[pl.ds(at, 8), :]
-        mu = moduli_ref[pl.ds(per + at, 8), :]
         w = [[v[a][i] - v[3][i] for i in range(3)] for a in range(3)]
         grad = [[w[0][i] * g[0][j] + w[1][i] * g[1][j] + w[2][i] * g[2][j] for j in range(3)] for i in range(3)]
-        strain = [[0.5 * (grad[i][j] + grad[j][i]) for j in range(3)] for i in range(3)]
-        bulk = lam * (strain[0][0] + strain[1][1] + strain[2][2])
-        stress = [[2.0 * mu * strain[i][j] + (bulk if i == j else 0.0) for j in range(3)] for i in range(3)]
-        work = sum(stress[i][i] * strain[i][i] for i in range(3))
-        work = work + 2.0 * (
-            stress[0][1] * strain[0][1] + stress[0][2] * strain[0][2] + stress[1][2] * strain[1][2]
-        )
-        energy_ref[...] += work
+        strain = [0.5 * (grad[i][j] + grad[j][i]) for i, j in PAIRS]
+        for p in range(6):
+            strain_ref[pl.ds(p * per + at, 8), :] = strain[p]
         if parts_ref is not None:
-            count = 4 * per
+            lam = moduli_ref[pl.ds(at, 8), :]
+            mu = moduli_ref[pl.ds(per + at, 8), :]
+            stress = stresses(strain, lam, mu)
             for i in range(3):
-                f = [sum(stress[i][j] * g[a][j] for j in range(3)) for a in range(3)]
+                f = [sum(stress[SYM[i][j]] * g[a][j] for j in range(3)) for a in range(3)]
                 f.append(-(f[0] + f[1] + f[2]))
                 for a in range(4):
                     pieces = split3(f[a])
@@ -169,7 +166,16 @@
         return carry
 
     lax.fori_loop(0, per // 8, step, 0)
-    return jnp.sum(energy_ref[...])
+
+
+def stresses(strain, lam, mu):
+    bulk = lam * (strain[0] + strain[1] + strain[2])
+    return [2.0 * mu * strain[p] + (bulk if p < 3 else 0.0) for p in range(6)]
+
+
+def work(stress, strain):
+    diag = stress[0] * strain[0] + stress[1] * strain[1] + stress[2] * strain[2]
+    return diag + 2.0 * (stress[3] * strain[3] + stress[4] * strain[4] + stress[5] * strain[5])
 
 
 def own_rows(own):
@@ -194,117 +200,143 @@
     return own_part + jnp.concatenate(pieces, axis=0)
 
 
-def add_received(own_part, col, recv_ref, own):
-    size = recv_ref.shape[0]
-    k = 3 * CI // LO
-    down = recv_ref[pl.ds(jnp.maximum(col - 1, 0), 1)][0]
-    up = recv_ref[pl.ds(jnp.minimum(col + 1, size - 1), 1)][0]
-    return add_halo(own_part, col, down[:k], up[:k], own, size)
-
-
-def pack(msg_ref, table, col, scalars, own):
-    size = msg_ref.shape[0]
-    k = CI // LO
-    lower, upper = shared(table, own)
-    rid = lax.broadcasted_iota(jnp.int32, (HP - 3 * k, LO), 0)
-    tail = jnp.zeros((HP - 3 * k, LO), jnp.float32)
-    for i, s in enumerate(scalars):
-        tail = jnp.where(rid == i, s, tail)
-    msg_ref[...] = jnp.broadcast_to(
-        jnp.concatenate([jnp.zeros((3 * k, LO), jnp.float32), tail], axis=0)[None], msg_ref.shape
-    )
-
-    @pl.when(col > 0)
-    def _():
-        msg_ref[pl.ds(col - 1, 1)] = jnp.concatenate([lower, tail], axis=0)[None]
-
-    @pl.when(col < size - 1)
-    def _():
-        msg_ref[pl.ds(col + 1, 1)] = jnp.concatenate([upper, tail], axis=0)[None]
-
-
-def reduced(recv_ref, i, width):
-    k = 3 * CI // LO if width == HP else 0
-    return jnp.sum(recv_ref[:, k + i : k + i + 1, 0:1])
-
-
-def first_kernel(col_ref, *refs, own, rows, groups):
+def first_kernel(*refs, own, rows, groups):
     sum_refs = refs[:groups]
-    mass_ref, idx_ref, grads_ref, moduli_ref, msg_ref, r_ref, f_ref, parts_ref, acc_ref, energy_ref = refs[groups:]
+    idx_ref, grads_ref, moduli_ref, v_ref, f_ref, lower_ref, upper_ref, strain_ref, parts_ref, acc_ref = refs[groups:]
     total = sum_refs[0][...]
     for ref in sum_refs[1:]:
         total = total + ref[...]
-    r_ref[...] = total
-    r = jnp.where(own_rows(own), total, 0.0)
-    mass = per_component(mass_ref[...])
-    rr = jnp.sum(r * r)
-    energy = apply_elements(r_ref, idx_ref, grads_ref, moduli_ref, parts_ref, energy_ref, rows)
-    curv = energy + jnp.sum(mass * r * r)
+    v_ref[...] = total
+    apply_elements(v_ref, idx_ref, grads_ref, moduli_ref, strain_ref, parts_ref, rows)
     f = scatter(idx_ref, parts_ref, acc_ref, idx_ref.shape[0])
     f_ref[...] = f
-    pack(msg_ref, f, col_ref[0], [rr, curv], own)
-
-
-def second_kernel(col_ref, recv_ref, r0_ref, f0_ref, mass_ref, idx_ref, grads_ref, moduli_ref,
-                  msg_ref, r_ref, f_ref, image_ref, sc_ref, parts_ref, acc_ref, energy_ref, *, own, rows):
-    col = col_ref[0]
+    lower_ref[...], upper_ref[...] = shared(f, own)
+
+
+def second_kernel(col_ref, before_ref, after_ref, v0_ref, f0_ref, mass_ref, idx_ref, grads_ref, moduli_ref,
+                  v_ref, f_ref, lower_ref, upper_ref, strain_ref, parts_ref, acc_ref, *, own, rows, size):
     mass = per_component(mass_ref[...])
-    rr0 = reduced(recv_ref, 0, HP)
-    curv0 = reduced(recv_ref, 1, HP)
-    alpha0 = rr0 / curv0
-    image = add_received(f0_ref[...] + mass * r0_ref[...], col, recv_ref, own)
-    image_ref[...] = image
-    r_ref[...] = r0_ref[...] - alpha0 * image
-    r = jnp.where(own_rows(own), r_ref[...], 0.0)
-    rr = jnp.sum(r * r)
-    cross = jnp.sum(r * image)
-    energy = apply_elements(r_ref, idx_ref, grads_ref, moduli_ref, parts_ref, energy_ref, rows)
-    own_curv = energy + jnp.sum(mass * r * r)
+    v_ref[...] = add_halo(
+        f0_ref[...] + mass * v0_ref[...], col_ref[0], before_ref[...], after_ref[...], own, size
+    )
+    apply_elements(v_ref, idx_ref, grads_ref, moduli_ref, strain_ref, parts_ref, rows)
     f = scatter(idx_ref, parts_ref, acc_ref, idx_ref.shape[0])
     f_ref[...] = f
-    pack(msg_ref, f, col, [rr, own_curv, cross], own)
-    sc_ref[0] = rr0
-    sc_ref[1] = curv0
-    sc_ref[2] = alpha0
-
-
-def third_kernel(col_ref, sc_ref, recv_ref, r0_ref, r1_ref, f1_ref, image_ref, mass_ref, idx_ref, grads_ref,
-                 moduli_ref, msg_ref, r_ref, d_ref, x_ref, out_sc_ref, energy_ref, *, own, rows):
-    col = col_ref[0]
+    lower_ref[...], upper_ref[...] = shared(f, own)
+
+
+def total(x):
+    return jnp.sum(x, axis=(0, 1), keepdims=True)
+
+
+def ratio(a, b):
+    return jnp.where(b > 0.0, a / jnp.where(b > 0.0, b, 1.0), 0.0)
+
+
+def third_kernel(col_ref, before_ref, after_ref, v0_ref, v1_ref, f1_ref, s0_ref, s1_ref, mass_ref, idx_ref,
+                 grads_ref, moduli_ref, msg_ref, v2_ref, s2_ref, *, own, rows, size):
     mass = per_component(mass_ref[...])
-    rr0, curv0, alpha0 = sc_ref[0], sc_ref[1], sc_ref[2]
-    rr1 = reduced(recv_ref, 0, HP)
-    own_curv = reduced(recv_ref, 1, HP)
-    cross = reduced(recv_ref, 2, HP)
-    beta = rr1 / rr0
-    curv1 = own_curv + 2.0 * beta * cross + beta * beta * curv0
+    v2 = add_halo(f1_ref[...] + mass * v1_ref[...], col_ref[0], before_ref[...], after_ref[...], own, size)
+    v2_ref[...] = v2
+    mine = own_rows(own)
+    x0 = jnp.where(mine, v0_ref[...], 0.0)
+    x1 = jnp.where(mine, v1_ref[...], 0.0)
+    x2 = jnp.where(mine, v2, 0.0)
+    rr0 = total(x0 * x0)
+    n1 = total(x1 * x1)
+    usable = (rr0 > 0.0) & (n1 > 0.0)
+    s = jnp.where(usable, jnp.sqrt(jnp.where(usable, rr0, 1.0)) / jnp.sqrt(jnp.where(usable, n1, 1.0)), 1.0)
+    v = s * x1
+    z = s * (s * x2)
+    vv = total(v * v)
+    a = ratio(total(x0 * v), vv)
+    q = ratio(total(z * v), vv)
+    u = x0 - a * v
+    w = z - q * v
+    t = v - a * z
+    uw = total(u * w)
+    ww = total(w * w)
+    g = ratio(uw, ww)
+    b = u - g * w
+    dots = [s, a, q, g, rr0, total(u * u), total(u * v), vv, total(u * t), uw, total(v * t), total(v * w),
+            total(b * b), total(b * v), total(b * w), ww, total(b * t), total(w * t)]
+    weight = jnp.where(mine, mass, 0.0)
+    pairs = [(b, b), (b, v), (b, w), (v, v), (v, w), (w, w)]
+    energy = [total(weight * (l * r)) for l, r in pairs]
+
+    apply_elements(v2_ref, idx_ref, grads_ref, moduli_ref, s2_ref, None, rows)
+    per = moduli_ref.shape[0] // 2
+
+    def step(j, sums):
+        at = j * 8
+        lam = moduli_ref[pl.ds(at, 8), :]
+        mu = moduli_ref[pl.ds(per + at, 8), :]
+        e0, e1, e2 = [[ref[pl.ds(p * per + at, 8), :] for p in range(6)] for ref in (s0_ref, s1_ref, s2_ref)]
+        ev = [s * e for e in e1]
+        ew = [s * (s * e) - q * h for e, h in zip(e2, ev)]
+        eb = [e - a * h - g * k for e, h, k in zip(e0, ev, ew)]
+        tb, tv, tw = [stresses(e, lam, mu) for e in (eb, ev, ew)]
+        new = [work(tb, eb), work(tb, ev), work(tb, ew), work(tv, ev), work(tv, ew), work(tw, ew)]
+        return tuple(x + y for x, y in zip(sums, new))
+
+    sums = lax.fori_loop(0, per // 8, step, (jnp.zeros((8, LANE), jnp.float32),) * 6)
+    numbers = dots + [e + total(x) for e, x in zip(energy, sums)]
+    lane = lax.broadcasted_iota(jnp.int32, (1, LANE), 1)
+    lines_ = []
+    for r in range(8):
+        line = jnp.broadcast_to(numbers[r], (1, LANE))
+        for i in range(r + 8, len(numbers), 8):
+            line = jnp.where(lane < i // 8 * (LANE // 4), line, numbers[i])
+        lines_.append(line)
+    msg_ref[...] = jnp.broadcast_to(jnp.concatenate(lines_, axis=0)[None], msg_ref.shape)
+
+
+def last_kernel(recv_ref, v0_ref, v1_ref, v2_ref, idx_ref, out_ref, table_ref, *, rows):
+    size = recv_ref.shape[0]
+
+    def number(i):
+        at = i // 8 * (LANE // 4)
+        return jnp.broadcast_to(recv_ref[:, i % 8, :][:, at : at + 1], (size, LANE))
+
+    def over(x):
+        return jnp.sum(x, axis=0, keepdims=True)
+
+    (s, a, q, g, rr0, uu, uv, vv, ut, uw, vt, vw, bb, bv, bw, ww, bt, wt,
+     ebb, ebv, ebw, evv, evw, eww) = [number(i) for i in range(24)]
+    inv = 1.0 / s
+    rr0 = over(rr0)
+    curv0 = over(inv * (uv + a * vv))
+    alpha0 = rr0 / curv0
+    a0 = alpha0 * inv
+    d = a - a0
+    rr1 = over(uu + d * (2.0 * uv + d * vv))
+    own1 = over(inv * (ut + d * (uw + q * uv + vt + d * (vw + q * vv))))
+    cross1 = over(inv * (uv + d * vv))
+    beta0 = rr1 / rr0
+    curv1 = own1 + beta0 * (2.0 * cross1 + beta0 * curv0)
     alpha1 = rr1 / curv1
-    r1 = r1_ref[...]
-    image = add_received(f1_ref[...] + mass * r1, col, recv_ref, own) + beta * image_ref[...]
-    d = r1 + beta * r0_ref[...]
-    d_ref[...] = d
-    x_ref[...] = alpha0 * r0_ref[...] + alpha1 * d
-    r_ref[...] = r1 - alpha1 * image
-    r = jnp.where(own_rows(own), r_ref[...], 0.0)
-    rr = jnp.sum(r * r)
-    cross = jnp.sum(r * image)
-    energy = apply_elements(r_ref, idx_ref, grads_ref, moduli_ref, None, energy_ref, rows)
-    own_curv = energy + jnp.sum(mass * r * r)
-    rid = lax.broadcasted_iota(jnp.int32, msg_ref.shape, 1)
-    msg_ref[...] = jnp.where(rid == 0, rr, jnp.where(rid == 1, own_curv, cross))
-    out_sc_ref[0] = rr1
-    out_sc_ref[1] = curv1
-
-
-def last_kernel(sc_ref, recv_ref, r_ref, d_ref, x_ref, idx_ref, out_ref, table_ref, *, rows):
-    rr1, curv1 = sc_ref[0], sc_ref[1]
-    rr2 = reduced(recv_ref, 0, 8)
-    own_curv = reduced(recv_ref, 1, 8)
-    cross = reduced(recv_ref, 2, 8)
-    beta = rr2 / rr1
-    curv2 = own_curv + 2.0 * beta * cross + beta * beta * curv1
+    a1 = alpha1 * inv
+    c2 = a0 * a1
+    m1 = g + c2
+    m0 = a - a0 - a1 * (1.0 + beta0) + q * c2
+    h = d * q + beta0
+    rr2 = over(bb + m0 * (2.0 * bv + m0 * vv) + m1 * (2.0 * (bw + m0 * vw) + m1 * ww))
+    cross2 = over(inv * (bt + d * bw + h * bv + m0 * (vt + d * vw + h * vv) + m1 * (wt + d * ww + h * vw)))
+    own2 = over(ebb + m0 * (2.0 * ebv + m0 * evv) + m1 * (2.0 * (ebw + m0 * evw) + m1 * eww))
+    beta1 = rr2 / rr1
+    curv2 = own2 + beta1 * (2.0 * cross2 + beta1 * curv1)
     alpha2 = rr2 / curv2
-    table_ref[...] = 0.5 * (x_ref[...] + alpha2 * (r_ref[...] + beta * d_ref[...]))
+
+    wide = lambda x: jnp.concatenate([x, x], axis=1)
+    alpha0, alpha1, alpha2, beta0, beta1 = [wide(x) for x in (alpha0, alpha1, alpha2, beta0, beta1)]
+    v0 = v0_ref[...]
+    v1 = v1_ref[...]
+    r1 = v0 - alpha0 * v1
+    d1 = r1 + beta0 * v0
+    image1 = (v1 - alpha0 * v2_ref[...]) + beta0 * v1
+    r2 = r1 - alpha1 * image1
+    d2 = r2 + beta1 * d1
+    table_ref[...] = 0.5 * (alpha0 * v0 + alpha1 * d1 + alpha2 * d2)
     per = idx_ref.shape[0] // 2
     for j in range(per // 8):
         v = gather(table_ref, [idx_ref[k * per + j * 8 : k * per + j * 8 + 8, :] for k in range(2)], rows)
@@ -348,17 +380,16 @@
         return pltpu.VMEM(shape, dtype), "v"
 
     table = kept(3 * HP, LO)
-    msg = kept(size, HP, LO)
-    scalars = lambda n: (jax.ShapeDtypeStruct((n,), jnp.float32), "s")
+    edge = kept(3 * k, LO)
     acc = pltpu.VMEM((LO, 9 * HP), jnp.float32)
     parts = pltpu.VMEM((9 * ecount, LANE), jnp.float32)
-    energy = pltpu.VMEM((8, LANE), jnp.float32)
+    strain = kept(6 * elems // LANE, LANE)
     mass2 = mass.reshape(own // LANE, LANE)
 
     partial, lower, upper, map_idx = call(
         functools.partial(rhs_kernel, own=own),
         [(col, "s"), (node_map, "h"), (fine_res, "h"), (mass2, "h")],
-        [table, kept(4 * k, LO), kept(3 * k, LO), kept(fcount, LANE, dtype=jnp.int32)],
+        [table, kept(4 * k, LO), edge, kept(fcount, LANE, dtype=jnp.int32)],
         [pltpu.VMEM((3 * fcount // 2, LANE), jnp.float32), pltpu.VMEM((9 * fcount, LANE), jnp.float32), acc],
     )
     before = rotated(upper, "sub", 1)
@@ -370,36 +401,38 @@
     )
     part, mass_ext = call(
         functools.partial(halo_kernel, own=own, size=size),
-        [(col, "s"), (partial, "v"), (before, "v"), (after, "v"), (mass2, "h")],
+        [(col, "s"), (partial, "v"), (before, "v"), (after, "v"), (mass2, "h"), (mod, "v")],
         [table, kept(HP, LO)],
     )
     sums = [part] + [rotated(part, "grp", i) for i in range(1, groups)]
-    elements = [(mass_ext, "v"), (idx, "v"), (g, "v"), (mod, "v")]
+    elements = [(idx, "v"), (g, "v"), (mod, "v")]
     kw = dict(own=own, rows=rows)
-    m0, r0, f0 = call(
+    v0, f0, lower, upper, s0 = call(
         functools.partial(first_kernel, groups=groups, **kw),
-        [(col, "s")] + [(x, "v") for x in sums] + elements,
-        [msg, table, table],
-        [parts, acc, energy],
-    )
-    m0 = lax.all_to_all(m0, "sub", 0, 0)
-    m1, r1, f1, image, sc = call(
-        functools.partial(second_kernel, **kw),
-        [(col, "s"), (m0, "v"), (r0, "v"), (f0, "v")] + elements,
-        [msg, table, table, table, scalars(3)],
-        [parts, acc, energy],
-    )
-    m1 = lax.all_to_all(m1, "sub", 0, 0)
-    m2, r2, d1, x2, sc = call(
-        functools.partial(third_kernel, **kw),
-        [(col, "s"), (sc, "s"), (m1, "v"), (r0, "v"), (r1, "v"), (f1, "v"), (image, "v")] + elements,
-        [kept(size, 8, LANE), table, table, table, scalars(2)],
-        [energy],
-    )
-    m2 = lax.all_to_all(m2, "sub", 0, 0)
+        [(x, "v") for x in sums] + elements,
+        [table, table, edge, edge, strain],
+        [parts, acc],
+    )
+    before = rotated(upper, "sub", 1)
+    after = rotated(lower, "sub", -1)
+    v1, f1, lower, upper, s1 = call(
+        functools.partial(second_kernel, size=size, **kw),
+        [(col, "s"), (before, "v"), (after, "v"), (v0, "v"), (f0, "v"), (mass_ext, "v")] + elements,
+        [table, table, edge, edge, strain],
+        [parts, acc],
+    )
+    before = rotated(upper, "sub", 1)
+    after = rotated(lower, "sub", -1)
+    msg, v2 = call(
+        functools.partial(third_kernel, size=size, **kw),
+        [(col, "s")] + [(x, "v") for x in (before, after, v0, v1, f1, s0, s1, mass_ext)] + elements,
+        [kept(size, 8, LANE), table],
+        [pltpu.VMEM((6 * elems // LANE, LANE), jnp.float32)],
+    )
+    recv = lax.all_to_all(msg, "sub", 0, 0)
     (out,) = call(
         functools.partial(last_kernel, rows=rows),
-        [(sc, "s"), (m2, "v"), (r2, "v"), (d1, "v"), (x2, "v"), (map_idx, "v")],
+        [(recv, "v"), (v0, "v"), (v1, "v"), (v2, "v"), (map_idx, "v")],
         [(jax.ShapeDtypeStruct((3, fine), jnp.float32), "h")],
         [pltpu.VMEM((3 * HP, LO), jnp.float32)],
     )

time: 65.4 us -> 60.2 us (0.920)
  blocking collectives: 28.5 us -> 12.5 us
  starting transfers between devices: 7.85 us -> 17.5 us
  waiting for transfers between devices: 8.74 us -> 12.1 us
  Pallas kernels: 19.9 us -> 17.8 us
    all_to_all x3 -> x1, blocking collectives: 28.5 us -> 12.5 us  [body(): recv = lax.all_to_all(msg, 'sub', 0, 0)]
    ppermute x5 -> x9, starting transfers between devices: 7.85 us -> 17.5 us  [rotated(): return lax.ppermute(x, axis, [(i, (i + by) % n) for i in range(n)])]
    ppermute x5 -> x9, waiting for transfers between devices: 8.74 us -> 12.1 us  [rotated(): return lax.ppermute(x, axis, [(i, (i + by) % n) for i in range(n)])]
    pallas_call x7, Pallas kernels: 19.9 us -> 17.8 us  [call(): pl.pallas_call(kernel, out_shape=[o for o, _ in outs], in_specs=[pl.Block...]
  transfers between devices with their start and end apart: 5 -> 9, of which waited for: 3 -> 5; matrix products, arithmetic and copies ran while one was open for 0% -> 0% of each run, Pallas kernels for 2% -> 2%
where the time goes in v3:
time: 60.2 us; the launch traced here: 60 us
  Pallas kernels  17.8 us (30%)
  starting transfers between devices  17.5 us (29%)
  blocking collectives  12.5 us (21%)
  waiting for transfers between devices  12.1 us (20%)
    pallas_call x7, Pallas kernels, call(): pl.pallas_call(kernel, out_shape=[o for o, _ in outs], in_specs=[pl.Block...  17.8 us
    ppermute x9, starting transfers between devices, rotated(): return lax.ppermute(x, axis, [(i, (i + by) % n) for i in range(n)])  17.5 us
    all_to_all x1, blocking collectives, body(): recv = lax.all_to_all(msg, 'sub', 0, 0)  12.5 us
    ppermute x9, waiting for transfers between devices, rotated(): return lax.ppermute(x, axis, [(i, (i + by) % n) for i in range(n)])  12.1 us
  transfers between devices with their start and end apart: 9, of which 5 were waited for; matrix products, arithmetic and copies ran while one was open for 0% of the time, Pallas kernels for 2%

profile of v3, /device:TPU:0, one launch (start us, length us, event | category | flops | bytes accessed | tf_op | source)
XLA Modules:
  0.0 60.0 jit_solution(12691511874657057557)
XLA Ops:
  0.0 2.5 %shard_map.64 = (f32[48,256]{1,0:T(8,128)S(1)}, f32[16,256]{1,0:T(8,128)S(1)}, f32[12,256]{1,0:T(8,128)S(1)}, s32[64,128]{1,0:T(8,128)S(1)}) custom-call(s32[1]{0:T(128)} %bitcast.col_ref, s32[2,4096]{1,0:T(2,128)} %map_ref.1, f32[3,4096]{1,0:T(4,128)} %fine_ref.1, f32[16,128]{1,0:T(8,128)} %bitcast.2), custom_call_target="tpu_custom_call" | custom-call | tf_op jit(solution)/shard_map/pallas_call | solution.py:353
  2.5 6.1 %collective-permute-start.1 = (f32[16,256]{1,0:T(8,128)S(1)}, f32[16,256]{1,0:T(8,128)S(1)}, u32[]{:S(2)}, u32[]{:S(2)}) collective-permute-start(f32[16,256]{1,0:T(8,128)S(1)} %get-tuple-element.28), channel_id=1, source_target_pairs={{0,7},{1,0},{2,1},{3,2},{4,3},{5,4},{6,5},{7,6},{8,15},{9,8},{10,9... | collective-permute-start | bytes 49160 | tf_op jit(solution)/shard_map/ppermute | solution.py:364
  8.6 0.0 collective-permute-start
  8.6 1.1 %shard_map.65 = (s32[128,128]{1,0:T(8,128)S(1)}, f32[288,128]{1,0:T(8,128)S(1)}, f32[64,128]{1,0:T(8,128)S(1)}) custom-call(s32[1]{0:T(128)} %bitcast.col_ref, s32[4,4096]{1,0:T(4,128)} %conn_ref.1, f32[3,3,4096]{2,1,0:T(4,128)} %grads_ref.1, f32[2,4096]{1,0:T(2,128)} %moduli_ref.1), custom_call_target="tpu_custom_call" | custom-call | tf_op jit(solution)/shard_map/pallas_call | solution.py:353
  9.7 5.3 %collective-permute-done.before_ref = f32[12,256]{1,0:T(8,128)S(1)} collective-permute-done((f32[12,256]{1,0:T(8,128)S(1)}, f32[12,256]{1,0:T(8,128)S(1)}, u32[]{:S(2)}, u32[]{:S(2)}) %collective-permute-start) | collective-permute-done | bytes 12320 | tf_op jit(solution)/shard_map/ppermute | solution.py:364
  15.0 0.0 collective-permute-done.1.after_ref
  15.0 0.7 %shard_map.66 = (f32[48,256]{1,0:T(8,128)S(1)}, f32[16,256]{1,0:T(8,128)S(1)}) custom-call(s32[1]{0:T(128)} %bitcast.col_ref, f32[48,256]{1,0:T(8,128)S(1)} %get-tuple-element.26.table_ref, f32[12,256]{1,0:T(8,128)S(1)} %collective-permute-done.before_ref, f32[16,256]{1,0:T(8,128)S(1)} %collective-permute-done.1.after_ref, f32[16,128]{1,0:T(8,128)} %bitcast.3, ...), custom_call_target="tpu_custom_call" | custom-call | tf_op jit(solution)/shard_map/pallas_call | solution.py:353
  15.8 0.1 collective-permute-start.4
  15.8 1.6 %collective-permute-start.3 = (f32[48,256]{1,0:T(8,128)S(1)}, f32[48,256]{1,0:T(8,128)S(1)}, u32[]{:S(2)}, u32[]{:S(2)}) collective-permute-start(f32[48,256]{1,0:T(8,128)S(1)} %get-tuple-element.30.refs_0_), channel_id=1, source_target_pairs={{0,16},{8,24},{16,0},{24,8},{1,17},{9,25},{17,1},{25,9},{2,18},{10... | collective-permute-start | bytes 147464 | tf_op jit(solution)/shard_map/ppermute | solution.py:364
  17.4 0.2 collective-permute-start.2
  17.5 0.0 collective-permute-done.4.refs_3_
  17.6 2.9 %collective-permute-done.3.refs_2_ = f32[48,256]{1,0:T(8,128)S(1)} collective-permute-done((f32[48,256]{1,0:T(8,128)S(1)}, f32[48,256]{1,0:T(8,128)S(1)}, u32[]{:S(2)}, u32[]{:S(2)}) %collective-permute-start.3) | collective-permute-done | bytes 49184 | tf_op jit(solution)/shard_map/ppermute | solution.py:364
  20.5 0.5 collective-permute-done.2.refs_1_
  20.9 4.7 %shard_map.67 = (f32[48,256]{1,0:T(8,128)S(1)}, f32[48,256]{1,0:T(8,128)S(1)}, f32[12,256]{1,0:T(8,128)S(1)}, f32[12,256]{1,0:T(8,128)S(1)}, f32[192,128]{1,0:T(8,128)S(1)}) custom-call(f32[48,256]{1,0:T(8,128)S(1)} %get-tuple-element.30.refs_0_, f32[48,256]{1,0:T(8,128)S(1)} %collective-permute-done.2.refs_1_, ...), custom_call_target="tpu_custom_call" | custom-call | tf_op jit(solution)/shard_map/pallas_call | solution.py:353
  25.7 0.1 collective-permute-start.5
  25.7 4.7 %collective-permute-start.6 = (f32[12,256]{1,0:T(8,128)S(1)}, f32[12,256]{1,0:T(8,128)S(1)}, u32[]{:S(2)}, u32[]{:S(2)}) collective-permute-start(f32[12,256]{1,0:T(8,128)S(1)} %get-tuple-element.34), channel_id=1, source_target_pairs={{0,7},{1,0},{2,1},{3,2},{4,3},{5,4},{6,5},{7,6},{8,15},{9,8},{10,9... | collective-permute-start | bytes 36872 | tf_op jit(solution)/shard_map/ppermute | solution.py:364
  30.5 1.7 %collective-permute-done.5.before_ref = f32[12,256]{1,0:T(8,128)S(1)} collective-permute-done((f32[12,256]{1,0:T(8,128)S(1)}, f32[12,256]{1,0:T(8,128)S(1)}, u32[]{:S(2)}, u32[]{:S(2)}) %collective-permute-start.5) | collective-permute-done | bytes 12320 | tf_op jit(solution)/shard_map/ppermute | solution.py:364
  32.2 0.0 collective-permute-done.6.after_ref
  32.2 4.7 %shard_map.68 = (f32[48,256]{1,0:T(8,128)S(1)}, f32[48,256]{1,0:T(8,128)S(1)}, f32[12,256]{1,0:T(8,128)S(1)}, f32[12,256]{1,0:T(8,128)S(1)}, f32[192,128]{1,0:T(8,128)S(1)}) custom-call(s32[1]{0:T(128)} %bitcast.col_ref, f32[12,256]{1,0:T(8,128)S(1)} %collective-permute-done.5.before_ref, f32[12,256]{1,0:T(8,128)S(1)} %collective-permute-done.6.after_ref, ...), custom_call_target="tpu_custom_call" | custom-call | tf_op jit(solution)/shard_map/pallas_call | solution.py:353
  36.9 0.1 collective-permute-start.7
  37.0 4.8 %collective-permute-start.8 = (f32[12,256]{1,0:T(8,128)S(1)}, f32[12,256]{1,0:T(8,128)S(1)}, u32[]{:S(2)}, u32[]{:S(2)}) collective-permute-start(f32[12,256]{1,0:T(8,128)S(1)} %get-tuple-element.39), channel_id=1, source_target_pairs={{0,7},{1,0},{2,1},{3,2},{4,3},{5,4},{6,5},{7,6},{8,15},{9,8},{10,9... | collective-permute-start | bytes 36872 | tf_op jit(solution)/shard_map/ppermute | solution.py:364
  41.8 1.7 %collective-permute-done.7.before_ref = f32[12,256]{1,0:T(8,128)S(1)} collective-permute-done((f32[12,256]{1,0:T(8,128)S(1)}, f32[12,256]{1,0:T(8,128)S(1)}, u32[]{:S(2)}, u32[]{:S(2)}) %collective-permute-start.7) | collective-permute-done | bytes 12320 | tf_op jit(solution)/shard_map/ppermute | solution.py:364
  43.4 0.0 collective-permute-done.8.after_ref
  43.4 2.4 %shard_map.69 = (f32[8,8,128]{2,1,0:T(8,128)S(1)}, f32[48,256]{1,0:T(8,128)S(1)}) custom-call(s32[1]{0:T(128)} %bitcast.col_ref, f32[12,256]{1,0:T(8,128)S(1)} %collective-permute-done.7.before_ref, f32[12,256]{1,0:T(8,128)S(1)} %collective-permute-done.8.after_ref, f32[48,256]{1,0:T(8,128)S(1)} %get-tuple-element.35.v0_ref, ...), custom_call_target="tpu_custom_call" | custom-call | tf_op jit(solution)/shard_map/pallas_call | solution.py:353
  45.8 12.5 %all_to_all.5.recv_ref = f32[8,8,128]{2,1,0:T(8,128)S(1)} all-to-all(f32[8,8,128]{2,1,0:T(8,128)S(1)} %get-tuple-element.44), channel_id=1, replica_groups=mesh['grp'=4,'sub'=8] {'sub'}, dimensions={0} | all-to-all | bytes 65536 | tf_op jit(solution)/shard_map/all_to_all | solution.py:432
  58.4 1.6 %shard_map.70 = f32[3,4096]{1,0:T(4,128)} custom-call(f32[8,8,128]{2,1,0:T(8,128)S(1)} %all_to_all.5.recv_ref, f32[48,256]{1,0:T(8,128)S(1)} %get-tuple-element.35.v0_ref, f32[48,256]{1,0:T(8,128)S(1)} %get-tuple-element.40.v1_ref, f32[48,256]{1,0:T(8,128)S(1)} %get-tuple-element.45.v2_ref, s32[64,128]{1,0:T(8,128)S(1)} %get-tuple-element.46.idx_ref), custom_call_target="tpu_custom_call" | custom-call | tf_op jit(solution)/shard_map/pallas_call | solution.py:353
Async XLA Ops:
  2.5 12.5 %collective-permute-start.1 = (f32[16,256]{1,0:T(8,128)S(1)}, f32[16,256]{1,0:T(8,128)S(1)}, u32[]{:S(2)}, u32[]{:S(2)}) collective-permute-start(f32[16,256]{1,0:T(8,128)S(1)} %get-tuple-element.28), channel_id=1, source_target_pairs={{0,7},{1,0},{2,1},{3,2},{4,3},{5,4},{6,5},{7,6},{8,15},{9,8},{10,9... | collective-permute-start | bytes 49160 | tf_op jit(solution)/shard_map/ppermute | solution.py:364
  8.6 6.4 %collective-permute-start = (f32[12,256]{1,0:T(8,128)S(1)}, f32[12,256]{1,0:T(8,128)S(1)}, u32[]{:S(2)}, u32[]{:S(2)}) collective-permute-start(f32[12,256]{1,0:T(8,128)S(1)} %get-tuple-element.27), channel_id=1, source_target_pairs={{0,1},{1,2},{2,3},{3,4},{4,5},{5,6},{6,7},{7,0},{8,9},{9,10},{10,1... | collective-permute-start | bytes 36872 | tf_op jit(solution)/shard_map/ppermute | solution.py:364
  15.8 1.8 %collective-permute-start.4 = (f32[48,256]{1,0:T(8,128)S(1)}, f32[48,256]{1,0:T(8,128)S(1)}, u32[]{:S(2)}, u32[]{:S(2)}) collective-permute-start(f32[48,256]{1,0:T(8,128)S(1)} %get-tuple-element.30.refs_0_), channel_id=1, source_target_pairs={{0,24},{8,0},{16,8},{24,16},{1,25},{9,1},{17,9},{25,17},{2,26},{10... | collective-permute-start | bytes 147464 | tf_op jit(solution)/shard_map/ppermute | solution.py:364
  15.8 4.7 %collective-permute-start.3 = (f32[48,256]{1,0:T(8,128)S(1)}, f32[48,256]{1,0:T(8,128)S(1)}, u32[]{:S(2)}, u32[]{:S(2)}) collective-permute-start(f32[48,256]{1,0:T(8,128)S(1)} %get-tuple-element.30.refs_0_), channel_id=1, source_target_pairs={{0,16},{8,24},{16,0},{24,8},{1,17},{9,25},{17,1},{25,9},{2,18},{10... | collective-permute-start | bytes 147464 | tf_op jit(solution)/shard_map/ppermute | solution.py:364
  17.4 3.6 %collective-permute-start.2 = (f32[48,256]{1,0:T(8,128)S(1)}, f32[48,256]{1,0:T(8,128)S(1)}, u32[]{:S(2)}, u32[]{:S(2)}) collective-permute-start(f32[48,256]{1,0:T(8,128)S(1)} %get-tuple-element.30.refs_0_), channel_id=1, source_target_pairs={{0,8},{8,16},{16,24},{24,0},{1,9},{9,17},{17,25},{25,1},{2,10},{10... | collective-permute-start | bytes 147464 | tf_op jit(solution)/shard_map/ppermute | solution.py:364
  25.7 6.5 %collective-permute-start.5 = (f32[12,256]{1,0:T(8,128)S(1)}, f32[12,256]{1,0:T(8,128)S(1)}, u32[]{:S(2)}, u32[]{:S(2)}) collective-permute-start(f32[12,256]{1,0:T(8,128)S(1)} %get-tuple-element.33), channel_id=1, source_target_pairs={{0,1},{1,2},{2,3},{3,4},{4,5},{5,6},{6,7},{7,0},{8,9},{9,10},{10,1... | collective-permute-start | bytes 36872 | tf_op jit(solution)/shard_map/ppermute | solution.py:364
  25.7 6.4 %collective-permute-start.6 = (f32[12,256]{1,0:T(8,128)S(1)}, f32[12,256]{1,0:T(8,128)S(1)}, u32[]{:S(2)}, u32[]{:S(2)}) collective-permute-start(f32[12,256]{1,0:T(8,128)S(1)} %get-tuple-element.34), channel_id=1, source_target_pairs={{0,7},{1,0},{2,1},{3,2},{4,3},{5,4},{6,5},{7,6},{8,15},{9,8},{10,9... | collective-permute-start | bytes 36872 | tf_op jit(solution)/shard_map/ppermute | solution.py:364
  36.9 6.5 %collective-permute-start.7 = (f32[12,256]{1,0:T(8,128)S(1)}, f32[12,256]{1,0:T(8,128)S(1)}, u32[]{:S(2)}, u32[]{:S(2)}) collective-permute-start(f32[12,256]{1,0:T(8,128)S(1)} %get-tuple-element.38), channel_id=1, source_target_pairs={{0,1},{1,2},{2,3},{3,4},{4,5},{5,6},{6,7},{7,0},{8,9},{9,10},{10,1... | collective-permute-start | bytes 36872 | tf_op jit(solution)/shard_map/ppermute | solution.py:364
  37.0 6.4 %collective-permute-start.8 = (f32[12,256]{1,0:T(8,128)S(1)}, f32[12,256]{1,0:T(8,128)S(1)}, u32[]{:S(2)}, u32[]{:S(2)}) collective-permute-start(f32[12,256]{1,0:T(8,128)S(1)} %get-tuple-element.39), channel_id=1, source_target_pairs={{0,7},{1,0},{2,1},{3,2},{4,3},{5,4},{6,5},{7,6},{8,15},{9,8},{10,9... | collective-permute-start | bytes 36872 | tf_op jit(solution)/shard_map/ppermute | solution.py:364

commit v4 on v3

--- a/solution.py
+++ b/solution.py
@@ -42,39 +42,32 @@
     return out
 
 
-def scatter(idx_ref, parts_ref, acc_ref, count):
+def scatter(idx_ref, cols_ref, parts_ref, acc_ref, count):
+    hi_iota = lax.broadcasted_iota(jnp.int32, (HP, LANE), 0)
+    lo_iota = lax.broadcasted_iota(jnp.int32, (LANE, LO), 1).astype(jnp.float32).astype(jnp.bfloat16)
+    one = jnp.bfloat16(1)
+    zero = jnp.bfloat16(0)
     acc_ref[...] = jnp.zeros(acc_ref.shape, jnp.float32)
-    lo_iota = lax.broadcasted_iota(jnp.int32, (LO, LANE), 0)
-    hi_iota = lax.broadcasted_iota(jnp.int32, (HP, LANE), 0)
-
-    def step(i, carry):
+    for i in range(count // RC):
         hot, moved = [], []
-        for t in range(RC):
-            row = i * RC + t
-            ix = idx_ref[pl.ds(row, 1), :]
-            hot.append(jnp.where(lo_iota == (ix & (LO - 1)), 1.0, 0.0).astype(jnp.bfloat16))
-            mask = hi_iota == (ix >> 8)
-            moved.append(
-                jnp.concatenate(
-                    [
-                        jnp.where(mask, parts_ref[pl.ds(p * count + row, 1), :], 0.0).astype(jnp.bfloat16)
-                        for p in range(9)
-                    ],
-                    axis=0,
-                )
-            )
+        for row in range(i * RC, i * RC + RC):
+            lo = (cols_ref[:, row : row + 1] & (LO - 1)).astype(jnp.float32)
+            lo = jnp.broadcast_to(lo, (LANE, LANE)).astype(jnp.bfloat16)
+            hot.append(jnp.where(lo_iota == jnp.concatenate([lo, lo], axis=1), one, zero))
+            mask = hi_iota == (idx_ref[row : row + 1, :] >> 8)
+            group = [
+                jnp.where(mask, parts_ref[p * count + row : p * count + row + 1, :], 0.0).astype(jnp.bfloat16)
+                for p in range(9)
+            ]
+            moved.append(jnp.concatenate(group, axis=0))
         acc_ref[...] += lax.dot_general(
-            jnp.concatenate(hot, axis=1),
             jnp.concatenate(moved, axis=1),
-            (((1,), (1,)), ((), ())),
+            jnp.concatenate(hot, axis=0),
+            (((1,), (0,)), ((), ())),
             preferred_element_type=jnp.float32,
         )
-        return carry
-
-    lax.fori_loop(0, count // RC, step, 0)
-    total = jnp.transpose(acc_ref[...])
     n = 3 * HP
-    return total[:n] + total[n : 2 * n] + total[2 * n :]
+    return acc_ref[:n] + acc_ref[n : 2 * n] + acc_ref[2 * n :]
 
 
 def lines(ref, lead, dst, base, f=lambda x: x):
@@ -83,13 +76,14 @@
         dst[base + q : base + q + 1, :] = f(ref[lead + (slice(q * LANE, (q + 1) * LANE),)])
 
 
-def rhs_kernel(col_ref, map_ref, fine_ref, mass_ref, out_ref, lower_ref, upper_ref, idx_ref,
-               half_ref, parts_ref, acc_ref, *, own):
+def rhs_kernel(col_ref, map_ref, fine_ref, mass_ref, out_ref, one_ref, two_ref, idx_ref,
+               half_ref, cols_ref, parts_ref, acc_ref, *, own):
     half = map_ref.shape[1] // LANE
     count = 2 * half
     shift = col_ref[0] * own
     for k in range(2):
         lines(map_ref, (slice(k, k + 1),), idx_ref, k * half, lambda x: x - shift)
+    cols_ref[...] = jnp.transpose(idx_ref[...])
     for c in range(3):
         lines(fine_ref, (slice(c, c + 1),), half_ref, c * half)
     for c in range(3):
@@ -98,20 +92,20 @@
             for k in range(2):
                 at = (s * 3 + c) * count + k * half
                 parts_ref[at : at + half, :] = pieces[s]
-    table = scatter(idx_ref, parts_ref, acc_ref, count)
+    table = scatter(idx_ref, cols_ref, parts_ref, acc_ref, count)
     out_ref[...] = table
     k = CI // LO
     lower, upper = shared(table, own)
     mass = jnp.concatenate([mass_ref[pl.ds(0, k, stride=2), :], mass_ref[pl.ds(1, k, stride=2), :]], axis=1)
-    lower_ref[...] = jnp.concatenate([lower, mass], axis=0)
-    upper_ref[...] = upper
-
-
-def prep_kernel(col_ref, conn_ref, grads_ref, moduli_ref, idx_ref, g_ref, m_ref, *, own):
+    send(one_ref, two_ref, col_ref[0], jnp.concatenate([lower, mass], axis=0), jnp.concatenate([upper, mass], axis=0))
+
+
+def prep_kernel(col_ref, conn_ref, grads_ref, moduli_ref, idx_ref, cols_ref, g_ref, m_ref, *, own):
     per = moduli_ref.shape[1] // LANE
     shift = col_ref[0] * own
     for a in range(4):
         lines(conn_ref, (slice(a, a + 1),), idx_ref, a * per, lambda x: x - shift)
+    cols_ref[...] = jnp.transpose(idx_ref[...])
     for d in range(3):
         for a in range(3):
             lines(grads_ref, (d, slice(a, a + 1)), g_ref, (d * 3 + a) * per)
@@ -127,11 +121,23 @@
     return lower, upper
 
 
-def halo_kernel(col_ref, table_ref, before_ref, after_ref, mass_ref, moduli_ref, out_ref, mass_out_ref, *, own, size):
+def send(one_ref, two_ref, col, lower, upper):
+    even = col % 2 == 0
+    one_ref[...] = jnp.where(even, upper, lower)
+    two_ref[...] = jnp.where(even, lower, upper)
+
+
+def received(one_ref, two_ref, col):
+    even = col % 2 == 0
+    one, two = one_ref[...], two_ref[...]
+    return jnp.where(even, two, one), jnp.where(even, one, two)
+
+
+def halo_kernel(col_ref, table_ref, one_ref, two_ref, mass_ref, moduli_ref, out_ref, mass_out_ref, *, own, size):
     col = col_ref[0]
     k = CI // LO
-    after = after_ref[...]
-    out_ref[...] = add_halo(table_ref[...], col, before_ref[...], after[: 3 * k], own, size)
+    before, after = received(one_ref, two_ref, col)
+    out_ref[...] = add_halo(table_ref[...], col, before[: 3 * k], after[: 3 * k], own, size)
     mine = jnp.concatenate(
         [mass_ref[pl.ds(0, own // LO, stride=2), :], mass_ref[pl.ds(1, own // LO, stride=2), :]], axis=1
     )
@@ -200,29 +206,29 @@
     return own_part + jnp.concatenate(pieces, axis=0)
 
 
-def first_kernel(*refs, own, rows, groups):
+def first_kernel(col_ref, *refs, own, rows, groups):
     sum_refs = refs[:groups]
-    idx_ref, grads_ref, moduli_ref, v_ref, f_ref, lower_ref, upper_ref, strain_ref, parts_ref, acc_ref = refs[groups:]
+    (idx_ref, cols_ref, grads_ref, moduli_ref, v_ref, f_ref, one_ref, two_ref, strain_ref, parts_ref,
+     acc_ref) = refs[groups:]
     total = sum_refs[0][...]
     for ref in sum_refs[1:]:
         total = total + ref[...]
     v_ref[...] = total
     apply_elements(v_ref, idx_ref, grads_ref, moduli_ref, strain_ref, parts_ref, rows)
-    f = scatter(idx_ref, parts_ref, acc_ref, idx_ref.shape[0])
+    f = scatter(idx_ref, cols_ref, parts_ref, acc_ref, idx_ref.shape[0])
     f_ref[...] = f
-    lower_ref[...], upper_ref[...] = shared(f, own)
-
-
-def second_kernel(col_ref, before_ref, after_ref, v0_ref, f0_ref, mass_ref, idx_ref, grads_ref, moduli_ref,
-                  v_ref, f_ref, lower_ref, upper_ref, strain_ref, parts_ref, acc_ref, *, own, rows, size):
+    send(one_ref, two_ref, col_ref[0], *shared(f, own))
+
+
+def second_kernel(col_ref, one_ref, two_ref, v0_ref, f0_ref, mass_ref, idx_ref, cols_ref, grads_ref, moduli_ref,
+                  v_ref, f_ref, one_out_ref, two_out_ref, strain_ref, parts_ref, acc_ref, *, own, rows, size):
     mass = per_component(mass_ref[...])
-    v_ref[...] = add_halo(
-        f0_ref[...] + mass * v0_ref[...], col_ref[0], before_ref[...], after_ref[...], own, size
-    )
+    before, after = received(one_ref, two_ref, col_ref[0])
+    v_ref[...] = add_halo(f0_ref[...] + mass * v0_ref[...], col_ref[0], before, after, own, size)
     apply_elements(v_ref, idx_ref, grads_ref, moduli_ref, strain_ref, parts_ref, rows)
-    f = scatter(idx_ref, parts_ref, acc_ref, idx_ref.shape[0])
+    f = scatter(idx_ref, cols_ref, parts_ref, acc_ref, idx_ref.shape[0])
     f_ref[...] = f
-    lower_ref[...], upper_ref[...] = shared(f, own)
+    send(one_out_ref, two_out_ref, col_ref[0], *shared(f, own))
 
 
 def total(x):
@@ -233,10 +239,11 @@
     return jnp.where(b > 0.0, a / jnp.where(b > 0.0, b, 1.0), 0.0)
 
 
-def third_kernel(col_ref, before_ref, after_ref, v0_ref, v1_ref, f1_ref, s0_ref, s1_ref, mass_ref, idx_ref,
+def third_kernel(col_ref, one_ref, two_ref, v0_ref, v1_ref, f1_ref, s0_ref, s1_ref, mass_ref, idx_ref,
                  grads_ref, moduli_ref, msg_ref, v2_ref, s2_ref, *, own, rows, size):
     mass = per_component(mass_ref[...])
-    v2 = add_halo(f1_ref[...] + mass * v1_ref[...], col_ref[0], before_ref[...], after_ref[...], own, size)
+    before, after = received(one_ref, two_ref, col_ref[0])
+    v2 = add_halo(f1_ref[...] + mass * v1_ref[...], col_ref[0], before, after, own, size)
     v2_ref[...] = v2
     mine = own_rows(own)
     x0 = jnp.where(mine, v0_ref[...], 0.0)
@@ -364,6 +371,23 @@
     return lax.ppermute(x, axis, [(i, (i + by) % n) for i in range(n)])
 
 
+def traded(one, two):
+    size = lax.axis_size("sub")
+    groups = lax.axis_size("grp")
+    outs = []
+    for x, first in ((one, 0), (two, 1)):
+        pairs = []
+        for g in range(groups):
+            for c in range(size):
+                other = c + 1 if c % 2 == first else c - 1
+                if 0 <= other < size:
+                    pairs.append((g * size + c, g * size + other))
+                else:
+                    pairs.append((g * size + c, (g ^ 1) * size + c))
+        outs.append(lax.ppermute(x, ("grp", "sub"), pairs))
+    return outs
+
+
 def body(fine_res, node_map, connect, grads, moduli, mass):
     size = lax.axis_size("sub")
     groups = lax.axis_size("grp")
@@ -381,51 +405,50 @@
 
     table = kept(3 * HP, LO)
     edge = kept(3 * k, LO)
-    acc = pltpu.VMEM((LO, 9 * HP), jnp.float32)
+    acc = pltpu.VMEM((9 * HP, LO), jnp.float32)
     parts = pltpu.VMEM((9 * ecount, LANE), jnp.float32)
     strain = kept(6 * elems // LANE, LANE)
     mass2 = mass.reshape(own // LANE, LANE)
 
-    partial, lower, upper, map_idx = call(
+    partial, one, two, map_idx = call(
         functools.partial(rhs_kernel, own=own),
         [(col, "s"), (node_map, "h"), (fine_res, "h"), (mass2, "h")],
-        [table, kept(4 * k, LO), edge, kept(fcount, LANE, dtype=jnp.int32)],
-        [pltpu.VMEM((3 * fcount // 2, LANE), jnp.float32), pltpu.VMEM((9 * fcount, LANE), jnp.float32), acc],
-    )
-    before = rotated(upper, "sub", 1)
-    after = rotated(lower, "sub", -1)
-    idx, g, mod = call(
+        [table, kept(4 * k, LO), kept(4 * k, LO), kept(fcount, LANE, dtype=jnp.int32)],
+        [pltpu.VMEM((3 * fcount // 2, LANE), jnp.float32), pltpu.VMEM((LANE, fcount), jnp.int32),
+         pltpu.VMEM((9 * fcount, LANE), jnp.float32), acc],
+    )
+    one, two = traded(one, two)
+    idx, cols, g, mod = call(
         functools.partial(prep_kernel, own=own),
         [(col, "s"), (connect, "h"), (grads, "h"), (moduli, "h")],
-        [kept(ecount, LANE, dtype=jnp.int32), kept(9 * elems // LANE, LANE), kept(2 * elems // LANE, LANE)],
+        [kept(ecount, LANE, dtype=jnp.int32), kept(LANE, ecount, dtype=jnp.int32), kept(9 * elems // LANE, LANE), kept(2 * elems // LANE, LANE)],
     )
     part, mass_ext = call(
         functools.partial(halo_kernel, own=own, size=size),
-        [(col, "s"), (partial, "v"), (before, "v"), (after, "v"), (mass2, "h"), (mod, "v")],
+        [(col, "s"), (partial, "v"), (one, "v"), (two, "v"), (mass2, "h"), (mod, "v")],
         [table, kept(HP, LO)],
     )
     sums = [part] + [rotated(part, "grp", i) for i in range(1, groups)]
     elements = [(idx, "v"), (g, "v"), (mod, "v")]
+    summing = [(idx, "v"), (cols, "v"), (g, "v"), (mod, "v")]
     kw = dict(own=own, rows=rows)
-    v0, f0, lower, upper, s0 = call(
+    v0, f0, one, two, s0 = call(
         functools.partial(first_kernel, groups=groups, **kw),
-        [(x, "v") for x in sums] + elements,
+        [(col, "s")] + [(x, "v") for x in sums] + summing,
         [table, table, edge, edge, strain],
         [parts, acc],
     )
-    before = rotated(upper, "sub", 1)
-    after = rotated(lower, "sub", -1)
-    v1, f1, lower, upper, s1 = call(
+    one, two = traded(one, two)
+    v1, f1, one, two, s1 = call(
         functools.partial(second_kernel, size=size, **kw),
-        [(col, "s"), (before, "v"), (after, "v"), (v0, "v"), (f0, "v"), (mass_ext, "v")] + elements,
+        [(col, "s"), (one, "v"), (two, "v"), (v0, "v"), (f0, "v"), (mass_ext, "v")] + summing,
         [table, table, edge, edge, strain],
         [parts, acc],
     )
-    before = rotated(upper, "sub", 1)
-    after = rotated(lower, "sub", -1)
+    one, two = traded(one, two)
     msg, v2 = call(
         functools.partial(third_kernel, size=size, **kw),
-        [(col, "s")] + [(x, "v") for x in (before, after, v0, v1, f1, s0, s1, mass_ext)] + elements,
+        [(col, "s")] + [(x, "v") for x in (one, two, v0, v1, f1, s0, s1, mass_ext)] + elements,
         [kept(size, 8, LANE), table],
         [pltpu.VMEM((6 * elems // LANE, LANE), jnp.float32)],
     )

time: 60.2 us -> 49.5 us (0.82)
  starting transfers between devices: 17.5 us -> 11.4 us
  waiting for transfers between devices: 12.1 us -> 7.45 us
  blocking collectives: 12.5 us -> 14.7 us
  Pallas kernels: 17.8 us -> 15.7 us
    ppermute x9 -> x3, starting transfers between devices: 17.5 us -> 2.27 us  [rotated(): return lax.ppermute(x, axis, [(i, (i + by) % n) for i in range(n)])]
    ppermute x0 -> x6, starting transfers between devices: none -> 9.09 us  [traded(): outs.append(lax.ppermute(x, ('grp', 'sub'), pairs))]
    ppermute x9 -> x3, waiting for transfers between devices: 12.1 us -> 3.48 us  [rotated(): return lax.ppermute(x, axis, [(i, (i + by) % n) for i in range(n)])]
    ppermute x0 -> x6, waiting for transfers between devices: none -> 3.97 us  [traded(): outs.append(lax.ppermute(x, ('grp', 'sub'), pairs))]
    pallas_call x7, Pallas kernels: 17.8 us -> 15.7 us  [call(): pl.pallas_call(kernel, out_shape=[o for o, _ in outs], in_specs=[pl.Block...]
    all_to_all x1, blocking collectives: 12.5 us -> 14.7 us  [body(): recv = lax.all_to_all(msg, 'sub', 0, 0)]
  transfers between devices with their start and end apart: 9 -> 9, of which waited for: 5 -> 6; matrix products, arithmetic and copies ran while one was open for 0% -> 0% of each run, Pallas kernels for 2% -> 2%
where the time goes in v4:
time: 49.5 us; the launch traced here: 49.2 us
  Pallas kernels  15.7 us (32%)
  blocking collectives  14.7 us (30%)
  starting transfers between devices  11.4 us (23%)
  waiting for transfers between devices  7.45 us (15%)
    pallas_call x7, Pallas kernels, call(): pl.pallas_call(kernel, out_shape=[o for o, _ in outs], in_specs=[pl.Block...  15.7 us
    all_to_all x1, blocking collectives, body(): recv = lax.all_to_all(msg, 'sub', 0, 0)  14.7 us
    ppermute x6, starting transfers between devices, traded(): outs.append(lax.ppermute(x, ('grp', 'sub'), pairs))  9.09 us
    ppermute x6, waiting for transfers between devices, traded(): outs.append(lax.ppermute(x, ('grp', 'sub'), pairs))  3.97 us
    ppermute x3, waiting for transfers between devices, rotated(): return lax.ppermute(x, axis, [(i, (i + by) % n) for i in range(n)])  3.48 us
    ppermute x3, starting transfers between devices, rotated(): return lax.ppermute(x, axis, [(i, (i + by) % n) for i in range(n)])  2.27 us
  transfers between devices with their start and end apart: 9, of which 6 were waited for; matrix products, arithmetic and copies ran while one was open for 0% of the time, Pallas kernels for 2%

profile of v4, /device:TPU:0, one launch (start us, length us, event | category | flops | bytes accessed | tf_op | source)
XLA Modules:
  0.0 49.2 jit_solution(6096151289206554644)
XLA Ops:
  0.0 2.2 %shard_map.64 = (f32[48,256]{1,0:T(8,128)S(1)}, f32[16,256]{1,0:T(8,128)S(1)}, f32[16,256]{1,0:T(8,128)S(1)}, s32[64,128]{1,0:T(8,128)S(1)}) custom-call(s32[1]{0:T(128)} %bitcast.col_ref, s32[2,4096]{1,0:T(2,128)} %map_ref.1, f32[3,4096]{1,0:T(4,128)} %fine_ref.1, f32[16,128]{1,0:T(8,128)} %bitcast.2), custom_call_target="tpu_custom_call" | custom-call | tf_op jit(solution)/shard_map/pallas_call | solution.py:360
  2.2 3.1 %collective-permute-start = (f32[16,256]{1,0:T(8,128)S(1)}, f32[16,256]{1,0:T(8,128)S(1)}, u32[]{:S(2)}, u32[]{:S(2)}) collective-permute-start(f32[16,256]{1,0:T(8,128)S(1)} %get-tuple-element.28), channel_id=1, source_target_pairs={{0,1},{1,0},{2,3},{3,2},{4,5},{5,4},{6,7},{7,6},{8,9},{9,8},{10,11... | collective-permute-start | bytes 49160 | tf_op jit(solution)/shard_map/ppermute | solution.py:387
  5.2 0.0 collective-permute-start.1
  5.2 1.2 %shard_map.65 = (s32[128,128]{1,0:T(8,128)S(1)}, s32[128,128]{1,0:T(8,128)S(1)}, f32[288,128]{1,0:T(8,128)S(1)}, f32[64,128]{1,0:T(8,128)S(1)}) custom-call(s32[1]{0:T(128)} %bitcast.col_ref, s32[4,4096]{1,0:T(4,128)} %conn_ref.1, f32[3,3,4096]{2,1,0:T(4,128)} %grads_ref.1, f32[2,4096]{1,0:T(2,128)} %moduli_ref.1), custom_call_target="tpu_custom_call" | custom-call | tf_op jit(solution)/shard_map/pallas_call | solution.py:360
  6.4 0.5 %collective-permute-done.one_ref = f32[16,256]{1,0:T(8,128)S(1)} collective-permute-done((f32[16,256]{1,0:T(8,128)S(1)}, f32[16,256]{1,0:T(8,128)S(1)}, u32[]{:S(2)}, u32[]{:S(2)}) %collective-permute-start) | collective-permute-done | bytes 16416 | tf_op jit(solution)/shard_map/ppermute | solution.py:387
  7.0 0.0 collective-permute-done.1.two_ref
  7.0 0.7 %shard_map.66 = (f32[48,256]{1,0:T(8,128)S(1)}, f32[16,256]{1,0:T(8,128)S(1)}) custom-call(s32[1]{0:T(128)} %bitcast.col_ref, f32[48,256]{1,0:T(8,128)S(1)} %get-tuple-element.27.table_ref, f32[16,256]{1,0:T(8,128)S(1)} %collective-permute-done.one_ref, f32[16,256]{1,0:T(8,128)S(1)} %collective-permute-done.1.two_ref, f32[16,128]{1,0:T(8,128)} %bitcast.3, ...), custom_call_target="tpu_custom_call" | custom-call | tf_op jit(solution)/shard_map/pallas_call | solution.py:360
  7.7 1.1 %collective-permute-start.4 = (f32[48,256]{1,0:T(8,128)S(1)}, f32[48,256]{1,0:T(8,128)S(1)}, u32[]{:S(2)}, u32[]{:S(2)}) collective-permute-start(f32[48,256]{1,0:T(8,128)S(1)} %get-tuple-element.31.refs_0_), channel_id=1, source_target_pairs={{0,24},{8,0},{16,8},{24,16},{1,25},{9,1},{17,9},{25,17},{2,26},{10... | collective-permute-start | bytes 147464 | tf_op jit(solution)/shard_map/ppermute | solution.py:371
  8.8 1.0 %collective-permute-start.3 = (f32[48,256]{1,0:T(8,128)S(1)}, f32[48,256]{1,0:T(8,128)S(1)}, u32[]{:S(2)}, u32[]{:S(2)}) collective-permute-start(f32[48,256]{1,0:T(8,128)S(1)} %get-tuple-element.31.refs_0_), channel_id=1, source_target_pairs={{0,16},{8,24},{16,0},{24,8},{1,17},{9,25},{17,1},{25,9},{2,18},{10... | collective-permute-start | bytes 147464 | tf_op jit(solution)/shard_map/ppermute | solution.py:371
  9.8 0.2 collective-permute-start.2
  9.9 0.6 %collective-permute-done.4.refs_3_ = f32[48,256]{1,0:T(8,128)S(1)} collective-permute-done((f32[48,256]{1,0:T(8,128)S(1)}, f32[48,256]{1,0:T(8,128)S(1)}, u32[]{:S(2)}, u32[]{:S(2)}) %collective-permute-start.4) | collective-permute-done | bytes 49184 | tf_op jit(solution)/shard_map/ppermute | solution.py:371
  10.6 2.5 %collective-permute-done.3.refs_2_ = f32[48,256]{1,0:T(8,128)S(1)} collective-permute-done((f32[48,256]{1,0:T(8,128)S(1)}, f32[48,256]{1,0:T(8,128)S(1)}, u32[]{:S(2)}, u32[]{:S(2)}) %collective-permute-start.3) | collective-permute-done | bytes 49184 | tf_op jit(solution)/shard_map/ppermute | solution.py:371
  13.0 0.4 collective-permute-done.2.refs_1_
  13.4 3.8 %shard_map.67 = (f32[48,256]{1,0:T(8,128)S(1)}, f32[48,256]{1,0:T(8,128)S(1)}, f32[12,256]{1,0:T(8,128)S(1)}, f32[12,256]{1,0:T(8,128)S(1)}, f32[192,128]{1,0:T(8,128)S(1)}) custom-call(s32[1]{0:T(128)} %bitcast.col_ref, f32[48,256]{1,0:T(8,128)S(1)} %get-tuple-element.31.refs_0_, f32[48,256]{1,0:T(8,128)S(1)} %collective-permute-done.2.refs_1_, ...), custom_call_target="tpu_custom_call" | custom-call | tf_op jit(solution)/shard_map/pallas_call | solution.py:360
  17.2 2.9 %collective-permute-start.5 = (f32[12,256]{1,0:T(8,128)S(1)}, f32[12,256]{1,0:T(8,128)S(1)}, u32[]{:S(2)}, u32[]{:S(2)}) collective-permute-start(f32[12,256]{1,0:T(8,128)S(1)} %get-tuple-element.35), channel_id=1, source_target_pairs={{0,1},{1,0},{2,3},{3,2},{4,5},{5,4},{6,7},{7,6},{8,9},{9,8},{10,11... | collective-permute-start | bytes 36872 | tf_op jit(solution)/shard_map/ppermute | solution.py:387
  20.1 0.0 collective-permute-start.6
  20.1 1.7 %collective-permute-done.5.one_ref = f32[12,256]{1,0:T(8,128)S(1)} collective-permute-done((f32[12,256]{1,0:T(8,128)S(1)}, f32[12,256]{1,0:T(8,128)S(1)}, u32[]{:S(2)}, u32[]{:S(2)}) %collective-permute-start.5) | collective-permute-done | bytes 12320 | tf_op jit(solution)/shard_map/ppermute | solution.py:387
  21.8 0.0 collective-permute-done.6.two_ref
  21.8 3.8 %shard_map.68 = (f32[48,256]{1,0:T(8,128)S(1)}, f32[48,256]{1,0:T(8,128)S(1)}, f32[12,256]{1,0:T(8,128)S(1)}, f32[12,256]{1,0:T(8,128)S(1)}, f32[192,128]{1,0:T(8,128)S(1)}) custom-call(s32[1]{0:T(128)} %bitcast.col_ref, f32[12,256]{1,0:T(8,128)S(1)} %collective-permute-done.5.one_ref, f32[12,256]{1,0:T(8,128)S(1)} %collective-permute-done.6.two_ref, ...), custom_call_target="tpu_custom_call" | custom-call | tf_op jit(solution)/shard_map/pallas_call | solution.py:360
  25.6 3.2 %collective-permute-start.7 = (f32[12,256]{1,0:T(8,128)S(1)}, f32[12,256]{1,0:T(8,128)S(1)}, u32[]{:S(2)}, u32[]{:S(2)}) collective-permute-start(f32[12,256]{1,0:T(8,128)S(1)} %get-tuple-element.40), channel_id=1, source_target_pairs={{0,1},{1,0},{2,3},{3,2},{4,5},{5,4},{6,7},{7,6},{8,9},{9,8},{10,11... | collective-permute-start | bytes 36872 | tf_op jit(solution)/shard_map/ppermute | solution.py:387
  28.8 0.0 collective-permute-start.8
  28.8 1.7 %collective-permute-done.7.one_ref = f32[12,256]{1,0:T(8,128)S(1)} collective-permute-done((f32[12,256]{1,0:T(8,128)S(1)}, f32[12,256]{1,0:T(8,128)S(1)}, u32[]{:S(2)}, u32[]{:S(2)}) %collective-permute-start.7) | collective-permute-done | bytes 12320 | tf_op jit(solution)/shard_map/ppermute | solution.py:387
  30.5 0.0 collective-permute-done.8.two_ref
  30.5 2.4 %shard_map.69 = (f32[8,8,128]{2,1,0:T(8,128)S(1)}, f32[48,256]{1,0:T(8,128)S(1)}) custom-call(s32[1]{0:T(128)} %bitcast.col_ref, f32[12,256]{1,0:T(8,128)S(1)} %collective-permute-done.7.one_ref, f32[12,256]{1,0:T(8,128)S(1)} %collective-permute-done.8.two_ref, f32[48,256]{1,0:T(8,128)S(1)} %get-tuple-element.37.v0_ref, ...), custom_call_target="tpu_custom_call" | custom-call | tf_op jit(solution)/shard_map/pallas_call | solution.py:360
  32.9 14.7 %all_to_all.5.recv_ref = f32[8,8,128]{2,1,0:T(8,128)S(1)} all-to-all(f32[8,8,128]{2,1,0:T(8,128)S(1)} %get-tuple-element.46), channel_id=1, replica_groups=mesh['grp'=4,'sub'=8] {'sub'}, dimensions={0} | all-to-all | bytes 65536 | tf_op jit(solution)/shard_map/all_to_all | solution.py:455
  47.6 1.6 %shard_map.70 = f32[3,4096]{1,0:T(4,128)} custom-call(f32[8,8,128]{2,1,0:T(8,128)S(1)} %all_to_all.5.recv_ref, f32[48,256]{1,0:T(8,128)S(1)} %get-tuple-element.37.v0_ref, f32[48,256]{1,0:T(8,128)S(1)} %get-tuple-element.42.v1_ref, f32[48,256]{1,0:T(8,128)S(1)} %get-tuple-element.47.v2_ref, s32[64,128]{1,0:T(8,128)S(1)} %get-tuple-element.48.idx_ref), custom_call_target="tpu_custom_call" | custom-call | tf_op jit(solution)/shard_map/pallas_call | solution.py:360
Async XLA Ops:
  2.2 4.8 %collective-permute-start = (f32[16,256]{1,0:T(8,128)S(1)}, f32[16,256]{1,0:T(8,128)S(1)}, u32[]{:S(2)}, u32[]{:S(2)}) collective-permute-start(f32[16,256]{1,0:T(8,128)S(1)} %get-tuple-element.28), channel_id=1, source_target_pairs={{0,1},{1,0},{2,3},{3,2},{4,5},{5,4},{6,7},{7,6},{8,9},{9,8},{10,11... | collective-permute-start | bytes 49160 | tf_op jit(solution)/shard_map/ppermute | solution.py:387
  5.2 1.7 %collective-permute-start.1 = (f32[16,256]{1,0:T(8,128)S(1)}, f32[16,256]{1,0:T(8,128)S(1)}, u32[]{:S(2)}, u32[]{:S(2)}) collective-permute-start(f32[16,256]{1,0:T(8,128)S(1)} %get-tuple-element.29), channel_id=1, source_target_pairs={{0,8},{1,2},{2,1},{3,4},{4,3},{5,6},{6,5},{7,15},{8,0},{9,10},{10,... | collective-permute-start | bytes 49160 | tf_op jit(solution)/shard_map/ppermute | solution.py:387
  7.7 2.9 %collective-permute-start.4 = (f32[48,256]{1,0:T(8,128)S(1)}, f32[48,256]{1,0:T(8,128)S(1)}, u32[]{:S(2)}, u32[]{:S(2)}) collective-permute-start(f32[48,256]{1,0:T(8,128)S(1)} %get-tuple-element.31.refs_0_), channel_id=1, source_target_pairs={{0,24},{8,0},{16,8},{24,16},{1,25},{9,1},{17,9},{25,17},{2,26},{10... | collective-permute-start | bytes 147464 | tf_op jit(solution)/shard_map/ppermute | solution.py:371
  8.8 4.2 %collective-permute-start.3 = (f32[48,256]{1,0:T(8,128)S(1)}, f32[48,256]{1,0:T(8,128)S(1)}, u32[]{:S(2)}, u32[]{:S(2)}) collective-permute-start(f32[48,256]{1,0:T(8,128)S(1)} %get-tuple-element.31.refs_0_), channel_id=1, source_target_pairs={{0,16},{8,24},{16,0},{24,8},{1,17},{9,25},{17,1},{25,9},{2,18},{10... | collective-permute-start | bytes 147464 | tf_op jit(solution)/shard_map/ppermute | solution.py:371
  9.8 3.6 %collective-permute-start.2 = (f32[48,256]{1,0:T(8,128)S(1)}, f32[48,256]{1,0:T(8,128)S(1)}, u32[]{:S(2)}, u32[]{:S(2)}) collective-permute-start(f32[48,256]{1,0:T(8,128)S(1)} %get-tuple-element.31.refs_0_), channel_id=1, source_target_pairs={{0,8},{8,16},{16,24},{24,0},{1,9},{9,17},{17,25},{25,1},{2,10},{10... | collective-permute-start | bytes 147464 | tf_op jit(solution)/shard_map/ppermute | solution.py:371
  17.2 4.6 %collective-permute-start.5 = (f32[12,256]{1,0:T(8,128)S(1)}, f32[12,256]{1,0:T(8,128)S(1)}, u32[]{:S(2)}, u32[]{:S(2)}) collective-permute-start(f32[12,256]{1,0:T(8,128)S(1)} %get-tuple-element.35), channel_id=1, source_target_pairs={{0,1},{1,0},{2,3},{3,2},{4,5},{5,4},{6,7},{7,6},{8,9},{9,8},{10,11... | collective-permute-start | bytes 36872 | tf_op jit(solution)/shard_map/ppermute | solution.py:387
  20.1 1.7 %collective-permute-start.6 = (f32[12,256]{1,0:T(8,128)S(1)}, f32[12,256]{1,0:T(8,128)S(1)}, u32[]{:S(2)}, u32[]{:S(2)}) collective-permute-start(f32[12,256]{1,0:T(8,128)S(1)} %get-tuple-element.36), channel_id=1, source_target_pairs={{0,8},{1,2},{2,1},{3,4},{4,3},{5,6},{6,5},{7,15},{8,0},{9,10},{10,... | collective-permute-start | bytes 36872 | tf_op jit(solution)/shard_map/ppermute | solution.py:387
  25.6 4.9 %collective-permute-start.7 = (f32[12,256]{1,0:T(8,128)S(1)}, f32[12,256]{1,0:T(8,128)S(1)}, u32[]{:S(2)}, u32[]{:S(2)}) collective-permute-start(f32[12,256]{1,0:T(8,128)S(1)} %get-tuple-element.40), channel_id=1, source_target_pairs={{0,1},{1,0},{2,3},{3,2},{4,5},{5,4},{6,7},{7,6},{8,9},{9,8},{10,11... | collective-permute-start | bytes 36872 | tf_op jit(solution)/shard_map/ppermute | solution.py:387
  28.8 1.7 %collective-permute-start.8 = (f32[12,256]{1,0:T(8,128)S(1)}, f32[12,256]{1,0:T(8,128)S(1)}, u32[]{:S(2)}, u32[]{:S(2)}) collective-permute-start(f32[12,256]{1,0:T(8,128)S(1)} %get-tuple-element.41), channel_id=1, source_target_pairs={{0,8},{1,2},{2,1},{3,4},{4,3},{5,6},{6,5},{7,15},{8,0},{9,10},{10,... | collective-permute-start | bytes 36872 | tf_op jit(solution)/shard_map/ppermute | solution.py:387

commit v5 on v4

--- a/solution.py
+++ b/solution.py
@@ -11,6 +11,7 @@
 LANE = 128
 LO = 256
 HP = 16
+ROOM = 16 << 20
 RC = 32
 
 PAIRS = ((0, 0), (1, 1), (2, 2), (0, 1), (0, 2), (1, 2))
@@ -70,10 +71,11 @@
     return acc_ref[:n] + acc_ref[n : 2 * n] + acc_ref[2 * n :]
 
 
-def lines(ref, lead, dst, base, f=lambda x: x):
+def lines(ref, lead, dst, base, f=lambda x: x, group=8):
     n = ref.shape[-1] // LANE
     for q in range(n):
-        dst[base + q : base + q + 1, :] = f(ref[lead + (slice(q * LANE, (q + 1) * LANE),)])
+        to = base + q // 8 * group + q % 8
+        dst[to : to + 1, :] = f(ref[lead + (slice(q * LANE, (q + 1) * LANE),)])
 
 
 def rhs_kernel(col_ref, map_ref, fine_ref, mass_ref, out_ref, one_ref, two_ref, idx_ref,
@@ -104,13 +106,22 @@
     per = moduli_ref.shape[1] // LANE
     shift = col_ref[0] * own
     for a in range(4):
-        lines(conn_ref, (slice(a, a + 1),), idx_ref, a * per, lambda x: x - shift)
+        lines(conn_ref, (slice(a, a + 1),), idx_ref, a * 8, lambda x: x - shift, 32)
     cols_ref[...] = jnp.transpose(idx_ref[...])
     for d in range(3):
         for a in range(3):
             lines(grads_ref, (d, slice(a, a + 1)), g_ref, (d * 3 + a) * per)
     for i in range(2):
         lines(moduli_ref, (slice(i, i + 1),), m_ref, i * per)
+
+
+def hot_kernel(cols_ref, hot_ref):
+    lo_iota = lax.broadcasted_iota(jnp.int32, (LANE, LO), 1).astype(jnp.float32).astype(jnp.bfloat16)
+    for row in range(cols_ref.shape[1]):
+        lo = (cols_ref[:, row : row + 1] & (LO - 1)).astype(jnp.float32)
+        lo = jnp.broadcast_to(lo, (LANE, LANE)).astype(jnp.bfloat16)
+        hit = lo_iota == jnp.concatenate([lo, lo], axis=1)
+        hot_ref[row * LANE : (row + 1) * LANE, :] = jnp.where(hit, jnp.bfloat16(1), jnp.bfloat16(0))
 
 
 def shared(table, own):
@@ -145,33 +156,60 @@
     mass_out_ref[...] = jnp.concatenate([mine, after[3 * k :], pad], axis=0)
 
 
-def apply_elements(table, idx_ref, grads_ref, moduli_ref, strain_ref, parts_ref, rows):
+def element_strains(table, idx_ref, grads_ref, strain_ref, j, rows):
+    per = grads_ref.shape[0] // 9
+    at = j * 8
+    v = gather(table, [idx_ref[j * 32 + k * 8 : j * 32 + k * 8 + 8, :] for k in range(4)], rows)
+    g = [[grads_ref[(d * 3 + a) * per + at : (d * 3 + a) * per + at + 8, :] for d in range(3)] for a in range(3)]
+    w = [[v[a][i] - v[3][i] for i in range(3)] for a in range(3)]
+    grad = [[w[0][i] * g[0][j] + w[1][i] * g[1][j] + w[2][i] * g[2][j] for j in range(3)] for i in range(3)]
+    strain = [0.5 * (grad[i][j] + grad[j][i]) for i, j in PAIRS]
+    for p in range(6):
+        strain_ref[p * per + at : p * per + at + 8, :] = strain[p]
+    return strain, g
+
+
+def apply_elements(table, idx_ref, hot_ref, grads_ref, moduli_ref, strain_ref, parts_ref, rows):
     per = moduli_ref.shape[0] // 2
     count = 4 * per
-
-    def step(j, carry):
+    hi_iota = lax.broadcasted_iota(jnp.int32, (HP, LANE), 0)
+    acc = jnp.zeros((9 * HP, LO), jnp.float32)
+
+    def forces(j):
         at = j * 8
-        v = gather(table, [idx_ref[pl.ds(k * per + at, 8), :] for k in range(4)], rows)
-        g = [[grads_ref[pl.ds((d * 3 + a) * per + at, 8), :] for d in range(3)] for a in range(3)]
-        w = [[v[a][i] - v[3][i] for i in range(3)] for a in range(3)]
-        grad = [[w[0][i] * g[0][j] + w[1][i] * g[1][j] + w[2][i] * g[2][j] for j in range(3)] for i in range(3)]
-        strain = [0.5 * (grad[i][j] + grad[j][i]) for i, j in PAIRS]
-        for p in range(6):
-            strain_ref[pl.ds(p * per + at, 8), :] = strain[p]
-        if parts_ref is not None:
-            lam = moduli_ref[pl.ds(at, 8), :]
-            mu = moduli_ref[pl.ds(per + at, 8), :]
-            stress = stresses(strain, lam, mu)
-            for i in range(3):
-                f = [sum(stress[SYM[i][j]] * g[a][j] for j in range(3)) for a in range(3)]
-                f.append(-(f[0] + f[1] + f[2]))
-                for a in range(4):
-                    pieces = split3(f[a])
-                    for s in range(3):
-                        parts_ref[pl.ds((s * 3 + i) * count + a * per + at, 8), :] = pieces[s]
-        return carry
-
-    lax.fori_loop(0, per // 8, step, 0)
+        strain, g = element_strains(table, idx_ref, grads_ref, strain_ref, j, rows)
+        stress = stresses(strain, moduli_ref[at : at + 8, :], moduli_ref[per + at : per + at + 8, :])
+        for i in range(3):
+            f = [sum(stress[SYM[i][j]] * g[a][j] for j in range(3)) for a in range(3)]
+            f.append(-(f[0] + f[1] + f[2]))
+            for a in range(4):
+                pieces = split3(f[a])
+                for s in range(3):
+                    to = (s * 3 + i) * count + j * 32 + a * 8
+                    parts_ref[to : to + 8, :] = pieces[s]
+
+    def summed(j, acc):
+        moved = []
+        for row in range(j * 32, j * 32 + 32):
+            mask = hi_iota == (idx_ref[row : row + 1, :] >> 8)
+            group = [
+                jnp.where(mask, parts_ref[p * count + row : p * count + row + 1, :], 0.0).astype(jnp.bfloat16)
+                for p in range(9)
+            ]
+            moved.append(jnp.concatenate(group, axis=0))
+        return acc + jnp.dot(
+            jnp.concatenate(moved, axis=1),
+            hot_ref[j * 32 * LANE : (j + 1) * 32 * LANE, :],
+            preferred_element_type=jnp.float32,
+        )
+
+    for j in range(per // 8 + 1):
+        if j < per // 8:
+            forces(j)
+        if j > 0:
+            acc = summed(j - 1, acc)
+    n = 3 * HP
+    return acc[:n] + acc[n : 2 * n] + acc[2 * n :]
 
 
 def stresses(strain, lam, mu):
@@ -208,25 +246,22 @@
 
 def first_kernel(col_ref, *refs, own, rows, groups):
     sum_refs = refs[:groups]
-    (idx_ref, cols_ref, grads_ref, moduli_ref, v_ref, f_ref, one_ref, two_ref, strain_ref, parts_ref,
-     acc_ref) = refs[groups:]
+    idx_ref, hot_ref, grads_ref, moduli_ref, v_ref, f_ref, one_ref, two_ref, strain_ref, parts_ref = refs[groups:]
     total = sum_refs[0][...]
     for ref in sum_refs[1:]:
         total = total + ref[...]
     v_ref[...] = total
-    apply_elements(v_ref, idx_ref, grads_ref, moduli_ref, strain_ref, parts_ref, rows)
-    f = scatter(idx_ref, cols_ref, parts_ref, acc_ref, idx_ref.shape[0])
+    f = apply_elements(v_ref, idx_ref, hot_ref, grads_ref, moduli_ref, strain_ref, parts_ref, rows)
     f_ref[...] = f
     send(one_ref, two_ref, col_ref[0], *shared(f, own))
 
 
-def second_kernel(col_ref, one_ref, two_ref, v0_ref, f0_ref, mass_ref, idx_ref, cols_ref, grads_ref, moduli_ref,
-                  v_ref, f_ref, one_out_ref, two_out_ref, strain_ref, parts_ref, acc_ref, *, own, rows, size):
+def second_kernel(col_ref, one_ref, two_ref, v0_ref, f0_ref, mass_ref, idx_ref, hot_ref, grads_ref, moduli_ref,
+                  v_ref, f_ref, one_out_ref, two_out_ref, strain_ref, parts_ref, *, own, rows, size):
     mass = per_component(mass_ref[...])
     before, after = received(one_ref, two_ref, col_ref[0])
     v_ref[...] = add_halo(f0_ref[...] + mass * v0_ref[...], col_ref[0], before, after, own, size)
-    apply_elements(v_ref, idx_ref, grads_ref, moduli_ref, strain_ref, parts_ref, rows)
-    f = scatter(idx_ref, cols_ref, parts_ref, acc_ref, idx_ref.shape[0])
+    f = apply_elements(v_ref, idx_ref, hot_ref, grads_ref, moduli_ref, strain_ref, parts_ref, rows)
     f_ref[...] = f
     send(one_out_ref, two_out_ref, col_ref[0], *shared(f, own))
 
@@ -271,14 +306,15 @@
     pairs = [(b, b), (b, v), (b, w), (v, v), (v, w), (w, w)]
     energy = [total(weight * (l * r)) for l, r in pairs]
 
-    apply_elements(v2_ref, idx_ref, grads_ref, moduli_ref, s2_ref, None, rows)
     per = moduli_ref.shape[0] // 2
+    for j in range(per // 8):
+        element_strains(v2_ref, idx_ref, grads_ref, s2_ref, j, rows)
 
     def step(j, sums):
         at = j * 8
-        lam = moduli_ref[pl.ds(at, 8), :]
-        mu = moduli_ref[pl.ds(per + at, 8), :]
-        e0, e1, e2 = [[ref[pl.ds(p * per + at, 8), :] for p in range(6)] for ref in (s0_ref, s1_ref, s2_ref)]
+        lam = moduli_ref[at : at + 8, :]
+        mu = moduli_ref[per + at : per + at + 8, :]
+        e0, e1, e2 = [[ref[p * per + at : p * per + at + 8, :] for p in range(6)] for ref in (s0_ref, s1_ref, s2_ref)]
         ev = [s * e for e in e1]
         ew = [s * (s * e) - q * h for e, h in zip(e2, ev)]
         eb = [e - a * h - g * k for e, h, k in zip(e0, ev, ew)]
@@ -286,7 +322,9 @@
         new = [work(tb, eb), work(tb, ev), work(tb, ew), work(tv, ev), work(tv, ew), work(tw, ew)]
         return tuple(x + y for x, y in zip(sums, new))
 
-    sums = lax.fori_loop(0, per // 8, step, (jnp.zeros((8, LANE), jnp.float32),) * 6)
+    sums = (jnp.zeros((8, LANE), jnp.float32),) * 6
+    for j in range(per // 8):
+        sums = step(j, sums)
     numbers = dots + [e + total(x) for e, x in zip(energy, sums)]
     lane = lax.broadcasted_iota(jnp.int32, (1, LANE), 1)
     lines_ = []
@@ -354,7 +392,7 @@
                 out_ref[c : c + 1, at : at + LANE] = got[q : q + 1, :]
 
 
-def call(kernel, args, outs, scratch=()):
+def call(kernel, args, outs, scratch=(), limit=None):
     spaces = {"s": pltpu.SMEM, "v": pltpu.VMEM, "h": pltpu.VMEM}
     arrays = [pltpu.with_memory_space_constraint(x, pltpu.VMEM) if m == "v" else x for x, m in args]
     return pl.pallas_call(
@@ -363,6 +401,7 @@
         in_specs=[pl.BlockSpec(memory_space=spaces[m]) for _, m in args],
         out_specs=[pl.BlockSpec(memory_space=spaces[m]) for _, m in outs],
         scratch_shapes=list(scratch),
+        compiler_params=pltpu.CompilerParams(vmem_limit_bytes=limit),
     )(*arrays)
 
 
@@ -429,21 +468,24 @@
         [table, kept(HP, LO)],
     )
     sums = [part] + [rotated(part, "grp", i) for i in range(1, groups)]
+    (hot,) = call(hot_kernel, [(cols, "v")], [kept(ecount * LANE, LO, dtype=jnp.bfloat16)], limit=ROOM)
     elements = [(idx, "v"), (g, "v"), (mod, "v")]
-    summing = [(idx, "v"), (cols, "v"), (g, "v"), (mod, "v")]
+    summing = [(idx, "v"), (hot, "v"), (g, "v"), (mod, "v")]
     kw = dict(own=own, rows=rows)
     v0, f0, one, two, s0 = call(
         functools.partial(first_kernel, groups=groups, **kw),
         [(col, "s")] + [(x, "v") for x in sums] + summing,
         [table, table, edge, edge, strain],
-        [parts, acc],
+        [parts],
+        ROOM,
     )
     one, two = traded(one, two)
     v1, f1, one, two, s1 = call(
         functools.partial(second_kernel, size=size, **kw),
         [(col, "s"), (one, "v"), (two, "v"), (v0, "v"), (f0, "v"), (mass_ext, "v")] + summing,
         [table, table, edge, edge, strain],
-        [parts, acc],
+        [parts],
+        ROOM,
     )
     one, two = traded(one, two)
     msg, v2 = call(

time: 49.5 us -> 47 us (0.949)
  waiting for transfers between devices: 7.45 us -> 5.89 us
  Pallas kernels: 15.7 us -> 14.8 us
    ppermute x3, waiting for transfers between devices: 3.48 us -> 1.92 us  [rotated(): return lax.ppermute(x, axis, [(i, (i + by) % n) for i in range(n)])]
    pallas_call x7 -> x8, Pallas kernels: 15.7 us -> 14.8 us  [call(): pl.pallas_call(kernel, out_shape=[o for o, _ in outs], in_specs=[pl.Block...]
  transfers between devices with their start and end apart: 9 -> 9, of which waited for: 6 -> 5; matrix products, arithmetic and copies ran while one was open for 0% -> 0% of each run, Pallas kernels for 2% -> 6%
where the time goes in v5:
time: 47 us; the launch traced here: 46.7 us
  Pallas kernels  14.8 us (31%)
  blocking collectives  14.7 us (31%)
  starting transfers between devices  11.4 us (24%)
  waiting for transfers between devices  5.89 us (13%)
    pallas_call x8, Pallas kernels, call(): pl.pallas_call(kernel, out_shape=[o for o, _ in outs], in_specs=[pl.Block...  14.8 us
    all_to_all x1, blocking collectives, body(): recv = lax.all_to_all(msg, 'sub', 0, 0)  14.7 us
    ppermute x6, starting transfers between devices, traded(): outs.append(lax.ppermute(x, ('grp', 'sub'), pairs))  9.09 us
    ppermute x6, waiting for transfers between devices, traded(): outs.append(lax.ppermute(x, ('grp', 'sub'), pairs))  3.97 us
    ppermute x3, starting transfers between devices, rotated(): return lax.ppermute(x, axis, [(i, (i + by) % n) for i in range(n)])  2.27 us
    ppermute x3, waiting for transfers between devices, rotated(): return lax.ppermute(x, axis, [(i, (i + by) % n) for i in range(n)])  1.92 us
  transfers between devices with their start and end apart: 9, of which 5 were waited for; matrix products, arithmetic and copies ran while one was open for 0% of the time, Pallas kernels for 6%

profile of v5, /device:TPU:0, one launch (start us, length us, event | category | flops | bytes accessed | tf_op | source)
XLA Modules:
  0.0 46.7 jit_solution(11954884845710166025)
XLA Ops:
  0.0 2.2 %shard_map.64 = (f32[48,256]{1,0:T(8,128)S(1)}, f32[16,256]{1,0:T(8,128)S(1)}, f32[16,256]{1,0:T(8,128)S(1)}, s32[64,128]{1,0:T(8,128)S(1)}) custom-call(s32[1]{0:T(128)} %bitcast.col_ref, s32[2,4096]{1,0:T(2,128)} %map_ref.1, f32[3,4096]{1,0:T(4,128)} %fine_ref.1, f32[16,128]{1,0:T(8,128)} %bitcast.2), custom_call_target="tpu_custom_call" | custom-call | tf_op jit(solution)/shard_map/pallas_call | solution.py:398
  2.2 3.1 %collective-permute-start = (f32[16,256]{1,0:T(8,128)S(1)}, f32[16,256]{1,0:T(8,128)S(1)}, u32[]{:S(2)}, u32[]{:S(2)}) collective-permute-start(f32[16,256]{1,0:T(8,128)S(1)} %get-tuple-element.28), channel_id=1, source_target_pairs={{0,1},{1,0},{2,3},{3,2},{4,5},{5,4},{6,7},{7,6},{8,9},{9,8},{10,11... | collective-permute-start | bytes 49160 | tf_op jit(solution)/shard_map/ppermute | solution.py:426
  5.2 0.0 collective-permute-start.1
  5.2 1.2 %shard_map.65 = (s32[128,128]{1,0:T(8,128)S(1)}, s32[128,128]{1,0:T(8,128)S(1)}, f32[288,128]{1,0:T(8,128)S(1)}, f32[64,128]{1,0:T(8,128)S(1)}) custom-call(s32[1]{0:T(128)} %bitcast.col_ref, s32[4,4096]{1,0:T(4,128)} %conn_ref.1, f32[3,3,4096]{2,1,0:T(4,128)} %grads_ref.1, f32[2,4096]{1,0:T(2,128)} %moduli_ref.1), custom_call_target="tpu_custom_call" | custom-call | tf_op jit(solution)/shard_map/pallas_call | solution.py:398
  6.4 0.5 %collective-permute-done.one_ref = f32[16,256]{1,0:T(8,128)S(1)} collective-permute-done((f32[16,256]{1,0:T(8,128)S(1)}, f32[16,256]{1,0:T(8,128)S(1)}, u32[]{:S(2)}, u32[]{:S(2)}) %collective-permute-start) | collective-permute-done | bytes 16416 | tf_op jit(solution)/shard_map/ppermute | solution.py:426
  7.0 0.0 collective-permute-done.1.two_ref
  7.0 0.7 %shard_map.66 = (f32[48,256]{1,0:T(8,128)S(1)}, f32[16,256]{1,0:T(8,128)S(1)}) custom-call(s32[1]{0:T(128)} %bitcast.col_ref, f32[48,256]{1,0:T(8,128)S(1)} %get-tuple-element.27.table_ref, f32[16,256]{1,0:T(8,128)S(1)} %collective-permute-done.one_ref, f32[16,256]{1,0:T(8,128)S(1)} %collective-permute-done.1.two_ref, f32[16,128]{1,0:T(8,128)} %bitcast.3, ...), custom_call_target="tpu_custom_call" | custom-call | tf_op jit(solution)/shard_map/pallas_call | solution.py:398
  7.7 1.1 %collective-permute-start.4 = (f32[48,256]{1,0:T(8,128)S(1)}, f32[48,256]{1,0:T(8,128)S(1)}, u32[]{:S(2)}, u32[]{:S(2)}) collective-permute-start(f32[48,256]{1,0:T(8,128)S(1)} %get-tuple-element.31.refs_0_), channel_id=1, source_target_pairs={{0,24},{8,0},{16,8},{24,16},{1,25},{9,1},{17,9},{25,17},{2,26},{10... | collective-permute-start | bytes 147464 | tf_op jit(solution)/shard_map/ppermute | solution.py:410
  8.8 1.0 %collective-permute-start.3 = (f32[48,256]{1,0:T(8,128)S(1)}, f32[48,256]{1,0:T(8,128)S(1)}, u32[]{:S(2)}, u32[]{:S(2)}) collective-permute-start(f32[48,256]{1,0:T(8,128)S(1)} %get-tuple-element.31.refs_0_), channel_id=1, source_target_pairs={{0,16},{8,24},{16,0},{24,8},{1,17},{9,25},{17,1},{25,9},{2,18},{10... | collective-permute-start | bytes 147464 | tf_op jit(solution)/shard_map/ppermute | solution.py:410
  9.8 0.2 collective-permute-start.2
  9.9 1.5 %shard_map.67.refs_5_.hot_ref = bf16[16384,256]{1,0:T(8,128)(2,1)S(1)} custom-call(s32[128,128]{1,0:T(8,128)S(1)} %get-tuple-element.33.cols_ref), custom_call_target="tpu_custom_call" | custom-call | tf_op jit(solution)/shard_map/pallas_call | solution.py:398
  11.5 0.0 collective-permute-done.4.refs_3_
  11.5 1.5 %collective-permute-done.3.refs_2_ = f32[48,256]{1,0:T(8,128)S(1)} collective-permute-done((f32[48,256]{1,0:T(8,128)S(1)}, f32[48,256]{1,0:T(8,128)S(1)}, u32[]{:S(2)}, u32[]{:S(2)}) %collective-permute-start.3) | collective-permute-done | bytes 49184 | tf_op jit(solution)/shard_map/ppermute | solution.py:410
  13.0 0.4 collective-permute-done.2.refs_1_
  13.4 2.9 %shard_map.68 = (f32[48,256]{1,0:T(8,128)S(1)}, f32[48,256]{1,0:T(8,128)S(1)}, f32[12,256]{1,0:T(8,128)S(1)}, f32[12,256]{1,0:T(8,128)S(1)}, f32[192,128]{1,0:T(8,128)S(1)}) custom-call(s32[1]{0:T(128)} %bitcast.col_ref, f32[48,256]{1,0:T(8,128)S(1)} %get-tuple-element.31.refs_0_, f32[48,256]{1,0:T(8,128)S(1)} %collective-permute-done.2.refs_1_, ...), custom_call_target="tpu_custom_call" | custom-call | tf_op jit(solution)/shard_map/pallas_call | solution.py:398
  16.4 2.9 %collective-permute-start.5 = (f32[12,256]{1,0:T(8,128)S(1)}, f32[12,256]{1,0:T(8,128)S(1)}, u32[]{:S(2)}, u32[]{:S(2)}) collective-permute-start(f32[12,256]{1,0:T(8,128)S(1)} %get-tuple-element.35), channel_id=1, source_target_pairs={{0,1},{1,0},{2,3},{3,2},{4,5},{5,4},{6,7},{7,6},{8,9},{9,8},{10,11... | collective-permute-start | bytes 36872 | tf_op jit(solution)/shard_map/ppermute | solution.py:426
  19.2 0.0 collective-permute-start.6
  19.2 1.7 %collective-permute-done.5.one_ref = f32[12,256]{1,0:T(8,128)S(1)} collective-permute-done((f32[12,256]{1,0:T(8,128)S(1)}, f32[12,256]{1,0:T(8,128)S(1)}, u32[]{:S(2)}, u32[]{:S(2)}) %collective-permute-start.5) | collective-permute-done | bytes 12320 | tf_op jit(solution)/shard_map/ppermute | solution.py:426
  20.9 0.0 collective-permute-done.6.two_ref
  20.9 2.9 %shard_map.69 = (f32[48,256]{1,0:T(8,128)S(1)}, f32[48,256]{1,0:T(8,128)S(1)}, f32[12,256]{1,0:T(8,128)S(1)}, f32[12,256]{1,0:T(8,128)S(1)}, f32[192,128]{1,0:T(8,128)S(1)}) custom-call(s32[1]{0:T(128)} %bitcast.col_ref, f32[12,256]{1,0:T(8,128)S(1)} %collective-permute-done.5.one_ref, f32[12,256]{1,0:T(8,128)S(1)} %collective-permute-done.6.two_ref, ...), custom_call_target="tpu_custom_call" | custom-call | tf_op jit(solution)/shard_map/pallas_call | solution.py:398
  23.9 3.2 %collective-permute-start.7 = (f32[12,256]{1,0:T(8,128)S(1)}, f32[12,256]{1,0:T(8,128)S(1)}, u32[]{:S(2)}, u32[]{:S(2)}) collective-permute-start(f32[12,256]{1,0:T(8,128)S(1)} %get-tuple-element.40), channel_id=1, source_target_pairs={{0,1},{1,0},{2,3},{3,2},{4,5},{5,4},{6,7},{7,6},{8,9},{9,8},{10,11... | collective-permute-start | bytes 36872 | tf_op jit(solution)/shard_map/ppermute | solution.py:426
  27.0 0.0 collective-permute-start.8
  27.0 1.7 %collective-permute-done.7.one_ref = f32[12,256]{1,0:T(8,128)S(1)} collective-permute-done((f32[12,256]{1,0:T(8,128)S(1)}, f32[12,256]{1,0:T(8,128)S(1)}, u32[]{:S(2)}, u32[]{:S(2)}) %collective-permute-start.7) | collective-permute-done | bytes 12320 | tf_op jit(solution)/shard_map/ppermute | solution.py:426
  28.8 0.0 collective-permute-done.8.two_ref
  28.8 1.7 %shard_map.70 = (f32[8,8,128]{2,1,0:T(8,128)S(1)}, f32[48,256]{1,0:T(8,128)S(1)}) custom-call(s32[1]{0:T(128)} %bitcast.col_ref, f32[12,256]{1,0:T(8,128)S(1)} %collective-permute-done.7.one_ref, f32[12,256]{1,0:T(8,128)S(1)} %collective-permute-done.8.two_ref, f32[48,256]{1,0:T(8,128)S(1)} %get-tuple-element.37.v0_ref, ...), custom_call_target="tpu_custom_call" | custom-call | tf_op jit(solution)/shard_map/pallas_call | solution.py:398
  30.4 14.7 %all_to_all.5.recv_ref = f32[8,8,128]{2,1,0:T(8,128)S(1)} all-to-all(f32[8,8,128]{2,1,0:T(8,128)S(1)} %get-tuple-element.46), channel_id=1, replica_groups=mesh['grp'=4,'sub'=8] {'sub'}, dimensions={0} | all-to-all | bytes 65536 | tf_op jit(solution)/shard_map/all_to_all | solution.py:497
  45.1 1.6 %shard_map.71 = f32[3,4096]{1,0:T(4,128)} custom-call(f32[8,8,128]{2,1,0:T(8,128)S(1)} %all_to_all.5.recv_ref, f32[48,256]{1,0:T(8,128)S(1)} %get-tuple-element.37.v0_ref, f32[48,256]{1,0:T(8,128)S(1)} %get-tuple-element.42.v1_ref, f32[48,256]{1,0:T(8,128)S(1)} %get-tuple-element.47.v2_ref, s32[64,128]{1,0:T(8,128)S(1)} %get-tuple-element.48.idx_ref), custom_call_target="tpu_custom_call" | custom-call | tf_op jit(solution)/shard_map/pallas_call | solution.py:398
Async XLA Ops:
  2.2 4.8 %collective-permute-start = (f32[16,256]{1,0:T(8,128)S(1)}, f32[16,256]{1,0:T(8,128)S(1)}, u32[]{:S(2)}, u32[]{:S(2)}) collective-permute-start(f32[16,256]{1,0:T(8,128)S(1)} %get-tuple-element.28), channel_id=1, source_target_pairs={{0,1},{1,0},{2,3},{3,2},{4,5},{5,4},{6,7},{7,6},{8,9},{9,8},{10,11... | collective-permute-start | bytes 49160 | tf_op jit(solution)/shard_map/ppermute | solution.py:426
  5.2 1.7 %collective-permute-start.1 = (f32[16,256]{1,0:T(8,128)S(1)}, f32[16,256]{1,0:T(8,128)S(1)}, u32[]{:S(2)}, u32[]{:S(2)}) collective-permute-start(f32[16,256]{1,0:T(8,128)S(1)} %get-tuple-element.29), channel_id=1, source_target_pairs={{0,8},{1,2},{2,1},{3,4},{4,3},{5,6},{6,5},{7,15},{8,0},{9,10},{10,... | collective-permute-start | bytes 49160 | tf_op jit(solution)/shard_map/ppermute | solution.py:426
  7.7 3.8 %collective-permute-start.4 = (f32[48,256]{1,0:T(8,128)S(1)}, f32[48,256]{1,0:T(8,128)S(1)}, u32[]{:S(2)}, u32[]{:S(2)}) collective-permute-start(f32[48,256]{1,0:T(8,128)S(1)} %get-tuple-element.31.refs_0_), channel_id=1, source_target_pairs={{0,24},{8,0},{16,8},{24,16},{1,25},{9,1},{17,9},{25,17},{2,26},{10... | collective-permute-start | bytes 147464 | tf_op jit(solution)/shard_map/ppermute | solution.py:410
  8.8 4.2 %collective-permute-start.3 = (f32[48,256]{1,0:T(8,128)S(1)}, f32[48,256]{1,0:T(8,128)S(1)}, u32[]{:S(2)}, u32[]{:S(2)}) collective-permute-start(f32[48,256]{1,0:T(8,128)S(1)} %get-tuple-element.31.refs_0_), channel_id=1, source_target_pairs={{0,16},{8,24},{16,0},{24,8},{1,17},{9,25},{17,1},{25,9},{2,18},{10... | collective-permute-start | bytes 147464 | tf_op jit(solution)/shard_map/ppermute | solution.py:410
  9.8 3.6 %collective-permute-start.2 = (f32[48,256]{1,0:T(8,128)S(1)}, f32[48,256]{1,0:T(8,128)S(1)}, u32[]{:S(2)}, u32[]{:S(2)}) collective-permute-start(f32[48,256]{1,0:T(8,128)S(1)} %get-tuple-element.31.refs_0_), channel_id=1, source_target_pairs={{0,8},{8,16},{16,24},{24,0},{1,9},{9,17},{17,25},{25,1},{2,10},{10... | collective-permute-start | bytes 147464 | tf_op jit(solution)/shard_map/ppermute | solution.py:410
  16.4 4.6 %collective-permute-start.5 = (f32[12,256]{1,0:T(8,128)S(1)}, f32[12,256]{1,0:T(8,128)S(1)}, u32[]{:S(2)}, u32[]{:S(2)}) collective-permute-start(f32[12,256]{1,0:T(8,128)S(1)} %get-tuple-element.35), channel_id=1, source_target_pairs={{0,1},{1,0},{2,3},{3,2},{4,5},{5,4},{6,7},{7,6},{8,9},{9,8},{10,11... | collective-permute-start | bytes 36872 | tf_op jit(solution)/shard_map/ppermute | solution.py:426
  19.2 1.7 %collective-permute-start.6 = (f32[12,256]{1,0:T(8,128)S(1)}, f32[12,256]{1,0:T(8,128)S(1)}, u32[]{:S(2)}, u32[]{:S(2)}) collective-permute-start(f32[12,256]{1,0:T(8,128)S(1)} %get-tuple-element.36), channel_id=1, source_target_pairs={{0,8},{1,2},{2,1},{3,4},{4,3},{5,6},{6,5},{7,15},{8,0},{9,10},{10,... | collective-permute-start | bytes 36872 | tf_op jit(solution)/shard_map/ppermute | solution.py:426
  23.9 4.9 %collective-permute-start.7 = (f32[12,256]{1,0:T(8,128)S(1)}, f32[12,256]{1,0:T(8,128)S(1)}, u32[]{:S(2)}, u32[]{:S(2)}) collective-permute-start(f32[12,256]{1,0:T(8,128)S(1)} %get-tuple-element.40), channel_id=1, source_target_pairs={{0,1},{1,0},{2,3},{3,2},{4,5},{5,4},{6,7},{7,6},{8,9},{9,8},{10,11... | collective-permute-start | bytes 36872 | tf_op jit(solution)/shard_map/ppermute | solution.py:426
  27.0 1.7 %collective-permute-start.8 = (f32[12,256]{1,0:T(8,128)S(1)}, f32[12,256]{1,0:T(8,128)S(1)}, u32[]{:S(2)}, u32[]{:S(2)}) collective-permute-start(f32[12,256]{1,0:T(8,128)S(1)} %get-tuple-element.41), channel_id=1, source_target_pairs={{0,8},{1,2},{2,1},{3,4},{4,3},{5,6},{6,5},{7,15},{8,0},{9,10},{10,... | collective-permute-start | bytes 36872 | tf_op jit(solution)/shard_map/ppermute | solution.py:426

commit v6 on v5

--- a/solution.py
+++ b/solution.py
@@ -78,7 +78,7 @@
         dst[to : to + 1, :] = f(ref[lead + (slice(q * LANE, (q + 1) * LANE),)])
 
 
-def rhs_kernel(col_ref, map_ref, fine_ref, mass_ref, out_ref, one_ref, two_ref, idx_ref,
+def rhs_kernel(col_ref, map_ref, fine_ref, mass_ref, out_ref, one_ref, two_ref, idx_ref, mine_ref,
                half_ref, cols_ref, parts_ref, acc_ref, *, own):
     half = map_ref.shape[1] // LANE
     count = 2 * half
@@ -98,7 +98,11 @@
     out_ref[...] = table
     k = CI // LO
     lower, upper = shared(table, own)
-    mass = jnp.concatenate([mass_ref[pl.ds(0, k, stride=2), :], mass_ref[pl.ds(1, k, stride=2), :]], axis=1)
+    mine = jnp.concatenate(
+        [mass_ref[pl.ds(0, own // LO, stride=2), :], mass_ref[pl.ds(1, own // LO, stride=2), :]], axis=1
+    )
+    mine_ref[...] = mine
+    mass = mine[:k]
     send(one_ref, two_ref, col_ref[0], jnp.concatenate([lower, mass], axis=0), jnp.concatenate([upper, mass], axis=0))
 
 
@@ -144,16 +148,13 @@
     return jnp.where(even, two, one), jnp.where(even, one, two)
 
 
-def halo_kernel(col_ref, table_ref, one_ref, two_ref, mass_ref, moduli_ref, out_ref, mass_out_ref, *, own, size):
+def halo_kernel(col_ref, table_ref, one_ref, two_ref, mine_ref, moduli_ref, out_ref, mass_out_ref, *, own, size):
     col = col_ref[0]
     k = CI // LO
     before, after = received(one_ref, two_ref, col)
     out_ref[...] = add_halo(table_ref[...], col, before[: 3 * k], after[: 3 * k], own, size)
-    mine = jnp.concatenate(
-        [mass_ref[pl.ds(0, own // LO, stride=2), :], mass_ref[pl.ds(1, own // LO, stride=2), :]], axis=1
-    )
     pad = jnp.zeros((HP - own // LO - k, LO), jnp.float32)
-    mass_out_ref[...] = jnp.concatenate([mine, after[3 * k :], pad], axis=0)
+    mass_out_ref[...] = jnp.concatenate([mine_ref[...], after[3 * k :], pad], axis=0)
 
 
 def element_strains(table, idx_ref, grads_ref, strain_ref, j, rows):
@@ -169,11 +170,11 @@
     return strain, g
 
 
-def apply_elements(table, idx_ref, hot_ref, grads_ref, moduli_ref, strain_ref, parts_ref, rows):
+def apply_elements(col, table, idx_ref, hot_ref, grads_ref, moduli_ref, strain_ref, parts_ref, acc_ref, rows):
     per = moduli_ref.shape[0] // 2
     count = 4 * per
     hi_iota = lax.broadcasted_iota(jnp.int32, (HP, LANE), 0)
-    acc = jnp.zeros((9 * HP, LO), jnp.float32)
+    acc_ref[...] = jnp.zeros((9 * HP, LO), jnp.float32)
 
     def forces(j):
         at = j * 8
@@ -188,7 +189,7 @@
                     to = (s * 3 + i) * count + j * 32 + a * 8
                     parts_ref[to : to + 8, :] = pieces[s]
 
-    def summed(j, acc):
+    def summed(j):
         moved = []
         for row in range(j * 32, j * 32 + 32):
             mask = hi_iota == (idx_ref[row : row + 1, :] >> 8)
@@ -197,19 +198,23 @@
                 for p in range(9)
             ]
             moved.append(jnp.concatenate(group, axis=0))
-        return acc + jnp.dot(
+        acc_ref[...] += jnp.dot(
             jnp.concatenate(moved, axis=1),
             hot_ref[j * 32 * LANE : (j + 1) * 32 * LANE, :],
             preferred_element_type=jnp.float32,
         )
 
     for j in range(per // 8 + 1):
-        if j < per // 8:
-            forces(j)
-        if j > 0:
-            acc = summed(j - 1, acc)
+
+        @pl.when(col >= 0)
+        def _():
+            if j > 0:
+                summed(j - 1)
+            if j < per // 8:
+                forces(j)
+
     n = 3 * HP
-    return acc[:n] + acc[n : 2 * n] + acc[2 * n :]
+    return acc_ref[:n] + acc_ref[n : 2 * n] + acc_ref[2 * n :]
 
 
 def stresses(strain, lam, mu):
@@ -246,22 +251,23 @@
 
 def first_kernel(col_ref, *refs, own, rows, groups):
     sum_refs = refs[:groups]
-    idx_ref, hot_ref, grads_ref, moduli_ref, v_ref, f_ref, one_ref, two_ref, strain_ref, parts_ref = refs[groups:]
+    (idx_ref, hot_ref, grads_ref, moduli_ref, v_ref, f_ref, one_ref, two_ref, strain_ref, parts_ref,
+     acc_ref) = refs[groups:]
     total = sum_refs[0][...]
     for ref in sum_refs[1:]:
         total = total + ref[...]
     v_ref[...] = total
-    f = apply_elements(v_ref, idx_ref, hot_ref, grads_ref, moduli_ref, strain_ref, parts_ref, rows)
+    f = apply_elements(col_ref[0], v_ref, idx_ref, hot_ref, grads_ref, moduli_ref, strain_ref, parts_ref, acc_ref, rows)
     f_ref[...] = f
     send(one_ref, two_ref, col_ref[0], *shared(f, own))
 
 
 def second_kernel(col_ref, one_ref, two_ref, v0_ref, f0_ref, mass_ref, idx_ref, hot_ref, grads_ref, moduli_ref,
-                  v_ref, f_ref, one_out_ref, two_out_ref, strain_ref, parts_ref, *, own, rows, size):
+                  v_ref, f_ref, one_out_ref, two_out_ref, strain_ref, parts_ref, acc_ref, *, own, rows, size):
     mass = per_component(mass_ref[...])
     before, after = received(one_ref, two_ref, col_ref[0])
     v_ref[...] = add_halo(f0_ref[...] + mass * v0_ref[...], col_ref[0], before, after, own, size)
-    f = apply_elements(v_ref, idx_ref, hot_ref, grads_ref, moduli_ref, strain_ref, parts_ref, rows)
+    f = apply_elements(col_ref[0], v_ref, idx_ref, hot_ref, grads_ref, moduli_ref, strain_ref, parts_ref, acc_ref, rows)
     f_ref[...] = f
     send(one_out_ref, two_out_ref, col_ref[0], *shared(f, own))
 
@@ -449,10 +455,10 @@
     strain = kept(6 * elems // LANE, LANE)
     mass2 = mass.reshape(own // LANE, LANE)
 
-    partial, one, two, map_idx = call(
+    partial, one, two, map_idx, mine = call(
         functools.partial(rhs_kernel, own=own),
         [(col, "s"), (node_map, "h"), (fine_res, "h"), (mass2, "h")],
-        [table, kept(4 * k, LO), kept(4 * k, LO), kept(fcount, LANE, dtype=jnp.int32)],
+        [table, kept(4 * k, LO), kept(4 * k, LO), kept(fcount, LANE, dtype=jnp.int32), kept(own // LO, LO)],
         [pltpu.VMEM((3 * fcount // 2, LANE), jnp.float32), pltpu.VMEM((LANE, fcount), jnp.int32),
          pltpu.VMEM((9 * fcount, LANE), jnp.float32), acc],
     )
@@ -464,7 +470,7 @@
     )
     part, mass_ext = call(
         functools.partial(halo_kernel, own=own, size=size),
-        [(col, "s"), (partial, "v"), (one, "v"), (two, "v"), (mass2, "h"), (mod, "v")],
+        [(col, "s"), (partial, "v"), (one, "v"), (two, "v"), (mine, "v"), (mod, "v")],
         [table, kept(HP, LO)],
     )
     sums = [part] + [rotated(part, "grp", i) for i in range(1, groups)]
@@ -476,7 +482,7 @@
         functools.partial(first_kernel, groups=groups, **kw),
         [(col, "s")] + [(x, "v") for x in sums] + summing,
         [table, table, edge, edge, strain],
-        [parts],
+        [parts, acc],
         ROOM,
     )
     one, two = traded(one, two)
@@ -484,7 +490,7 @@
         functools.partial(second_kernel, size=size, **kw),
         [(col, "s"), (one, "v"), (two, "v"), (v0, "v"), (f0, "v"), (mass_ext, "v")] + summing,
         [table, table, edge, edge, strain],
-        [parts],
+        [parts, acc],
         ROOM,
     )
     one, two = traded(one, two)

time: 47 us -> 46.2 us (0.983)
  Pallas kernels: 14.8 us -> 14 us
    pallas_call x8, Pallas kernels: 14.8 us -> 14 us  [call(): pl.pallas_call(kernel, out_shape=[o for o, _ in outs], in_specs=[pl.Block...]
where the time goes in v6:
time: 46.2 us; the launch traced here: 45.9 us
  blocking collectives  14.7 us (32%)
  Pallas kernels  14 us (30%)
  starting transfers between devices  11.4 us (25%)
  waiting for transfers between devices  5.89 us (13%)
    all_to_all x1, blocking collectives, body(): recv = lax.all_to_all(msg, 'sub', 0, 0)  14.7 us
    pallas_call x8, Pallas kernels, call(): pl.pallas_call(kernel, out_shape=[o for o, _ in outs], in_specs=[pl.Block...  14 us
    ppermute x6, starting transfers between devices, traded(): outs.append(lax.ppermute(x, ('grp', 'sub'), pairs))  9.09 us
    ppermute x6, waiting for transfers between devices, traded(): outs.append(lax.ppermute(x, ('grp', 'sub'), pairs))  3.97 us
    ppermute x3, starting transfers between devices, rotated(): return lax.ppermute(x, axis, [(i, (i + by) % n) for i in range(n)])  2.27 us
    ppermute x3, waiting for transfers between devices, rotated(): return lax.ppermute(x, axis, [(i, (i + by) % n) for i in range(n)])  1.92 us
  transfers between devices with their start and end apart: 9, of which 5 were waited for; matrix products, arithmetic and copies ran while one was open for 0% of the time, Pallas kernels for 6%

profile of v6, /device:TPU:0, one launch (start us, length us, event | category | flops | bytes accessed | tf_op | source)
XLA Modules:
  0.0 45.9 jit_solution(8883465667596278147)
XLA Ops:
  0.0 2.2 %shard_map.64 = (f32[48,256]{1,0:T(8,128)S(1)}, f32[16,256]{1,0:T(8,128)S(1)}, f32[16,256]{1,0:T(8,128)S(1)}, s32[64,128]{1,0:T(8,128)S(1)}, f32[8,256]{1,0:T(8,128)S(1)}) custom-call(s32[1]{0:T(128)} %bitcast.col_ref, s32[2,4096]{1,0:T(2,128)} %map_ref.1, f32[3,4096]{1,0:T(4,128)} %fine_ref.1, f32[16,128]{1,0:T(8,128)} %bitcast.2), custom_call_target="tpu_custom_call" | custom-call | tf_op jit(solution)/shard_map/pallas_call | solution.py:404
  2.2 3.1 %collective-permute-start = (f32[16,256]{1,0:T(8,128)S(1)}, f32[16,256]{1,0:T(8,128)S(1)}, u32[]{:S(2)}, u32[]{:S(2)}) collective-permute-start(f32[16,256]{1,0:T(8,128)S(1)} %get-tuple-element.29), channel_id=1, source_target_pairs={{0,1},{1,0},{2,3},{3,2},{4,5},{5,4},{6,7},{7,6},{8,9},{9,8},{10,11... | collective-permute-start | bytes 49160 | tf_op jit(solution)/shard_map/ppermute | solution.py:432
  5.2 0.0 collective-permute-start.1
  5.2 1.2 %shard_map.65 = (s32[128,128]{1,0:T(8,128)S(1)}, s32[128,128]{1,0:T(8,128)S(1)}, f32[288,128]{1,0:T(8,128)S(1)}, f32[64,128]{1,0:T(8,128)S(1)}) custom-call(s32[1]{0:T(128)} %bitcast.col_ref, s32[4,4096]{1,0:T(4,128)} %conn_ref.1, f32[3,3,4096]{2,1,0:T(4,128)} %grads_ref.1, f32[2,4096]{1,0:T(2,128)} %moduli_ref.1), custom_call_target="tpu_custom_call" | custom-call | tf_op jit(solution)/shard_map/pallas_call | solution.py:404
  6.4 0.5 %collective-permute-done.one_ref = f32[16,256]{1,0:T(8,128)S(1)} collective-permute-done((f32[16,256]{1,0:T(8,128)S(1)}, f32[16,256]{1,0:T(8,128)S(1)}, u32[]{:S(2)}, u32[]{:S(2)}) %collective-permute-start) | collective-permute-done | bytes 16416 | tf_op jit(solution)/shard_map/ppermute | solution.py:432
  7.0 0.0 collective-permute-done.1.two_ref
  7.0 1.1 %collective-permute-start.4 = (f32[48,256]{1,0:T(8,128)S(1)}, f32[48,256]{1,0:T(8,128)S(1)}, u32[]{:S(2)}, u32[]{:S(2)}) collective-permute-start(f32[48,256]{1,0:T(8,128)S(1)} %get-tuple-element.33.refs_0_), channel_id=1, source_target_pairs={{0,24},{8,0},{16,8},{24,16},{1,25},{9,1},{17,9},{25,17},{2,26},{10... | collective-permute-start | bytes 147464 | tf_op jit(solution)/shard_map/ppermute | solution.py:416
  8.1 1.0 %collective-permute-start.3 = (f32[48,256]{1,0:T(8,128)S(1)}, f32[48,256]{1,0:T(8,128)S(1)}, u32[]{:S(2)}, u32[]{:S(2)}) collective-permute-start(f32[48,256]{1,0:T(8,128)S(1)} %get-tuple-element.33.refs_0_), channel_id=1, source_target_pairs={{0,16},{8,24},{16,0},{24,8},{1,17},{9,25},{17,1},{25,9},{2,18},{10... | collective-permute-start | bytes 147464 | tf_op jit(solution)/shard_map/ppermute | solution.py:416
  9.1 0.2 collective-permute-start.2
  9.3 1.5 %shard_map.67.refs_5_.hot_ref = bf16[16384,256]{1,0:T(8,128)(2,1)S(1)} custom-call(s32[128,128]{1,0:T(8,128)S(1)} %get-tuple-element.35.cols_ref), custom_call_target="tpu_custom_call" | custom-call | tf_op jit(solution)/shard_map/pallas_call | solution.py:404
  10.8 0.0 collective-permute-done.4.refs_3_
  10.8 1.5 %collective-permute-done.3.refs_2_ = f32[48,256]{1,0:T(8,128)S(1)} collective-permute-done((f32[48,256]{1,0:T(8,128)S(1)}, f32[48,256]{1,0:T(8,128)S(1)}, u32[]{:S(2)}, u32[]{:S(2)}) %collective-permute-start.3) | collective-permute-done | bytes 49184 | tf_op jit(solution)/shard_map/ppermute | solution.py:416
  12.3 0.4 collective-permute-done.2.refs_1_
  12.7 2.9 %shard_map.68 = (f32[48,256]{1,0:T(8,128)S(1)}, f32[48,256]{1,0:T(8,128)S(1)}, f32[12,256]{1,0:T(8,128)S(1)}, f32[12,256]{1,0:T(8,128)S(1)}, f32[192,128]{1,0:T(8,128)S(1)}) custom-call(s32[1]{0:T(128)} %bitcast.col_ref, f32[48,256]{1,0:T(8,128)S(1)} %get-tuple-element.33.refs_0_, f32[48,256]{1,0:T(8,128)S(1)} %collective-permute-done.2.refs_1_, ...), custom_call_target="tpu_custom_call" | custom-call | tf_op jit(solution)/shard_map/pallas_call | solution.py:404
  15.6 2.9 %collective-permute-start.5 = (f32[12,256]{1,0:T(8,128)S(1)}, f32[12,256]{1,0:T(8,128)S(1)}, u32[]{:S(2)}, u32[]{:S(2)}) collective-permute-start(f32[12,256]{1,0:T(8,128)S(1)} %get-tuple-element.37), channel_id=1, source_target_pairs={{0,1},{1,0},{2,3},{3,2},{4,5},{5,4},{6,7},{7,6},{8,9},{9,8},{10,11... | collective-permute-start | bytes 36872 | tf_op jit(solution)/shard_map/ppermute | solution.py:432
  18.5 0.0 collective-permute-start.6
  18.5 1.7 %collective-permute-done.5.one_ref = f32[12,256]{1,0:T(8,128)S(1)} collective-permute-done((f32[12,256]{1,0:T(8,128)S(1)}, f32[12,256]{1,0:T(8,128)S(1)}, u32[]{:S(2)}, u32[]{:S(2)}) %collective-permute-start.5) | collective-permute-done | bytes 12320 | tf_op jit(solution)/shard_map/ppermute | solution.py:432
  20.2 0.0 collective-permute-done.6.two_ref
  20.2 2.9 %shard_map.69 = (f32[48,256]{1,0:T(8,128)S(1)}, f32[48,256]{1,0:T(8,128)S(1)}, f32[12,256]{1,0:T(8,128)S(1)}, f32[12,256]{1,0:T(8,128)S(1)}, f32[192,128]{1,0:T(8,128)S(1)}) custom-call(s32[1]{0:T(128)} %bitcast.col_ref, f32[12,256]{1,0:T(8,128)S(1)} %collective-permute-done.5.one_ref, f32[12,256]{1,0:T(8,128)S(1)} %collective-permute-done.6.two_ref, ...), custom_call_target="tpu_custom_call" | custom-call | tf_op jit(solution)/shard_map/pallas_call | solution.py:404
  23.1 3.2 %collective-permute-start.7 = (f32[12,256]{1,0:T(8,128)S(1)}, f32[12,256]{1,0:T(8,128)S(1)}, u32[]{:S(2)}, u32[]{:S(2)}) collective-permute-start(f32[12,256]{1,0:T(8,128)S(1)} %get-tuple-element.42), channel_id=1, source_target_pairs={{0,1},{1,0},{2,3},{3,2},{4,5},{5,4},{6,7},{7,6},{8,9},{9,8},{10,11... | collective-permute-start | bytes 36872 | tf_op jit(solution)/shard_map/ppermute | solution.py:432
  26.3 0.0 collective-permute-start.8
  26.3 1.7 %collective-permute-done.7.one_ref = f32[12,256]{1,0:T(8,128)S(1)} collective-permute-done((f32[12,256]{1,0:T(8,128)S(1)}, f32[12,256]{1,0:T(8,128)S(1)}, u32[]{:S(2)}, u32[]{:S(2)}) %collective-permute-start.7) | collective-permute-done | bytes 12320 | tf_op jit(solution)/shard_map/ppermute | solution.py:432
  28.0 0.0 collective-permute-done.8.two_ref
  28.0 1.7 %shard_map.70 = (f32[8,8,128]{2,1,0:T(8,128)S(1)}, f32[48,256]{1,0:T(8,128)S(1)}) custom-call(s32[1]{0:T(128)} %bitcast.col_ref, f32[12,256]{1,0:T(8,128)S(1)} %collective-permute-done.7.one_ref, f32[12,256]{1,0:T(8,128)S(1)} %collective-permute-done.8.two_ref, f32[48,256]{1,0:T(8,128)S(1)} %get-tuple-element.39.v0_ref, ...), custom_call_target="tpu_custom_call" | custom-call | tf_op jit(solution)/shard_map/pallas_call | solution.py:404
  29.6 14.7 %all_to_all.5.recv_ref = f32[8,8,128]{2,1,0:T(8,128)S(1)} all-to-all(f32[8,8,128]{2,1,0:T(8,128)S(1)} %get-tuple-element.48), channel_id=1, replica_groups=mesh['grp'=4,'sub'=8] {'sub'}, dimensions={0} | all-to-all | bytes 65536 | tf_op jit(solution)/shard_map/all_to_all | solution.py:503
  44.3 1.6 %shard_map.71 = f32[3,4096]{1,0:T(4,128)} custom-call(f32[8,8,128]{2,1,0:T(8,128)S(1)} %all_to_all.5.recv_ref, f32[48,256]{1,0:T(8,128)S(1)} %get-tuple-element.39.v0_ref, f32[48,256]{1,0:T(8,128)S(1)} %get-tuple-element.44.v1_ref, f32[48,256]{1,0:T(8,128)S(1)} %get-tuple-element.49.v2_ref, s32[64,128]{1,0:T(8,128)S(1)} %get-tuple-element.50.idx_ref), custom_call_target="tpu_custom_call" | custom-call | tf_op jit(solution)/shard_map/pallas_call | solution.py:404
  (1 shorter events, 0.0 us)
Async XLA Ops:
  2.2 4.8 %collective-permute-start = (f32[16,256]{1,0:T(8,128)S(1)}, f32[16,256]{1,0:T(8,128)S(1)}, u32[]{:S(2)}, u32[]{:S(2)}) collective-permute-start(f32[16,256]{1,0:T(8,128)S(1)} %get-tuple-element.29), channel_id=1, source_target_pairs={{0,1},{1,0},{2,3},{3,2},{4,5},{5,4},{6,7},{7,6},{8,9},{9,8},{10,11... | collective-permute-start | bytes 49160 | tf_op jit(solution)/shard_map/ppermute | solution.py:432
  5.2 1.7 %collective-permute-start.1 = (f32[16,256]{1,0:T(8,128)S(1)}, f32[16,256]{1,0:T(8,128)S(1)}, u32[]{:S(2)}, u32[]{:S(2)}) collective-permute-start(f32[16,256]{1,0:T(8,128)S(1)} %get-tuple-element.30), channel_id=1, source_target_pairs={{0,8},{1,2},{2,1},{3,4},{4,3},{5,6},{6,5},{7,15},{8,0},{9,10},{10,... | collective-permute-start | bytes 49160 | tf_op jit(solution)/shard_map/ppermute | solution.py:432
  7.0 3.8 %collective-permute-start.4 = (f32[48,256]{1,0:T(8,128)S(1)}, f32[48,256]{1,0:T(8,128)S(1)}, u32[]{:S(2)}, u32[]{:S(2)}) collective-permute-start(f32[48,256]{1,0:T(8,128)S(1)} %get-tuple-element.33.refs_0_), channel_id=1, source_target_pairs={{0,24},{8,0},{16,8},{24,16},{1,25},{9,1},{17,9},{25,17},{2,26},{10... | collective-permute-start | bytes 147464 | tf_op jit(solution)/shard_map/ppermute | solution.py:416
  8.1 4.2 %collective-permute-start.3 = (f32[48,256]{1,0:T(8,128)S(1)}, f32[48,256]{1,0:T(8,128)S(1)}, u32[]{:S(2)}, u32[]{:S(2)}) collective-permute-start(f32[48,256]{1,0:T(8,128)S(1)} %get-tuple-element.33.refs_0_), channel_id=1, source_target_pairs={{0,16},{8,24},{16,0},{24,8},{1,17},{9,25},{17,1},{25,9},{2,18},{10... | collective-permute-start | bytes 147464 | tf_op jit(solution)/shard_map/ppermute | solution.py:416
  9.1 3.6 %collective-permute-start.2 = (f32[48,256]{1,0:T(8,128)S(1)}, f32[48,256]{1,0:T(8,128)S(1)}, u32[]{:S(2)}, u32[]{:S(2)}) collective-permute-start(f32[48,256]{1,0:T(8,128)S(1)} %get-tuple-element.33.refs_0_), channel_id=1, source_target_pairs={{0,8},{8,16},{16,24},{24,0},{1,9},{9,17},{17,25},{25,1},{2,10},{10... | collective-permute-start | bytes 147464 | tf_op jit(solution)/shard_map/ppermute | solution.py:416
  15.6 4.6 %collective-permute-start.5 = (f32[12,256]{1,0:T(8,128)S(1)}, f32[12,256]{1,0:T(8,128)S(1)}, u32[]{:S(2)}, u32[]{:S(2)}) collective-permute-start(f32[12,256]{1,0:T(8,128)S(1)} %get-tuple-element.37), channel_id=1, source_target_pairs={{0,1},{1,0},{2,3},{3,2},{4,5},{5,4},{6,7},{7,6},{8,9},{9,8},{10,11... | collective-permute-start | bytes 36872 | tf_op jit(solution)/shard_map/ppermute | solution.py:432
  18.5 1.7 %collective-permute-start.6 = (f32[12,256]{1,0:T(8,128)S(1)}, f32[12,256]{1,0:T(8,128)S(1)}, u32[]{:S(2)}, u32[]{:S(2)}) collective-permute-start(f32[12,256]{1,0:T(8,128)S(1)} %get-tuple-element.38), channel_id=1, source_target_pairs={{0,8},{1,2},{2,1},{3,4},{4,3},{5,6},{6,5},{7,15},{8,0},{9,10},{10,... | collective-permute-start | bytes 36872 | tf_op jit(solution)/shard_map/ppermute | solution.py:432
  23.1 4.9 %collective-permute-start.7 = (f32[12,256]{1,0:T(8,128)S(1)}, f32[12,256]{1,0:T(8,128)S(1)}, u32[]{:S(2)}, u32[]{:S(2)}) collective-permute-start(f32[12,256]{1,0:T(8,128)S(1)} %get-tuple-element.42), channel_id=1, source_target_pairs={{0,1},{1,0},{2,3},{3,2},{4,5},{5,4},{6,7},{7,6},{8,9},{9,8},{10,11... | collective-permute-start | bytes 36872 | tf_op jit(solution)/shard_map/ppermute | solution.py:432
  26.3 1.7 %collective-permute-start.8 = (f32[12,256]{1,0:T(8,128)S(1)}, f32[12,256]{1,0:T(8,128)S(1)}, u32[]{:S(2)}, u32[]{:S(2)}) collective-permute-start(f32[12,256]{1,0:T(8,128)S(1)} %get-tuple-element.43), channel_id=1, source_target_pairs={{0,8},{1,2},{2,1},{3,4},{4,3},{5,6},{6,5},{7,15},{8,0},{9,10},{10,... | collective-permute-start | bytes 36872 | tf_op jit(solution)/shard_map/ppermute | solution.py:432

commit v7 on v6

--- a/solution.py
+++ b/solution.py
@@ -52,8 +52,7 @@
     for i in range(count // RC):
         hot, moved = [], []
         for row in range(i * RC, i * RC + RC):
-            lo = (cols_ref[:, row : row + 1] & (LO - 1)).astype(jnp.float32)
-            lo = jnp.broadcast_to(lo, (LANE, LANE)).astype(jnp.bfloat16)
+            lo = jnp.broadcast_to(cols_ref[:, row : row + 1], (LANE, LANE)).astype(jnp.bfloat16)
             hot.append(jnp.where(lo_iota == jnp.concatenate([lo, lo], axis=1), one, zero))
             mask = hi_iota == (idx_ref[row : row + 1, :] >> 8)
             group = [
@@ -85,7 +84,7 @@
     shift = col_ref[0] * own
     for k in range(2):
         lines(map_ref, (slice(k, k + 1),), idx_ref, k * half, lambda x: x - shift)
-    cols_ref[...] = jnp.transpose(idx_ref[...])
+    cols_ref[...] = jnp.transpose((idx_ref[...] & (LO - 1)).astype(jnp.float32))
     for c in range(3):
         lines(fine_ref, (slice(c, c + 1),), half_ref, c * half)
     for c in range(3):
@@ -111,7 +110,7 @@
     shift = col_ref[0] * own
     for a in range(4):
         lines(conn_ref, (slice(a, a + 1),), idx_ref, a * 8, lambda x: x - shift, 32)
-    cols_ref[...] = jnp.transpose(idx_ref[...])
+    cols_ref[...] = jnp.transpose((idx_ref[...] & (LO - 1)).astype(jnp.float32))
     for d in range(3):
         for a in range(3):
             lines(grads_ref, (d, slice(a, a + 1)), g_ref, (d * 3 + a) * per)
@@ -122,8 +121,7 @@
 def hot_kernel(cols_ref, hot_ref):
     lo_iota = lax.broadcasted_iota(jnp.int32, (LANE, LO), 1).astype(jnp.float32).astype(jnp.bfloat16)
     for row in range(cols_ref.shape[1]):
-        lo = (cols_ref[:, row : row + 1] & (LO - 1)).astype(jnp.float32)
-        lo = jnp.broadcast_to(lo, (LANE, LANE)).astype(jnp.bfloat16)
+        lo = jnp.broadcast_to(cols_ref[:, row : row + 1], (LANE, LANE)).astype(jnp.bfloat16)
         hit = lo_iota == jnp.concatenate([lo, lo], axis=1)
         hot_ref[row * LANE : (row + 1) * LANE, :] = jnp.where(hit, jnp.bfloat16(1), jnp.bfloat16(0))
 
@@ -174,7 +172,7 @@
     per = moduli_ref.shape[0] // 2
     count = 4 * per
     hi_iota = lax.broadcasted_iota(jnp.int32, (HP, LANE), 0)
-    acc_ref[...] = jnp.zeros((9 * HP, LO), jnp.float32)
+    acc_ref[...] = jnp.zeros(acc_ref.shape, jnp.float32)
 
     def forces(j):
         at = j * 8
@@ -198,11 +196,15 @@
                 for p in range(9)
             ]
             moved.append(jnp.concatenate(group, axis=0))
-        acc_ref[...] += jnp.dot(
-            jnp.concatenate(moved, axis=1),
-            hot_ref[j * 32 * LANE : (j + 1) * 32 * LANE, :],
-            preferred_element_type=jnp.float32,
-        )
+        half = 16
+        n = 9 * HP
+        for h in range(2):
+            at = (j * 32 + h * half) * LANE
+            acc_ref[h * n : (h + 1) * n, :] += jnp.dot(
+                jnp.concatenate(moved[h * half : (h + 1) * half], axis=1),
+                hot_ref[at : at + half * LANE, :],
+                preferred_element_type=jnp.float32,
+            )
 
     for j in range(per // 8 + 1):
 
@@ -214,7 +216,7 @@
                 forces(j)
 
     n = 3 * HP
-    return acc_ref[:n] + acc_ref[n : 2 * n] + acc_ref[2 * n :]
+    return sum(acc_ref[p * n : (p + 1) * n] for p in range(6))
 
 
 def stresses(strain, lam, mu):
@@ -459,14 +461,14 @@
         functools.partial(rhs_kernel, own=own),
         [(col, "s"), (node_map, "h"), (fine_res, "h"), (mass2, "h")],
         [table, kept(4 * k, LO), kept(4 * k, LO), kept(fcount, LANE, dtype=jnp.int32), kept(own // LO, LO)],
-        [pltpu.VMEM((3 * fcount // 2, LANE), jnp.float32), pltpu.VMEM((LANE, fcount), jnp.int32),
+        [pltpu.VMEM((3 * fcount // 2, LANE), jnp.float32), pltpu.VMEM((LANE, fcount), jnp.float32),
          pltpu.VMEM((9 * fcount, LANE), jnp.float32), acc],
     )
     one, two = traded(one, two)
     idx, cols, g, mod = call(
         functools.partial(prep_kernel, own=own),
         [(col, "s"), (connect, "h"), (grads, "h"), (moduli, "h")],
-        [kept(ecount, LANE, dtype=jnp.int32), kept(LANE, ecount, dtype=jnp.int32), kept(9 * elems // LANE, LANE), kept(2 * elems // LANE, LANE)],
+        [kept(ecount, LANE, dtype=jnp.int32), kept(LANE, ecount), kept(9 * elems // LANE, LANE), kept(2 * elems // LANE, LANE)],
     )
     part, mass_ext = call(
         functools.partial(halo_kernel, own=own, size=size),
@@ -482,7 +484,7 @@
         functools.partial(first_kernel, groups=groups, **kw),
         [(col, "s")] + [(x, "v") for x in sums] + summing,
         [table, table, edge, edge, strain],
-        [parts, acc],
+        [parts, pltpu.VMEM((18 * HP, LO), jnp.float32)],
         ROOM,
     )
     one, two = traded(one, two)
@@ -490,7 +492,7 @@
         functools.partial(second_kernel, size=size, **kw),
         [(col, "s"), (one, "v"), (two, "v"), (v0, "v"), (f0, "v"), (mass_ext, "v")] + summing,
         [table, table, edge, edge, strain],
-        [parts, acc],
+        [parts, pltpu.VMEM((18 * HP, LO), jnp.float32)],
         ROOM,
     )
     one, two = traded(one, two)

time: 46.2 us -> 45.2 us (0.978)
  Pallas kernels: 14 us -> 12.9 us
    pallas_call x8, Pallas kernels: 14 us -> 12.9 us  [call(): pl.pallas_call(kernel, out_shape=[o for o, _ in outs], in_specs=[pl.Block...]
where the time goes in v7:
time: 45.2 us; the launch traced here: 45 us
  blocking collectives  14.7 us (33%)
  Pallas kernels  12.9 us (29%)
  starting transfers between devices  11.4 us (25%)
  waiting for transfers between devices  6.02 us (13%)
    all_to_all x1, blocking collectives, body(): recv = lax.all_to_all(msg, 'sub', 0, 0)  14.7 us
    pallas_call x8, Pallas kernels, call(): pl.pallas_call(kernel, out_shape=[o for o, _ in outs], in_specs=[pl.Block...  12.9 us
    ppermute x6, starting transfers between devices, traded(): outs.append(lax.ppermute(x, ('grp', 'sub'), pairs))  9.08 us
    ppermute x6, waiting for transfers between devices, traded(): outs.append(lax.ppermute(x, ('grp', 'sub'), pairs))  3.97 us
    ppermute x3, starting transfers between devices, rotated(): return lax.ppermute(x, axis, [(i, (i + by) % n) for i in range(n)])  2.28 us
    ppermute x3, waiting for transfers between devices, rotated(): return lax.ppermute(x, axis, [(i, (i + by) % n) for i in range(n)])  2.06 us
  transfers between devices with their start and end apart: 9, of which 5 were waited for; matrix products, arithmetic and copies ran while one was open for 0% of the time, Pallas kernels for 6%

profile of v7, /device:TPU:0, one launch (start us, length us, event | category | flops | bytes accessed | tf_op | source)
XLA Modules:
  0.0 45.0 jit_solution(9936940159449543566)
XLA Ops:
  0.0 2.2 %shard_map.64 = (f32[48,256]{1,0:T(8,128)S(1)}, f32[16,256]{1,0:T(8,128)S(1)}, f32[16,256]{1,0:T(8,128)S(1)}, s32[64,128]{1,0:T(8,128)S(1)}, f32[8,256]{1,0:T(8,128)S(1)}) custom-call(s32[1]{0:T(128)} %bitcast.col_ref, s32[2,4096]{1,0:T(2,128)} %map_ref.1, f32[3,4096]{1,0:T(4,128)} %fine_ref.1, f32[16,128]{1,0:T(8,128)} %bitcast.2), custom_call_target="tpu_custom_call" | custom-call | tf_op jit(solution)/shard_map/pallas_call | solution.py:406
  2.2 3.1 %collective-permute-start = (f32[16,256]{1,0:T(8,128)S(1)}, f32[16,256]{1,0:T(8,128)S(1)}, u32[]{:S(2)}, u32[]{:S(2)}) collective-permute-start(f32[16,256]{1,0:T(8,128)S(1)} %get-tuple-element.29), channel_id=1, source_target_pairs={{0,1},{1,0},{2,3},{3,2},{4,5},{5,4},{6,7},{7,6},{8,9},{9,8},{10,11... | collective-permute-start | bytes 49160 | tf_op jit(solution)/shard_map/ppermute | solution.py:434
  5.2 0.0 collective-permute-start.1
  5.2 1.2 %shard_map.65 = (s32[128,128]{1,0:T(8,128)S(1)}, f32[128,128]{1,0:T(8,128)S(1)}, f32[288,128]{1,0:T(8,128)S(1)}, f32[64,128]{1,0:T(8,128)S(1)}) custom-call(s32[1]{0:T(128)} %bitcast.col_ref, s32[4,4096]{1,0:T(4,128)} %conn_ref.1, f32[3,3,4096]{2,1,0:T(4,128)} %grads_ref.1, f32[2,4096]{1,0:T(2,128)} %moduli_ref.1), custom_call_target="tpu_custom_call" | custom-call | tf_op jit(solution)/shard_map/pallas_call | solution.py:406
  6.4 0.5 %collective-permute-done.one_ref = f32[16,256]{1,0:T(8,128)S(1)} collective-permute-done((f32[16,256]{1,0:T(8,128)S(1)}, f32[16,256]{1,0:T(8,128)S(1)}, u32[]{:S(2)}, u32[]{:S(2)}) %collective-permute-start) | collective-permute-done | bytes 16416 | tf_op jit(solution)/shard_map/ppermute | solution.py:434
  7.0 0.0 collective-permute-done.1.two_ref
  7.0 1.1 %collective-permute-start.4 = (f32[48,256]{1,0:T(8,128)S(1)}, f32[48,256]{1,0:T(8,128)S(1)}, u32[]{:S(2)}, u32[]{:S(2)}) collective-permute-start(f32[48,256]{1,0:T(8,128)S(1)} %get-tuple-element.33.refs_0_), channel_id=1, source_target_pairs={{0,24},{8,0},{16,8},{24,16},{1,25},{9,1},{17,9},{25,17},{2,26},{10... | collective-permute-start | bytes 147464 | tf_op jit(solution)/shard_map/ppermute | solution.py:418
  8.1 1.0 %collective-permute-start.3 = (f32[48,256]{1,0:T(8,128)S(1)}, f32[48,256]{1,0:T(8,128)S(1)}, u32[]{:S(2)}, u32[]{:S(2)}) collective-permute-start(f32[48,256]{1,0:T(8,128)S(1)} %get-tuple-element.33.refs_0_), channel_id=1, source_target_pairs={{0,16},{8,24},{16,0},{24,8},{1,17},{9,25},{17,1},{25,9},{2,18},{10... | collective-permute-start | bytes 147464 | tf_op jit(solution)/shard_map/ppermute | solution.py:418
  9.1 0.2 collective-permute-start.2
  9.3 1.4 %shard_map.67.refs_5_.hot_ref = bf16[16384,256]{1,0:T(8,128)(2,1)S(1)} custom-call(f32[128,128]{1,0:T(8,128)S(1)} %get-tuple-element.35.cols_ref), custom_call_target="tpu_custom_call" | custom-call | tf_op jit(solution)/shard_map/pallas_call | solution.py:406
  10.7 0.0 collective-permute-done.4.refs_3_
  10.7 1.6 %collective-permute-done.3.refs_2_ = f32[48,256]{1,0:T(8,128)S(1)} collective-permute-done((f32[48,256]{1,0:T(8,128)S(1)}, f32[48,256]{1,0:T(8,128)S(1)}, u32[]{:S(2)}, u32[]{:S(2)}) %collective-permute-start.3) | collective-permute-done | bytes 49184 | tf_op jit(solution)/shard_map/ppermute | solution.py:418
  12.3 0.4 collective-permute-done.2.refs_1_
  12.7 2.4 %shard_map.68 = (f32[48,256]{1,0:T(8,128)S(1)}, f32[48,256]{1,0:T(8,128)S(1)}, f32[12,256]{1,0:T(8,128)S(1)}, f32[12,256]{1,0:T(8,128)S(1)}, f32[192,128]{1,0:T(8,128)S(1)}) custom-call(s32[1]{0:T(128)} %bitcast.col_ref, f32[48,256]{1,0:T(8,128)S(1)} %get-tuple-element.33.refs_0_, f32[48,256]{1,0:T(8,128)S(1)} %collective-permute-done.2.refs_1_, ...), custom_call_target="tpu_custom_call" | custom-call | tf_op jit(solution)/shard_map/pallas_call | solution.py:406
  15.1 2.9 %collective-permute-start.5 = (f32[12,256]{1,0:T(8,128)S(1)}, f32[12,256]{1,0:T(8,128)S(1)}, u32[]{:S(2)}, u32[]{:S(2)}) collective-permute-start(f32[12,256]{1,0:T(8,128)S(1)} %get-tuple-element.37), channel_id=1, source_target_pairs={{0,1},{1,0},{2,3},{3,2},{4,5},{5,4},{6,7},{7,6},{8,9},{9,8},{10,11... | collective-permute-start | bytes 36872 | tf_op jit(solution)/shard_map/ppermute | solution.py:434
  18.0 0.0 collective-permute-start.6
  18.0 1.7 %collective-permute-done.5.one_ref = f32[12,256]{1,0:T(8,128)S(1)} collective-permute-done((f32[12,256]{1,0:T(8,128)S(1)}, f32[12,256]{1,0:T(8,128)S(1)}, u32[]{:S(2)}, u32[]{:S(2)}) %collective-permute-start.5) | collective-permute-done | bytes 12320 | tf_op jit(solution)/shard_map/ppermute | solution.py:434
  19.7 0.0 collective-permute-done.6.two_ref
  19.7 2.4 %shard_map.69 = (f32[48,256]{1,0:T(8,128)S(1)}, f32[48,256]{1,0:T(8,128)S(1)}, f32[12,256]{1,0:T(8,128)S(1)}, f32[12,256]{1,0:T(8,128)S(1)}, f32[192,128]{1,0:T(8,128)S(1)}) custom-call(s32[1]{0:T(128)} %bitcast.col_ref, f32[12,256]{1,0:T(8,128)S(1)} %collective-permute-done.5.one_ref, f32[12,256]{1,0:T(8,128)S(1)} %collective-permute-done.6.two_ref, ...), custom_call_target="tpu_custom_call" | custom-call | tf_op jit(solution)/shard_map/pallas_call | solution.py:406
  22.1 3.2 %collective-permute-start.7 = (f32[12,256]{1,0:T(8,128)S(1)}, f32[12,256]{1,0:T(8,128)S(1)}, u32[]{:S(2)}, u32[]{:S(2)}) collective-permute-start(f32[12,256]{1,0:T(8,128)S(1)} %get-tuple-element.42), channel_id=1, source_target_pairs={{0,1},{1,0},{2,3},{3,2},{4,5},{5,4},{6,7},{7,6},{8,9},{9,8},{10,11... | collective-permute-start | bytes 36872 | tf_op jit(solution)/shard_map/ppermute | solution.py:434
  25.3 0.0 collective-permute-start.8
  25.3 1.7 %collective-permute-done.7.one_ref = f32[12,256]{1,0:T(8,128)S(1)} collective-permute-done((f32[12,256]{1,0:T(8,128)S(1)}, f32[12,256]{1,0:T(8,128)S(1)}, u32[]{:S(2)}, u32[]{:S(2)}) %collective-permute-start.7) | collective-permute-done | bytes 12320 | tf_op jit(solution)/shard_map/ppermute | solution.py:434
  27.0 0.0 collective-permute-done.8.two_ref
  27.0 1.7 %shard_map.70 = (f32[8,8,128]{2,1,0:T(8,128)S(1)}, f32[48,256]{1,0:T(8,128)S(1)}) custom-call(s32[1]{0:T(128)} %bitcast.col_ref, f32[12,256]{1,0:T(8,128)S(1)} %collective-permute-done.7.one_ref, f32[12,256]{1,0:T(8,128)S(1)} %collective-permute-done.8.two_ref, f32[48,256]{1,0:T(8,128)S(1)} %get-tuple-element.39.v0_ref, ...), custom_call_target="tpu_custom_call" | custom-call | tf_op jit(solution)/shard_map/pallas_call | solution.py:406
  28.7 14.7 %all_to_all.5.recv_ref = f32[8,8,128]{2,1,0:T(8,128)S(1)} all-to-all(f32[8,8,128]{2,1,0:T(8,128)S(1)} %get-tuple-element.48), channel_id=1, replica_groups=mesh['grp'=4,'sub'=8] {'sub'}, dimensions={0} | all-to-all | bytes 65536 | tf_op jit(solution)/shard_map/all_to_all | solution.py:505
  43.4 1.6 %shard_map.71 = f32[3,4096]{1,0:T(4,128)} custom-call(f32[8,8,128]{2,1,0:T(8,128)S(1)} %all_to_all.5.recv_ref, f32[48,256]{1,0:T(8,128)S(1)} %get-tuple-element.39.v0_ref, f32[48,256]{1,0:T(8,128)S(1)} %get-tuple-element.44.v1_ref, f32[48,256]{1,0:T(8,128)S(1)} %get-tuple-element.49.v2_ref, s32[64,128]{1,0:T(8,128)S(1)} %get-tuple-element.50.idx_ref), custom_call_target="tpu_custom_call" | custom-call | tf_op jit(solution)/shard_map/pallas_call | solution.py:406
  (1 shorter events, 0.0 us)
Async XLA Ops:
  2.2 4.8 %collective-permute-start = (f32[16,256]{1,0:T(8,128)S(1)}, f32[16,256]{1,0:T(8,128)S(1)}, u32[]{:S(2)}, u32[]{:S(2)}) collective-permute-start(f32[16,256]{1,0:T(8,128)S(1)} %get-tuple-element.29), channel_id=1, source_target_pairs={{0,1},{1,0},{2,3},{3,2},{4,5},{5,4},{6,7},{7,6},{8,9},{9,8},{10,11... | collective-permute-start | bytes 49160 | tf_op jit(solution)/shard_map/ppermute | solution.py:434
  5.2 1.7 %collective-permute-start.1 = (f32[16,256]{1,0:T(8,128)S(1)}, f32[16,256]{1,0:T(8,128)S(1)}, u32[]{:S(2)}, u32[]{:S(2)}) collective-permute-start(f32[16,256]{1,0:T(8,128)S(1)} %get-tuple-element.30), channel_id=1, source_target_pairs={{0,8},{1,2},{2,1},{3,4},{4,3},{5,6},{6,5},{7,15},{8,0},{9,10},{10,... | collective-permute-start | bytes 49160 | tf_op jit(solution)/shard_map/ppermute | solution.py:434
  7.0 3.7 %collective-permute-start.4 = (f32[48,256]{1,0:T(8,128)S(1)}, f32[48,256]{1,0:T(8,128)S(1)}, u32[]{:S(2)}, u32[]{:S(2)}) collective-permute-start(f32[48,256]{1,0:T(8,128)S(1)} %get-tuple-element.33.refs_0_), channel_id=1, source_target_pairs={{0,24},{8,0},{16,8},{24,16},{1,25},{9,1},{17,9},{25,17},{2,26},{10... | collective-permute-start | bytes 147464 | tf_op jit(solution)/shard_map/ppermute | solution.py:418
  8.1 4.2 %collective-permute-start.3 = (f32[48,256]{1,0:T(8,128)S(1)}, f32[48,256]{1,0:T(8,128)S(1)}, u32[]{:S(2)}, u32[]{:S(2)}) collective-permute-start(f32[48,256]{1,0:T(8,128)S(1)} %get-tuple-element.33.refs_0_), channel_id=1, source_target_pairs={{0,16},{8,24},{16,0},{24,8},{1,17},{9,25},{17,1},{25,9},{2,18},{10... | collective-permute-start | bytes 147464 | tf_op jit(solution)/shard_map/ppermute | solution.py:418
  9.1 3.6 %collective-permute-start.2 = (f32[48,256]{1,0:T(8,128)S(1)}, f32[48,256]{1,0:T(8,128)S(1)}, u32[]{:S(2)}, u32[]{:S(2)}) collective-permute-start(f32[48,256]{1,0:T(8,128)S(1)} %get-tuple-element.33.refs_0_), channel_id=1, source_target_pairs={{0,8},{8,16},{16,24},{24,0},{1,9},{9,17},{17,25},{25,1},{2,10},{10... | collective-permute-start | bytes 147464 | tf_op jit(solution)/shard_map/ppermute | solution.py:418
  15.1 4.6 %collective-permute-start.5 = (f32[12,256]{1,0:T(8,128)S(1)}, f32[12,256]{1,0:T(8,128)S(1)}, u32[]{:S(2)}, u32[]{:S(2)}) collective-permute-start(f32[12,256]{1,0:T(8,128)S(1)} %get-tuple-element.37), channel_id=1, source_target_pairs={{0,1},{1,0},{2,3},{3,2},{4,5},{5,4},{6,7},{7,6},{8,9},{9,8},{10,11... | collective-permute-start | bytes 36872 | tf_op jit(solution)/shard_map/ppermute | solution.py:434
  18.0 1.7 %collective-permute-start.6 = (f32[12,256]{1,0:T(8,128)S(1)}, f32[12,256]{1,0:T(8,128)S(1)}, u32[]{:S(2)}, u32[]{:S(2)}) collective-permute-start(f32[12,256]{1,0:T(8,128)S(1)} %get-tuple-element.38), channel_id=1, source_target_pairs={{0,8},{1,2},{2,1},{3,4},{4,3},{5,6},{6,5},{7,15},{8,0},{9,10},{10,... | collective-permute-start | bytes 36872 | tf_op jit(solution)/shard_map/ppermute | solution.py:434
  22.1 4.9 %collective-permute-start.7 = (f32[12,256]{1,0:T(8,128)S(1)}, f32[12,256]{1,0:T(8,128)S(1)}, u32[]{:S(2)}, u32[]{:S(2)}) collective-permute-start(f32[12,256]{1,0:T(8,128)S(1)} %get-tuple-element.42), channel_id=1, source_target_pairs={{0,1},{1,0},{2,3},{3,2},{4,5},{5,4},{6,7},{7,6},{8,9},{9,8},{10,11... | collective-permute-start | bytes 36872 | tf_op jit(solution)/shard_map/ppermute | solution.py:434
  25.3 1.7 %collective-permute-start.8 = (f32[12,256]{1,0:T(8,128)S(1)}, f32[12,256]{1,0:T(8,128)S(1)}, u32[]{:S(2)}, u32[]{:S(2)}) collective-permute-start(f32[12,256]{1,0:T(8,128)S(1)} %get-tuple-element.43), channel_id=1, source_target_pairs={{0,8},{1,2},{2,1},{3,4},{4,3},{5,6},{6,5},{7,15},{8,0},{9,10},{10,... | collective-permute-start | bytes 36872 | tf_op jit(solution)/shard_map/ppermute | solution.py:434
